TPU v7x, 32 devices: a whole 2x2x4 slice. The times are simulated.
32 devices in a mesh: tm: 8 (over z, y), space: 4 (over x, core).
Axes of the slice: x: 2, y: 2, z: 4, core: 2. Of those that a mesh axis runs over, the one named last changes fastest.
Arguments:
- starts: float32 [8, 5, 16, 64, 128], P('tm', None, 'space'), may hold values from -4 to 4
- source: float32 [5, 16, 64, 128], P(None, 'space'), may hold values from -4 to 4
Outputs:
- ends: float32 [8, 5, 16, 64, 128], P('tm', None, 'space')
- slice_norms: float32 [8], P('tm')
- total_norm: float32 [1], replicated
All inputs are finite; a program needn't handle non-finite values.
Results may differ from a plain program's by a relative error of at most 0.0003.
Values sent between devices are 32-bit elements; how exact they have to be, the bound alone decides.
No kernel may reach another device: no remote copies, remote signals or barrier semaphores. Data moves between devices by JAX's collectives and lax.ppermute only.
A program may use at most 64 MiB of HBM per device.

v0:
```python
import math

import jax
import jax.numpy as jnp
from jax import lax
from jax.sharding import PartitionSpec as P

viscosity = 0.08
diffusivity = 0.05
compress_rate = 0.25
time_step = 0.5
diffusion_number = 0.08
advect_xaxis = 0.2
advect_yaxis = 0.15
advect_zaxis = 0.1
epsilon = 1e-06
highest = lax.Precision.HIGHEST


def with_halo(cells, sides, width):
    for axis, dim in sides:
        count = lax.axis_size(axis)
        head = lax.slice_in_dim(cells, 0, width, axis=dim)
        tail = lax.slice_in_dim(cells, cells.shape[dim] - width, cells.shape[dim], axis=dim)
        cells = jnp.concatenate(
            [
                lax.ppermute(tail, axis, [(i, (i + 1) % count) for i in range(count)]),
                cells,
                lax.ppermute(head, axis, [((i + 1) % count, i) for i in range(count)]),
            ],
            axis=dim,
        )
    return cells


def across(values, axis):
    return 0.5 * (jnp.roll(values, -1, axis) - jnp.roll(values, 1, axis))


def vertical(values):
    return 0.5 * (values[2:] - values[:-2])


def laplace(values):
    interior = values[1:-1]
    summed = values[2:] + values[:-2] - 6.0 * interior
    for axis in (1, 2):
        summed = summed + jnp.roll(interior, -1, axis) + jnp.roll(interior, 1, axis)
    return summed


def tendency(padded, source):
    speed_xaxis = advect_xaxis + padded[0]
    speed_yaxis = advect_yaxis + padded[1]
    speed_zaxis = advect_zaxis + padded[2]

    def transport(quantity):
        return (
            across((speed_xaxis * quantity)[1:-1], 2)
            + across((speed_yaxis * quantity)[1:-1], 1)
            + vertical(speed_zaxis * quantity)
        )

    pressure = padded[3]
    xmomentum = -transport(padded[0]) - across(pressure[1:-1], 2) + viscosity * laplace(padded[0])
    ymomentum = -transport(padded[1]) - across(pressure[1:-1], 1) + viscosity * laplace(padded[1])
    zmomentum = -transport(padded[2]) - vertical(pressure) + viscosity * laplace(padded[2])
    pressure_rate = -compress_rate * (
        across(padded[0][1:-1], 2) + across(padded[1][1:-1], 1) + vertical(padded[2])
    )
    scalar_rate = -transport(padded[4]) + diffusivity * laplace(padded[4])
    return jnp.stack([xmomentum, ymomentum, zmomentum, pressure_rate, scalar_rate]) + source


def slab_rates(current, source):
    padded = with_halo(current, (("space", 1),), 1)
    return tendency(padded, source)


def kept_modes(keep):
    mode_ids = jnp.arange(2 * keep, dtype=jnp.int32)
    return jnp.where(mode_ids < keep, mode_ids, mode_ids - 2 * keep)


def wave_table(cell_ids, mode_ids, length):
    products = cell_ids[:, None] * mode_ids[None, :] % length
    angles = 2.0 * math.pi / length * products.astype(jnp.float32)
    return (jnp.cos(angles), jnp.sin(angles))


def shards(starts, source):
    state_now = starts[0]
    fields, slab_depth, grid_rows, grid_cols = state_now.shape
    width_space = lax.axis_size("space")
    width_time = lax.axis_size("tm")
    grid_depth = slab_depth * width_space
    keep_y = grid_rows // 8
    keep_x = grid_cols // 16
    mode_count = 4 * keep_y * keep_x
    current = state_now
    section_one = slab_rates(current, source)
    section_two = slab_rates(current + 0.5 * time_step * section_one, source)
    section_three = slab_rates(current + 0.5 * time_step * section_two, source)
    section_four = slab_rates(current + time_step * section_three, source)
    current = current + time_step / 6.0 * (
        section_one + 2.0 * section_two + 2.0 * section_three + section_four
    )
    xmodes = kept_modes(keep_x)
    ymodes = kept_modes(keep_y)
    xcosines, xsines = wave_table(jnp.arange(grid_cols, dtype=jnp.int32), xmodes, grid_cols)
    ycosines, ysines = wave_table(jnp.arange(grid_rows, dtype=jnp.int32), ymodes, grid_rows)
    stacked = jnp.stack([current, state_now]).reshape(2 * fields, slab_depth, grid_rows, grid_cols)
    real_x = jnp.einsum("bzyx,xk->bzyk", stacked, xcosines, precision=highest)
    imag_x = -jnp.einsum("bzyx,xk->bzyk", stacked, xsines, precision=highest)
    real_y = jnp.einsum("bzyk,yj->bzjk", real_x, ycosines, precision=highest) + jnp.einsum(
        "bzyk,yj->bzjk", imag_x, ysines, precision=highest
    )
    imag_y = jnp.einsum("bzyk,yj->bzjk", imag_x, ycosines, precision=highest) - jnp.einsum(
        "bzyk,yj->bzjk", real_x, ysines, precision=highest
    )
    real_y = real_y.reshape(2 * fields, slab_depth, mode_count)
    imag_y = imag_y.reshape(2 * fields, slab_depth, mode_count)
    space_pos = lax.axis_index("space")
    zcells = space_pos * slab_depth + jnp.arange(slab_depth, dtype=jnp.int32)
    zwaves = jnp.arange(lax.axis_size("space") * slab_depth, dtype=jnp.int32)
    zcosines, zsines = wave_table(zwaves, zcells, grid_depth)
    term_real = jnp.einsum("qz,bzm->qbm", zcosines, real_y, precision=highest) + jnp.einsum(
        "qz,bzm->qbm", zsines, imag_y, precision=highest
    )
    term_imag = jnp.einsum("qz,bzm->qbm", zcosines, imag_y, precision=highest) - jnp.einsum(
        "qz,bzm->qbm", zsines, real_y, precision=highest
    )
    spectrum = lax.psum_scatter(
        jnp.stack([term_real, term_imag], axis=1), "space", scatter_dimension=0, tiled=True
    )
    zangles = 2.0 * math.pi / grid_depth * zcells.astype(jnp.float32)
    yangles = 2.0 * math.pi / grid_rows * ymodes.astype(jnp.float32)
    xangles = 2.0 * math.pi / grid_cols * xmodes.astype(jnp.float32)
    keeper = (
        ((ymodes != -keep_y)[:, None] & (xmodes != -keep_x)[None, :])
        .astype(jnp.float32)
        .reshape(mode_count)
    )
    plane_cos = (
        (2.0 * jnp.cos(yangles) - 2.0)[:, None] + (2.0 * jnp.cos(xangles) - 2.0)[None, :]
    ).reshape(mode_count)
    plane_sin = (
        advect_yaxis * jnp.sin(yangles)[:, None] + advect_xaxis * jnp.sin(xangles)[None, :]
    ).reshape(mode_count)
    sym_real = (
        1.0 + diffusion_number * ((2.0 * jnp.cos(zangles) - 2.0)[:, None] + plane_cos[None, :])
    ) * keeper[None, :]
    sym_imag = -(advect_zaxis * jnp.sin(zangles)[:, None] + plane_sin[None, :]) * keeper[None, :]
    sym_real = sym_real[:, None, :]
    sym_imag = sym_imag[:, None, :]
    log_size = jnp.where(
        keeper[None, None, :] > 0.0,
        0.5 * jnp.log(sym_real * sym_real + sym_imag * sym_imag + (1.0 - keeper[None, None, :])),
        -60.0,
    )
    turning = jnp.arctan2(sym_imag, sym_real)
    fine_real = spectrum[:, 0, :fields]
    fine_imag = spectrum[:, 1, :fields]
    start_real = spectrum[:, 0, fields:]
    start_imag = spectrum[:, 1, fields:]
    position = lax.axis_index("tm")
    later_flag = (position > 0).astype(jnp.float32)
    coarse_real = sym_real * start_real - sym_imag * start_imag
    coarse_imag = sym_real * start_imag + sym_imag * start_real
    jumps = jnp.stack([fine_real - later_flag * coarse_real, fine_imag - later_flag * coarse_imag])
    portion = lax.all_gather(jumps[None], "tm", axis=0, tiled=True)
    source_rows = jnp.arange(portion.shape[0], dtype=jnp.int32)
    gaps = position - 1 - source_rows
    live = (gaps >= 0).astype(jnp.float32)[:, None, None, None]
    exponent = jnp.maximum(gaps, 0).astype(jnp.float32)[:, None, None, None]
    damping = live * jnp.exp(exponent * log_size[None])
    cosine = damping * jnp.cos(exponent * turning[None])
    sine_part = damping * jnp.sin(exponent * turning[None])
    added_real = jnp.sum(cosine * portion[:, 0] - sine_part * portion[:, 1], axis=0)
    added_imag = jnp.sum(cosine * portion[:, 1] + sine_part * portion[:, 0], axis=0)
    prior_sum = jnp.stack([added_real, added_imag])
    diff_real = prior_sum[0] - later_flag * start_real
    diff_imag = prior_sum[1] - later_flag * start_imag
    spectral_fix = jnp.stack(
        [sym_real * diff_real - sym_imag * diff_imag, sym_real * diff_imag + sym_imag * diff_real],
        axis=1,
    )
    portion = lax.all_gather(spectral_fix, "space", axis=0, tiled=True)
    zwaves = jnp.arange(portion.shape[0], dtype=jnp.int32)
    zcosines, zsines = wave_table(zcells, zwaves, grid_depth)
    back_real = jnp.einsum("zq,qfm->zfm", zcosines, portion[:, 0], precision=highest) - jnp.einsum(
        "zq,qfm->zfm", zsines, portion[:, 1], precision=highest
    )
    back_imag = jnp.einsum("zq,qfm->zfm", zcosines, portion[:, 1], precision=highest) + jnp.einsum(
        "zq,qfm->zfm", zsines, portion[:, 0], precision=highest
    )
    local_depth = jnp.stack([back_real, back_imag], axis=1)
    planes = local_depth.reshape(slab_depth, 2, fields, 2 * keep_y, 2 * keep_x)
    plane_real = jnp.einsum(
        "zfjk,yj->zfyk", planes[:, 0], ycosines, precision=highest
    ) - jnp.einsum("zfjk,yj->zfyk", planes[:, 1], ysines, precision=highest)
    plane_imag = jnp.einsum(
        "zfjk,yj->zfyk", planes[:, 1], ycosines, precision=highest
    ) + jnp.einsum("zfjk,yj->zfyk", planes[:, 0], ysines, precision=highest)
    correction = (
        jnp.einsum("zfyk,xk->fzyx", plane_real, xcosines, precision=highest)
        - jnp.einsum("zfyk,xk->fzyx", plane_imag, xsines, precision=highest)
    ) / (grid_depth * grid_rows * grid_cols)
    end_states = current + correction
    local_sum = jnp.sum(correction * correction)
    cell_total = fields * grid_depth * grid_rows * grid_cols
    slice_sum = lax.psum(local_sum, "space")
    every_sum = lax.psum(slice_sum, "tm")
    slice_value = jnp.sqrt(slice_sum / cell_total + epsilon).reshape(1)
    total_value = jnp.sqrt(every_sum / (cell_total * width_time) + epsilon).reshape(1)
    return (end_states[None], slice_value, total_value)


def solution(mesh):
    in_specs = (P("tm", None, "space", None, None), P(None, "space", None, None))
    out_specs = (P("tm", None, "space", None, None), P("tm"), P())
    return jax.shard_map(shards, mesh=mesh, in_specs=in_specs, out_specs=out_specs, check_vma=False)
```

profile of v0, /device:TPU:0, one launch (start us, length us, event | category | flops | bytes accessed | tf_op | source)
XLA Modules:
  0.0 202.2 jit_solution(17779550570251596355)
XLA Ops:
  7.2 1.8 fusion.450
  9.0 0.5 collective-permute-start
  9.5 1.9 collective-permute-start.1
  11.4 1.2 slice_bitcast_fusion.17
  12.6 0.8 slice_bitcast_fusion.51
  13.4 0.8 slice_bitcast_fusion.50
  14.4 0.8 slice_bitcast_fusion.48
  15.2 0.8 fusion.568
  16.0 0.9 fusion.569
  16.9 0.9 fusion.571
  17.8 0.6 sine_multiply_fusion.2
  18.4 0.6 multiply_add_fusion.5
  19.0 0.6 sine_multiply_fusion
  19.8 0.6 broadcast_subtract_fusion
  20.4 0.5 broadcast_compare_fusion
  20.9 0.7 broadcast_add_fusion.1
  21.7 0.8 broadcast_add_fusion
  22.5 0.7 add.1066
  23.2 0.8 multiply_select_fusion
  24.0 1.2 dynamic-slice
  25.9 0.5 maximum_convert_fusion
  28.0 0.5 copy-done.7
  29.2 0.6 copy-done.2
  30.3 0.6 copy-done.13
  31.6 0.8 copy-done.1
  33.7 0.7 collective-permute-start.2
  34.4 1.1 collective-permute-start.3
  35.5 3.0 %collective-permute-done.2 = f32[5,1,64,128]{3,2,1,0:T(8,128)S(1)} collective-permute-done((f32[5,1,64,128]{3,2,1,0:T(8,128)S(1)}, f32[5,1,64,128]{3,2,1,0:T(8,128)S(1)}, u32[]{:S(2)}, u32[]{:S(2)}) %collective-permute-start.2) | collective-permute-done | bytes 163872 | tf_op jit(solution)/shard_map/ppermute | solution.py:27
  38.5 1.6 collective-permute-done.3
  44.1 0.9 collective-permute-start.4
  45.0 1.4 collective-permute-start.5
  46.4 2.9 %collective-permute-done.4 = f32[5,1,64,128]{3,2,1,0:T(8,128)S(1)} collective-permute-done((f32[5,1,64,128]{3,2,1,0:T(8,128)S(1)}, f32[5,1,64,128]{3,2,1,0:T(8,128)S(1)}, u32[]{:S(2)}, u32[]{:S(2)}) %collective-permute-start.4) | collective-permute-done | bytes 163872 | tf_op jit(solution)/shard_map/ppermute | solution.py:27
  49.3 1.3 collective-permute-done.5
  53.5 0.4 multiply_add_fusion
  55.2 0.9 collective-permute-start.6
  56.1 1.3 collective-permute-start.7
  57.4 2.8 %collective-permute-done.6 = f32[5,1,64,128]{3,2,1,0:T(8,128)S(1)} collective-permute-done((f32[5,1,64,128]{3,2,1,0:T(8,128)S(1)}, f32[5,1,64,128]{3,2,1,0:T(8,128)S(1)}, u32[]{:S(2)}, u32[]{:S(2)}) %collective-permute-start.6) | collective-permute-done | bytes 163872 | tf_op jit(solution)/shard_map/ppermute | solution.py:27
  60.2 1.2 collective-permute-done.7
  64.5 3.2 %fusion.304 = f32[10,4,64,16]{2,3,1,0:T(8,128)S(1)} fusion(f32[10,4,64,128]{3,2,1,0:T(8,128)S(1)} %bitcast.754, s32[16]{0:T(128)S(1)} %compare_select_fusion), kind=kOutput, calls=%fused_computation.540 | convolution fusion | flops 62943232 | bytes 1474624 | tf_op jit(solution)/shard_map/bzyx,xk->bzyk/dot_general | solution.py:113
  67.7 3.2 %convolution_negate_fusion = f32[10,4,64,16]{2,3,1,0:T(8,128)S(1)} fusion(f32[10,4,64,128]{3,2,1,0:T(8,128)S(1)} %bitcast.755, s32[16]{0:T(128)S(1)} %compare_select_fusion), kind=kOutput, calls=%fused_computation.8 | convolution fusion | flops 62984192 | bytes 1474624 | tf_op jit(solution)/shard_map/bzyx,xk->bzyk/dot_general | solution.py:114
  70.9 2.5 %fusion.310 = f32[16,10,4,16]{3,0,2,1:T(8,128)S(1)} fusion(f32[10,4,64,16]{2,3,1,0:T(8,128)S(1)} %fusion.304, s32[16]{0:T(128)S(1)} %compare_select_fusion), kind=kOutput, calls=%fused_computation.546 | convolution fusion | flops 7878656 | bytes 204864 | tf_op jit(solution)/shard_map/bzyk,yj->bzjk/dot_general | solution.py:115
  73.4 2.5 %fusion.308 = f32[16,10,4,16]{3,0,2,1:T(8,128)S(1)} fusion(f32[10,4,64,16]{2,3,1,0:T(8,128)S(1)} %convolution_negate_fusion, s32[16]{0:T(128)S(1)} %compare_select_fusion), kind=kOutput, calls=%fused_computation.544 | convolution fusion | flops 7878656 | bytes 204864 | tf_op jit(solution)/shard_map/bzyk,yj->bzjk/dot_general | solution.py:118
  75.9 2.5 %fusion.3 = f32[10,4,16,16]{3,2,1,0:T(8,128)S(1)} fusion(f32[16,10,4,16]{3,0,2,1:T(8,128)S(1)} %fusion.310, f32[10,4,64,16]{2,3,1,0:T(8,128)S(1)} %convolution_negate_fusion, s32[16]{0:T(128)S(1)} %compare_select_fusion), kind=kOutput, calls=%fused_computation.7 | convolution fusion | flops 7888896 | bytes 245824 | tf_op jit(solution)/shard_map/bzyk,yj->bzjk/dot_general | solution.py:115
  78.6 2.5 %fusion.2 = f32[10,4,16,16]{3,2,1,0:T(8,128)S(1)} fusion(f32[16,10,4,16]{3,0,2,1:T(8,128)S(1)} %fusion.308, f32[10,4,64,16]{2,3,1,0:T(8,128)S(1)} %fusion.304, s32[16]{0:T(128)S(1)} %compare_select_fusion), kind=kOutput, calls=%fused_computation.5 | convolution fusion | flops 7888896 | bytes 245824 | tf_op jit(solution)/shard_map/bzyk,yj->bzjk/dot_general | solution.py:118
  81.3 0.5 fusion.346
  81.8 0.5 fusion.344
  82.3 0.5 fusion.7
  82.8 0.5 fusion.6
  83.3 0.7 pad_maximum_fusion.1
  84.1 0.3 fusion.282
  84.4 32.7 %all-reduce.3.cloned.1.call-done = f32[16,2,10,256]{3,0,2,1:T(8,128)} async-done(((f32[16,2,10,256]{3,0,2,1:T(8,128)}), f32[16,2,10,256]{3,0,2,1:T(8,128)}) %all-reduce.3.cloned.1.call-update) | async-done | bytes 327696
  117.1 0.9 fusion.285
  118.0 31.1 %all-gather = f32[16,4,5,256]{3,1,2,0:T(4,128)S(1)} all-gather(f32[2,4,5,256]{3,1,2,0:T(4,128)S(1)} %pad_maximum_fusion.26), channel_id=2, replica_groups=mesh['tm'=8,'space'=4] {'tm'}, dimensions={0}, use_global_device_ids=true | all-gather | bytes 368640 | tf_op jit(solution)/shard_map/all_gather | solution.py:171
  149.2 0.8 multiply_subtract_fusion
  150.1 5.7 %all_gather.7 = f32[16,2,5,256]{3,1,2,0:T(2,128)S(1)} all-gather(f32[4,2,5,256]{3,1,2,0:T(2,128)S(1)} %copy.243), channel_id=1, replica_groups=mesh['tm'=8,'space'=4] {'space'}, dimensions={0}, use_global_device_ids=true | all-gather | bytes 204800 | tf_op jit(solution)/shard_map/all_gather | solution.py:188
  157.0 0.5 fusion.13
  157.9 0.5 fusion.17
  158.4 0.5 fusion.4
  158.8 0.5 fusion.5
  159.3 1.2 fusion.302
  160.5 1.8 multiply_reduce_fusion
  162.4 6.6 %psum.14 = f32[]{:T(128)} all-reduce(f32[]{:T(128)} %get-tuple-element.60), channel_id=1, replica_groups=mesh['tm'=8,'space'=4] {'space'}, use_global_device_ids=true, to_apply=%region_4.5 | all-reduce | flops 1 | bytes 8 | tf_op jit(solution)/shard_map/psum | solution.py:212
  169.0 0.9 copy.250
  169.9 21.8 %psum.15 = f32[]{:T(128)} all-reduce(f32[]{:T(128)} %psum.14), channel_id=1, replica_groups=mesh['tm'=8,'space'=4] {'tm'}, use_global_device_ids=true, to_apply=%region_5.6 | all-reduce | flops 1 | bytes 8 | tf_op jit(solution)/shard_map/psum | solution.py:213
  (229 shorter events, 17.3 us)
Async XLA Ops:
  7.2 110.0 %all-reduce.3.cloned.1.call-start = ((), (), s32[]{:S(2)}) async-start(), calls=%async_computation | async-start | bytes 655360
  9.0 17.5 %collective-permute-start = (f32[5,1,64,128]{3,2,1,0:T(8,128)}, f32[5,1,64,128]{3,2,1,0:T(8,128)S(1)}, u32[]{:S(2)}, u32[]{:S(2)}) collective-permute-start(f32[5,1,64,128]{3,2,1,0:T(8,128)} %get-tuple-element.91), channel_id=1, source_target_pairs={{0,1},{1,2},{2,3},{3,0},{4,5},{5,6},{6,7},{7,4},{8,9},{9,10},{10,1... | collective-permute-start | bytes 491528 | tf_op jit(solution)/shard_map/ppermute | solution.py:27
  9.5 17.0 %collective-permute-start.1 = (f32[5,1,64,128]{3,2,1,0:T(8,128)}, f32[5,1,64,128]{3,2,1,0:T(8,128)S(1)}, u32[]{:S(2)}, u32[]{:S(2)}) collective-permute-start(f32[5,1,64,128]{3,2,1,0:T(8,128)} %get-tuple-element.90), channel_id=1, source_target_pairs={{1,0},{2,1},{3,2},{0,3},{5,4},{6,5},{7,6},{4,7},{9,8},{10,9},{11,1... | collective-permute-start | bytes 491528 | tf_op jit(solution)/shard_map/ppermute | solution.py:29
  16.0 10.4 %copy-start = (f32[1,5,4,64,128]{4,3,2,1,0:T(8,128)S(1)}, f32[1,5,4,64,128]{4,3,2,1,0:T(8,128)}, u32[]{:S(2)}) copy-start(f32[1,5,4,64,128]{4,3,2,1,0:T(8,128)} %param.2) | copy-start | bytes 1966084
  27.6 0.9 copy-start.7
  27.6 1.0 copy-start.8
  27.6 1.0 copy-start.9
  27.7 1.1 copy-start.10
  27.7 1.1 copy-start.11
  27.7 1.2 copy-start.12
  28.8 0.9 copy-start.2
  28.8 1.0 copy-start.3
  28.8 1.0 copy-start.4
  28.8 1.1 copy-start.5
  28.9 1.2 copy-start.6
  30.0 0.9 copy-start.13
  30.0 1.0 copy-start.14
  30.0 1.0 copy-start.15
  30.0 1.1 copy-start.16
  30.0 1.2 copy-start.17
  30.0 1.2 copy-start.18
  31.4 1.1 copy-start.1
  33.7 4.8 %collective-permute-start.2 = (f32[5,1,64,128]{3,2,1,0:T(8,128)S(1)}, f32[5,1,64,128]{3,2,1,0:T(8,128)S(1)}, u32[]{:S(2)}, u32[]{:S(2)}) collective-permute-start(f32[5,1,64,128]{3,2,1,0:T(8,128)S(1)} %get-tuple-element.84), channel_id=1, source_target_pairs={{0,1},{1,2},{2,3},{3,0},{4,5},{5,6},{6,7},{7,4},{8,9},{9,10},{10,1... | collective-permute-start | bytes 491528 | tf_op jit(solution)/shard_map/ppermute | solution.py:27
  34.4 5.7 %collective-permute-start.3 = (f32[5,1,64,128]{3,2,1,0:T(8,128)S(1)}, f32[5,1,64,128]{3,2,1,0:T(8,128)S(1)}, u32[]{:S(2)}, u32[]{:S(2)}) collective-permute-start(f32[5,1,64,128]{3,2,1,0:T(8,128)S(1)} %get-tuple-element.83), channel_id=1, source_target_pairs={{1,0},{2,1},{3,2},{0,3},{5,4},{6,5},{7,6},{4,7},{9,8},{10,9},{11,1... | collective-permute-start | bytes 491528 | tf_op jit(solution)/shard_map/ppermute | solution.py:29
  44.1 5.2 %collective-permute-start.4 = (f32[5,1,64,128]{3,2,1,0:T(8,128)S(1)}, f32[5,1,64,128]{3,2,1,0:T(8,128)S(1)}, u32[]{:S(2)}, u32[]{:S(2)}) collective-permute-start(f32[5,1,64,128]{3,2,1,0:T(8,128)S(1)} %get-tuple-element.76), channel_id=1, source_target_pairs={{0,1},{1,2},{2,3},{3,0},{4,5},{5,6},{6,7},{7,4},{8,9},{9,10},{10,1... | collective-permute-start | bytes 491528 | tf_op jit(solution)/shard_map/ppermute | solution.py:27
  45.0 5.6 %collective-permute-start.5 = (f32[5,1,64,128]{3,2,1,0:T(8,128)S(1)}, f32[5,1,64,128]{3,2,1,0:T(8,128)S(1)}, u32[]{:S(2)}, u32[]{:S(2)}) collective-permute-start(f32[5,1,64,128]{3,2,1,0:T(8,128)S(1)} %get-tuple-element.75), channel_id=1, source_target_pairs={{1,0},{2,1},{3,2},{0,3},{5,4},{6,5},{7,6},{4,7},{9,8},{10,9},{11,1... | collective-permute-start | bytes 491528 | tf_op jit(solution)/shard_map/ppermute | solution.py:29
  55.2 5.0 %collective-permute-start.6 = (f32[5,1,64,128]{3,2,1,0:T(8,128)S(1)}, f32[5,1,64,128]{3,2,1,0:T(8,128)S(1)}, u32[]{:S(2)}, u32[]{:S(2)}) collective-permute-start(f32[5,1,64,128]{3,2,1,0:T(8,128)S(1)} %get-tuple-element.68), channel_id=1, source_target_pairs={{0,1},{1,2},{2,3},{3,0},{4,5},{5,6},{6,7},{7,4},{8,9},{9,10},{10,1... | collective-permute-start | bytes 491528 | tf_op jit(solution)/shard_map/ppermute | solution.py:27
  56.1 5.3 %collective-permute-start.7 = (f32[5,1,64,128]{3,2,1,0:T(8,128)S(1)}, f32[5,1,64,128]{3,2,1,0:T(8,128)S(1)}, u32[]{:S(2)}, u32[]{:S(2)}) collective-permute-start(f32[5,1,64,128]{3,2,1,0:T(8,128)S(1)} %get-tuple-element.67), channel_id=1, source_target_pairs={{1,0},{2,1},{3,2},{0,3},{5,4},{6,5},{7,6},{4,7},{9,8},{10,9},{11,1... | collective-permute-start | bytes 491528 | tf_op jit(solution)/shard_map/ppermute | solution.py:29
  81.1 3.0 %copy-start.19 = (f32[8]{0:T(128)S(1)}, f32[8]{0:T(128)}, u32[]{:S(2)}) copy-start(f32[8]{0:T(128)} %maximum_convert_fusion) | copy-start | bytes 100
Sparse Core Ops, SparseCore 0:
  84.2 32.9 all-reduce.2
where the time goes:
time: 203 us; the launch traced here: 202 us
  blocking collectives  65.3 us (32%)
  waiting for transfers between devices  45.6 us (22%)
  matrix products  24.5 us (12%)
  local copies, waits for them, and re-layouts  22.2 us (11%)
  between operations  19.9 us (10%)
  other arithmetic  16 us (8%)
  starting transfers between devices  8.72 us (4%)
    unnamed x2, waiting for transfers between devices  32.7 us
    all_gather x1, blocking collectives, shards(): portion = lax.all_gather(jumps[None], 'tm', axis=0, tiled=True)  31.1 us
    psum x1, blocking collectives, shards(): every_sum = lax.psum(slice_sum, 'tm')  21.8 us
    ppermute x4, waiting for transfers between devices, with_halo(): lax.ppermute(tail, axis, [(i, (i + 1) % count) for i in range(count)])  8.68 us
    psum x1, blocking collectives, shards(): slice_sum = lax.psum(local_sum, 'space')  6.61 us
    all_gather x1, blocking collectives, shards(): portion = lax.all_gather(spectral_fix, 'space', axis=0, tiled=True)  5.73 us
    ppermute x4, starting transfers between devices, with_halo(): lax.ppermute(head, axis, [((i + 1) % count, i) for i in range(count)])  5.7 us
    unnamed x42, local copies, waits for them, and re-layouts  5.61 us
  transfers between devices with their start and end apart: 9, of which 7 were waited for; matrix products, arithmetic and copies ran while one was open for 7% of the time, Pallas kernels for 0%

commit v1 on v0

v1 whole, which is shorter than its diff:
```python
import functools
import math

import jax
import jax.numpy as jnp
import numpy as np
from jax import lax
from jax.experimental import pallas as pl
from jax.experimental.pallas import tpu as pltpu
from jax.sharding import PartitionSpec as P

viscosity = 0.08
diffusivity = 0.05
compress_rate = 0.25
time_step = 0.5
diffusion_number = 0.08
advect_xaxis = 0.2
advect_yaxis = 0.15
advect_zaxis = 0.1
epsilon = 1e-06
spread = (viscosity, viscosity, viscosity, None, diffusivity)


def hi_lo(table):
    table = np.asarray(table, np.float32)
    high = table.astype(jnp.bfloat16)
    low = (table - high.astype(np.float32)).astype(jnp.bfloat16)
    return high, low


@functools.lru_cache(None)
def make_tables(slab, width, rows, cols):
    depth = slab * width
    keep_y, keep_x = rows // 8, cols // 16
    ky = np.arange(2 * keep_y)
    ky = np.where(ky < keep_y, ky, ky - 2 * keep_y)
    kx = np.arange(keep_x)
    half = slab * 2 * keep_y
    turn = 2.0 * np.pi
    tables = {}
    angle = turn * kx[:, None] * np.arange(cols)[None, :] / cols
    wave = np.concatenate([np.cos(angle), -np.sin(angle)])
    high, low = hi_lo(wave)
    tables["xforward"] = np.block([[high, high], [low, np.zeros_like(low)]])
    weight = np.where(kx == 0, 1.0, 2.0)[:, None] / (depth * rows * cols)
    wave = np.concatenate([weight * np.cos(angle), -weight * np.sin(angle)])
    high, low = hi_lo(wave)
    tables["xinverse"] = np.concatenate([high, high, low])
    kz = np.arange(depth).reshape(width, 1, slab, 1)
    kyb = ky.reshape(1, 1, 1, -1)

    def joint(layers):
        layers = np.asarray(layers).reshape(-1, 1, 1, 1, 1, 1)
        cells = np.arange(rows).reshape(1, -1, 1, 1, 1, 1)
        theta = turn * (kz[None, None] * layers / depth + kyb[None, None] * cells / rows)
        return theta.reshape(-1, width, 1, slab, 2 * keep_y)

    def forward(layers):
        theta = joint(layers)
        c, s = np.cos(theta), np.sin(theta)
        real = np.concatenate([c, -s], axis=2)
        imag = np.concatenate([s, c], axis=2)
        count = theta.shape[0]
        return real.reshape(count, -1), imag.reshape(count, -1)

    inner = forward(range(slab))
    outer = forward([-1, slab])
    tables["yzforward"] = hi_lo(np.concatenate([inner[0], inner[1], outer[0], outer[1]]))
    theta = joint(range(slab))
    count = theta.shape[0]
    c, s = np.cos(theta), np.sin(theta)
    real = np.concatenate([c, -s], axis=2).reshape(count, -1).T
    imag = np.concatenate([s, c], axis=2).reshape(count, -1).T
    tables["yzinverse"] = hi_lo(np.concatenate([real, imag], axis=1))
    place = np.arange(width).reshape(-1, 1, 1, 1)
    theta = turn * ((kz.reshape(1, width, slab, 1) * place) % width) / width
    theta = np.broadcast_to(theta, (width, width, slab, 2 * keep_y)).reshape(width, width, half)
    c, s = np.cos(theta), np.sin(theta)
    tables["phase"] = np.stack(
        [np.concatenate([c, c], -1), np.concatenate([s, -s], -1)], axis=1
    ).astype(np.float32)
    tz = turn * np.arange(depth).reshape(width, 1, slab, 1) / depth
    ty = turn * ky.reshape(1, 1, 1, -1) / rows
    tx = turn * kx.reshape(1, -1, 1, 1) / cols
    keeper = (np.abs(ky) < keep_y).reshape(1, 1, 1, -1)
    real = 1.0 + diffusion_number * (2 * np.cos(tz) + 2 * np.cos(ty) + 2 * np.cos(tx) - 6.0)
    imag = -(advect_zaxis * np.sin(tz) + advect_yaxis * np.sin(ty) + advect_xaxis * np.sin(tx))
    real = (real * keeper).reshape(width, keep_x, half)
    imag = (imag * keeper).reshape(width, keep_x, half)
    tables["symbol"] = np.stack(
        [np.concatenate([real, real], -1), np.concatenate([-imag, imag], -1)], axis=1
    ).astype(np.float32)
    tables["share"] = np.broadcast_to(
        np.where(kx == 0, 1.0, 2.0)[:, None] / (depth * rows * cols), (keep_x, 2 * half)
    ).astype(np.float32)
    return tables


on_chip = pl.BlockSpec(memory_space=pltpu.VMEM)
in_scalars = pl.BlockSpec(memory_space=pltpu.SMEM)


def local_call(kernel, out_shape, operands, scratch=(), places=None):
    specs = [in_scalars if operand.dtype == jnp.int32 else on_chip for operand in operands]
    for index, spec in (places or {}).items():
        specs[index] = spec
    return pl.pallas_call(
        kernel,
        out_shape=out_shape,
        in_specs=specs,
        out_specs=jax.tree.map(lambda _: on_chip, out_shape),
        scratch_shapes=list(scratch),
        compiler_params=pltpu.CompilerParams(vmem_limit_bytes=16 * 1024 * 1024),
    )(*operands)


def split(values):
    high = values.astype(jnp.bfloat16)
    low = (values - high.astype(jnp.float32)).astype(jnp.bfloat16)
    return high, low


def dot(left, right):
    return jnp.dot(left, right, preferred_element_type=jnp.float32)


def three_pass(values, high_table, low_table):
    count = values.shape[0]
    high, low = split(values)
    both = dot(jnp.concatenate([high, low]), high_table)
    return both[:count] + both[count:] + dot(high, low_table)


def along_x(cells, table):
    high, low = split(cells)
    both = lax.dot_general(
        table,
        jnp.concatenate([high, low], axis=1),
        (((1,), (1,)), ((), ())),
        preferred_element_type=jnp.float32,
    )
    count = table.shape[0] // 2
    return both[:count] + both[count:]


def by_field(waves, fields, keep):
    lanes = waves.shape[1] // fields
    real = [waves[:keep, f * lanes : (f + 1) * lanes] for f in range(fields)]
    imag = [waves[keep:, f * lanes : (f + 1) * lanes] for f in range(fields)]
    return jnp.concatenate(real), jnp.concatenate(imag)


def flux(state, sign):
    u, v, w, p, s = state
    c = (0.5 * sign) * (advect_zaxis + w)
    momentum = viscosity + c
    return [
        momentum * u,
        momentum * v,
        momentum * w + (0.5 * sign) * p,
        (0.5 * sign * compress_rate) * w,
        (diffusivity + c) * s,
    ]


def level_rate(state, source):
    u, v, w, p, s = state
    rates = list(source)
    rows, cols = u.shape
    for axis, length, speed, velocity, lead in (
        (1, cols, advect_xaxis + u, u, 0),
        (0, rows, advect_yaxis + v, v, 1),
    ):
        half = 0.5 * speed
        for index, field in enumerate(state):
            if index == 3:
                plus = (0.5 * compress_rate) * velocity
                minus = -plus
            else:
                plus = (spread[index] + half) * field
                minus = (spread[index] - half) * field
            if index == lead:
                plus = plus + 0.5 * p
                minus = minus - 0.5 * p
            rates[index] = (
                rates[index] + pltpu.roll(plus, 1, axis) + pltpu.roll(minus, length - 1, axis)
            )
    for index, field in enumerate(state):
        if index != 3:
            rates[index] = rates[index] - (6.0 * spread[index]) * field
    return rates


def slab_rates(states, sources, put):
    slab = len(states)
    for layer in range(slab):
        rates = level_rate(states[layer](), sources[layer]())
        if layer > 0:
            rates = [r + g for r, g in zip(rates, flux(states[layer - 1](), 1.0))]
        if layer < slab - 1:
            rates = [r + g for r, g in zip(rates, flux(states[layer + 1](), -1.0))]
        put(layer, rates)


def reader(ref, layer):
    return lambda: [ref[f, layer] for f in range(ref.shape[0])]


def readers(ref):
    return [reader(ref, layer) for layer in range(ref.shape[1])]


def first_flux_kernel(state_ref, up_ref, down_ref, top_ref, bottom_ref, sems):
    last = state_ref.shape[1] - 1
    top = pltpu.make_async_copy(state_ref.at[:, last], top_ref, sems.at[0])
    bottom = pltpu.make_async_copy(state_ref.at[:, 0], bottom_ref, sems.at[1])
    top.start()
    bottom.start()
    fields = state_ref.shape[0]
    top.wait()
    for f, value in enumerate(flux([top_ref[f] for f in range(fields)], 1.0)):
        up_ref[f] = value
    bottom.wait()
    for f, value in enumerate(flux([bottom_ref[f] for f in range(fields)], -1.0)):
        down_ref[f] = value


def first_rate_kernel(state_ref, source_ref, table_ref, rate_ref, waves_ref):
    fields, slab, rows, cols = state_ref.shape

    def put(layer, rates):
        for f in range(fields):
            rate_ref[f, layer] = rates[f]

    slab_rates(readers(state_ref), readers(source_ref), put)
    keep = table_ref.shape[0] // 4
    cells = state_ref[...].reshape(fields * slab * rows, cols)
    real, imag = by_field(along_x(cells, table_ref[...]), fields, keep)
    lanes = real.shape[1]
    waves_ref[:, :lanes] = real
    waves_ref[:, lanes:] = imag


def edge_kernel(state_ref, rate_ref, below_ref, above_ref, edge_ref, up_ref, down_ref, *, step):
    fields, slab = state_ref.shape[:2]
    last = slab - 1
    top = [
        state_ref[f, last] + step * (rate_ref[f, last] + above_ref[f]) for f in range(fields)
    ]
    for f, value in enumerate(flux(top, 1.0)):
        edge_ref[1, f] = top[f]
        up_ref[f] = value
    bottom = [state_ref[f, 0] + step * (rate_ref[f, 0] + below_ref[f]) for f in range(fields)]
    for f, value in enumerate(flux(bottom, -1.0)):
        edge_ref[0, f] = bottom[f]
        down_ref[f] = value


def fill_stage(state_ref, rate_ref, edge_ref, stage_ref, step):
    fields, slab = state_ref.shape[:2]
    for f in range(fields):
        stage_ref[f, 0] = edge_ref[0, f]
        for layer in range(1, slab - 1):
            stage_ref[f, layer] = state_ref[f, layer] + step * rate_ref[f, layer]
        stage_ref[f, slab - 1] = edge_ref[1, f]


def rate_kernel(
    state_ref, rate_ref, edge_ref, source_ref, sum_ref, next_ref, total_ref, stage_ref, *, step, share
):
    fields = state_ref.shape[0]
    fill_stage(state_ref, rate_ref, edge_ref, stage_ref, step)

    def put(layer, rates):
        for f in range(fields):
            next_ref[f, layer] = rates[f]
            total_ref[f, layer] = sum_ref[f, layer] * share[0] + stage_ref[f, layer] * share[1]

    slab_rates(readers(stage_ref), readers(source_ref), put)


def forward_kernel(
    place_ref,
    state_ref,
    rate_ref,
    below_ref,
    above_ref,
    source_ref,
    sum_ref,
    shifted_ref,
    table_ref,
    high_ref,
    low_ref,
    phase_ref,
    out_ref,
    inner_ref,
    outer_ref,
    edge_ref,
    stage_ref,
    *,
    step,
    weight,
):
    fields, slab, rows, cols = state_ref.shape
    last = slab - 1
    for f in range(fields):
        edge_ref[0, f] = state_ref[f, 0] + step * (rate_ref[f, 0] + below_ref[f])
        edge_ref[1, f] = state_ref[f, last] + step * (rate_ref[f, last] + above_ref[f])
    fill_stage(state_ref, rate_ref, edge_ref, stage_ref, step)

    def put(layer, rates):
        for f in range(fields):
            inner_ref[f, layer] = (
                sum_ref[f, layer] + stage_ref[f, layer] * (1.0 / 3.0) + weight * rates[f]
            )

    slab_rates(readers(stage_ref), readers(source_ref), put)
    for f, value in enumerate(flux([edge_ref[0, f] for f in range(fields)], -1.0)):
        outer_ref[0, f] = weight * value
    for f, value in enumerate(flux([edge_ref[1, f] for f in range(fields)], 1.0)):
        outer_ref[1, f] = weight * value

    width = out_ref.shape[0]
    keep = table_ref.shape[0] // 4
    half = out_ref.shape[2] // 2
    place = place_ref[0]
    table = table_ref[...]
    real, imag = by_field(
        along_x(inner_ref[...].reshape(fields * slab * rows, cols), table), fields, keep
    )
    outer_cells = jnp.concatenate(
        [outer_ref[side, f] for f in range(fields) for side in range(2)]
    )
    outer_real, outer_imag = by_field(along_x(outer_cells, table), fields, keep)
    shifted = shifted_ref[...]
    lanes = real.shape[1]
    left = jnp.concatenate(
        [real - shifted[:, :lanes], imag - shifted[:, lanes:], outer_real, outer_imag], axis=1
    )
    waves = three_pass(left, high_ref[...], low_ref[...])
    for group in range(width):
        block = waves[:, group * 2 * half : (group + 1) * 2 * half]
        turned = (
            block * phase_ref[place, 0, group, :][None, :]
            + pltpu.roll(block, half, 1) * phase_ref[place, 1, group, :][None, :]
        )
        out_ref[lax.rem(group - place + width, width)] = turned


def coarse_kernel(place_ref, slot_ref, jump_ref, symbol_ref, share_ref, out_ref, kept_ref):
    slices, lines, lanes = jump_ref.shape
    keep = share_ref.shape[0]
    fields = lines // keep
    place = place_ref[0]
    moment = place_ref[1]
    real = symbol_ref[place, 0]
    imag = symbol_ref[place, 1]
    share = share_ref[...]
    current = [jnp.zeros((keep, lanes), jnp.float32) for _ in range(fields)]
    sizes = []
    kept_ref[0] = jnp.zeros((lines, lanes), jnp.float32)
    for moment_id in range(slices):
        total = jnp.zeros((keep, lanes), jnp.float32)
        for f in range(fields):
            total = total + current[f] * current[f]
        sizes.append(jnp.sum(total * share, axis=0, keepdims=True))
        if moment_id == slices - 1:
            break
        slot = slot_ref[moment_id]
        for f in range(fields):
            value = jump_ref[slot, f * keep : (f + 1) * keep, :] + current[f]
            current[f] = value * real + pltpu.roll(value, lanes // 2, 1) * imag
            kept_ref[moment_id + 1, f * keep : (f + 1) * keep, :] = current[f]
    out_ref[:lines, :] = kept_ref[moment]
    sums = jnp.sum(jnp.concatenate(sizes), axis=1, keepdims=True)
    spare = out_ref.shape[0] - lines - slices
    if spare > 0:
        out_ref[lines + slices :, :] = jnp.zeros((spare, lanes), jnp.float32)
    out_ref[lines : lines + slices, :] = jnp.broadcast_to(sums, (slices, lanes))


def inverse_kernel(
    place_ref,
    *refs,
    width,
    scales,
):
    block_refs = refs[:width]
    (
        fine_ref,
        below_ref,
        above_ref,
        high_ref,
        low_ref,
        table_ref,
        phase_ref,
        ends_ref,
        norm_ref,
        order_ref,
    ) = refs[width:]
    fields, slab, rows, cols = fine_ref.shape
    place = place_ref[0]
    moment = place_ref[1]
    lines, lanes = order_ref.shape[1:]
    keep = lines // fields
    sums = None
    for step in range(width):
        group = lax.rem(place - step + width, width)
        block = block_refs[step][:lines, :]
        order_ref[group] = (
            block * phase_ref[place, 0, group, :][None, :]
            - pltpu.roll(block, lanes // 2, 1) * phase_ref[place, 1, group, :][None, :]
        )
        part = block_refs[step][lines:, :]
        sums = part if sums is None else sums + part
    line = lax.broadcasted_iota(jnp.int32, sums.shape, 0)
    own = jnp.sum(jnp.where(line == moment, sums, 0.0), axis=0, keepdims=True)
    whole = jnp.sum(sums, axis=0, keepdims=True)
    norm_ref[0:1, :] = jnp.sqrt(own * scales[0] + epsilon)
    norm_ref[1:2, :] = jnp.sqrt(whole * scales[1] + epsilon)
    left = jnp.concatenate([order_ref[group] for group in range(width)], axis=1)
    waves = three_pass(left, high_ref[...], low_ref[...])
    count = slab * rows
    for f in range(fields):
        both = jnp.concatenate(
            [waves[f * keep : (f + 1) * keep, :count], waves[f * keep : (f + 1) * keep, count:]]
        )
        high, low = split(both)
        change = lax.dot_general(
            jnp.concatenate([high, low, high]),
            table_ref[...],
            (((0,), (0,)), ((), ())),
            preferred_element_type=jnp.float32,
        ).reshape(slab, rows, cols)
        for layer in range(slab):
            value = fine_ref[f, layer] + change[layer]
            if layer == 0:
                value = value + below_ref[f]
            if layer == slab - 1:
                value = value + above_ref[f]
            ends_ref[f, layer] = value


def halo(up, down):
    count = lax.axis_size("space")
    ups = [(i, (i + 1) % count) for i in range(count)]
    downs = [((i + 1) % count, i) for i in range(count)]
    return lax.ppermute(up, "space", ups), lax.ppermute(down, "space", downs)


def radices(count):
    parts = []
    while count % 4 == 0 and count > 4:
        parts.append(4)
        count //= 4
    if count > 1:
        parts.append(count)
    return sorted(parts)


def shards(starts, source):
    state_now = starts[0]
    fields, slab, rows, cols = state_now.shape
    width = lax.axis_size("space")
    slices = lax.axis_size("tm")
    depth = slab * width
    keep_y, keep_x = rows // 8, cols // 16
    lines, lanes = fields * keep_x, 2 * slab * 2 * keep_y
    tables = make_tables(slab, width, rows, cols)
    place = lax.axis_index("space").astype(jnp.int32)
    moment = lax.axis_index("tm").astype(jnp.int32)
    where = jnp.stack([place, moment])
    real = jnp.float32

    layer_shape = jax.ShapeDtypeStruct((fields, rows, cols), real)
    edge_shape = jax.ShapeDtypeStruct((2, fields, rows, cols), real)
    slab_shape = jax.ShapeDtypeStruct((fields, slab, rows, cols), real)
    layer = pltpu.VMEM((fields, rows, cols), real)
    whole_slab = pltpu.VMEM((fields, slab, rows, cols), real)

    up, down = local_call(
        first_flux_kernel,
        (layer_shape, layer_shape),
        [state_now],
        [layer, layer, pltpu.SemaphoreType.DMA((2,))],
        {0: pl.BlockSpec(memory_space=pl.ANY)},
    )
    below, above = halo(up, down)
    rates, start_waves = local_call(
        first_rate_kernel,
        (slab_shape, jax.ShapeDtypeStruct((lines, 2 * slab * rows), real)),
        [state_now, source, tables["xforward"]],
    )
    next_waves = lax.ppermute(start_waves, "tm", [(i + 1, i) for i in range(slices - 1)])
    total = state_now
    for stage in range(2):
        step = 0.5 * time_step
        edge, up, down = local_call(
            functools.partial(edge_kernel, step=step),
            (edge_shape, layer_shape, layer_shape),
            [state_now, rates, below, above],
        )
        below, above = halo(up, down)
        share = ((-1.0 / 3.0, 1.0 / 3.0), (1.0, 2.0 / 3.0))[stage]
        rates, total = local_call(
            functools.partial(rate_kernel, step=step, share=share),
            (slab_shape, slab_shape),
            [state_now, rates, edge, source, total],
            [whole_slab],
        )
    waves, fine_inner, fine_outer = local_call(
        functools.partial(forward_kernel, step=time_step, weight=time_step / 6.0),
        (
            jax.ShapeDtypeStruct((width, lines, lanes), real),
            slab_shape,
            edge_shape,
        ),
        [
            where,
            state_now,
            rates,
            below,
            above,
            source,
            total,
            next_waves,
            tables["xforward"],
            *tables["yzforward"],
            tables["phase"],
        ],
        [pltpu.VMEM((2, fields, rows, cols), real), whole_slab],
    )
    jump = waves[0]
    for step in range(1, width):
        jump = jump + lax.ppermute(
            waves[step], "space", [(i, (i + step) % width) for i in range(width)]
        )

    up, down, jump = lax.optimization_barrier((fine_outer[1], fine_outer[0], jump))
    below, above = halo(up, down)

    jumps = jump[None]
    stride = 1
    slots = jnp.zeros((slices,), jnp.int32)
    ids = jnp.arange(slices, dtype=jnp.int32)
    for radix in radices(slices):
        parts = [jumps]
        for step in range(1, radix):
            pairs = []
            for i in range(slices):
                digit = i // stride % radix
                pairs.append((i, i + ((digit + step) % radix - digit) * stride))
            parts.append(lax.ppermute(jumps, "tm", pairs))
        jumps = jnp.concatenate(parts)
        slots = slots + (moment // stride - ids // stride) % radix * stride
        stride *= radix

    message = local_call(
        coarse_kernel,
        jax.ShapeDtypeStruct((lines + -(-slices // 8) * 8, lanes), real),
        [where, slots, jumps, tables["symbol"], tables["share"]],
        [pltpu.VMEM((slices, lines, lanes), real)],
    )
    blocks = [message]
    for step in range(1, width):
        blocks.append(
            lax.ppermute(message, "space", [(i, (i + step) % width) for i in range(width)])
        )
    cells = fields * depth * rows * cols
    ends, norms = local_call(
        functools.partial(
            inverse_kernel, width=width, scales=(1.0 / cells, 1.0 / (cells * slices))
        ),
        (
            jax.ShapeDtypeStruct((fields, slab, rows, cols), real),
            jax.ShapeDtypeStruct((2, lanes), real),
        ),
        [
            where,
            *blocks,
            fine_inner,
            below,
            above,
            *tables["yzinverse"],
            tables["xinverse"],
            tables["phase"],
        ],
        [pltpu.VMEM((width, lines, lanes), real)],
    )
    return ends[None], norms[0, :1], norms[1, :1]


def solution(mesh):
    in_specs = (P("tm", None, "space", None, None), P(None, "space", None, None))
    out_specs = (P("tm", None, "space", None, None), P("tm"), P())
    return jax.shard_map(shards, mesh=mesh, in_specs=in_specs, out_specs=out_specs, check_vma=False)
```

time: 203 us -> 53.3 us (0.26)
  blocking collectives: 65.3 us -> 0 us
  waiting for transfers between devices: 45.6 us -> 14.3 us
  matrix products: 24.5 us -> 0 us
  between operations: 19.9 us -> 0.8 us
  local copies, waits for them, and re-layouts: 22.2 us -> 5.09 us
  other arithmetic: 16 us -> 0.1 us
  starting transfers between devices: 8.72 us -> 21.9 us
  Pallas kernels: 0 us -> 10.6 us
    all_gather x2 -> x0, blocking collectives: 36.8 us -> none  [the longest x1 31.1 us: shards(): portion = lax.all_gather(jumps[None], 'tm', axis=0, tiled=True)]
    unnamed x2 -> x0, waiting for transfers between devices: 32.7 us -> none
    psum x2 -> x0, blocking collectives: 28.5 us -> none  [the longest x1 21.8 us: shards(): every_sum = lax.psum(slice_sum, 'tm')]
    dot_general x20 -> x0, matrix products: 24.5 us -> none  [the longest x1 3.22 us: shards(): imag_x = -jnp.einsum('bzyx,xk->bzyk', stacked, xsines, precision=highest)]
    ppermute x8 -> x19, starting transfers between devices: 8.69 us -> 21.9 us  [the longest x8 8.3 us: halo(): return (lax.ppermute(up, 'space', ups), lax.ppermute(down, 'space', downs))]
    slice x125 -> x1, local copies, waits for them, and re-layouts: 11.9 us -> 0.52 us  [shards(): return (ends[None], norms[0, :1], norms[1, :1])]
    pallas_call x0 -> x9, Pallas kernels: none -> 10.6 us  [local_call(): pl.pallas_call(kernel, out_shape=out_shape, in_specs=specs, out_specs=jax...]
    unnamed x14 -> x0, other arithmetic: 3.68 us -> none
  transfers between devices with their start and end apart: 9 -> 19, of which waited for: 7 -> 15; matrix products, arithmetic and copies ran while one was open for 7% -> 0% of each run, Pallas kernels for 0% -> 10%
where the time goes in v1:
time: 53.3 us; the launch traced here: 52.7 us
  starting transfers between devices  21.9 us (41%)
  waiting for transfers between devices  14.3 us (27%)
  Pallas kernels  10.6 us (20%)
  local copies, waits for them, and re-layouts  5.09 us (10%)
  between operations  0.8 us (2%)
    pallas_call x9, Pallas kernels, local_call(): pl.pallas_call(kernel, out_shape=out_shape, in_specs=specs, out_specs=jax...  10.6 us
    ppermute x8, starting transfers between devices, halo(): return (lax.ppermute(up, 'space', ups), lax.ppermute(down, 'space', downs))  8.3 us
    ppermute x8, waiting for transfers between devices, halo(): return (lax.ppermute(up, 'space', ups), lax.ppermute(down, 'space', downs))  7.72 us
    ppermute x4, starting transfers between devices, shards(): parts.append(lax.ppermute(jumps, 'tm', pairs))  5.95 us
    unnamed x36, local copies, waits for them, and re-layouts  4.54 us
    ppermute x4, waiting for transfers between devices, shards(): parts.append(lax.ppermute(jumps, 'tm', pairs))  3.64 us
    ppermute x3, starting transfers between devices, shards(): lax.ppermute(waves[step], 'space', [(i, (i + step) % width) for i in rang...  3.5 us
    ppermute x3, starting transfers between devices, shards(): lax.ppermute(message, 'space', [(i, (i + step) % width) for i in range(wi...  2.85 us
  transfers between devices with their start and end apart: 19, of which 15 were waited for; matrix products, arithmetic and copies ran while one was open for 0% of the time, Pallas kernels for 10%

profile of v1, /device:TPU:0, one launch (start us, length us, event | category | flops | bytes accessed | tf_op | source)
XLA Modules:
  0.0 52.7 jit_solution(11481547817042492791)
XLA Ops:
  0.6 0.0 copy-start.12
  0.6 0.0 copy-start
  0.7 1.1 %copy-done = f32[1,5,4,64,128]{4,3,2,1,0:T(8,128)S(1)} copy-done((f32[1,5,4,64,128]{4,3,2,1,0:T(8,128)S(1)}, f32[1,5,4,64,128]{4,3,2,1,0:T(8,128)}, u32[]{:S(2)}) %copy-start) | copy-done | bytes 655384
  1.7 0.1 shard_map.131
  1.9 0.5 %collective-permute-start = (f32[5,64,128]{2,1,0:T(8,128)S(1)}, f32[5,64,128]{2,1,0:T(8,128)S(1)}, u32[]{:S(2)}, u32[]{:S(2)}) collective-permute-start(f32[5,64,128]{2,1,0:T(8,128)S(1)} %get-tuple-element.26), channel_id=1, source_target_pairs={{0,1},{1,2},{2,3},{3,0},{4,5},{5,6},{6,7},{7,4},{8,9},{9,10},{10,1... | collective-permute-start | bytes 491528 | tf_op jit(solution)/shard_map/ppermute | solution.py:448
  2.4 2.0 %collective-permute-start.1 = (f32[5,64,128]{2,1,0:T(8,128)S(1)}, f32[5,64,128]{2,1,0:T(8,128)S(1)}, u32[]{:S(2)}, u32[]{:S(2)}) collective-permute-start(f32[5,64,128]{2,1,0:T(8,128)S(1)} %get-tuple-element.27), channel_id=1, source_target_pairs={{1,0},{2,1},{3,2},{0,3},{5,4},{6,5},{7,6},{4,7},{9,8},{10,9},{11,1... | collective-permute-start | bytes 491528 | tf_op jit(solution)/shard_map/ppermute | solution.py:448
  4.4 0.0 copy-done.12
  4.4 0.0 copy-done.2
  4.4 1.3 %shard_map.130 = (f32[5,4,64,128]{3,2,1,0:T(8,128)S(1)}, f32[40,512]{1,0:T(8,128)}) custom-call(f32[5,4,64,128]{3,2,1,0:T(8,128)S(1)} %bitcast.25, f32[5,4,64,128]{3,2,1,0:T(8,128)S(1)} %copy-done.2, bf16[32,256]{1,0:T(8,128)(2,1)S(1)} %copy-done.12), custom_call_target="tpu_custom_call" | custom-call | tf_op jit(solution)/shard_map/pallas_call | solution.py:107
  5.7 1.7 %collective-permute-done.below_ref = f32[5,64,128]{2,1,0:T(8,128)S(1)} collective-permute-done((f32[5,64,128]{2,1,0:T(8,128)S(1)}, f32[5,64,128]{2,1,0:T(8,128)S(1)}, u32[]{:S(2)}, u32[]{:S(2)}) %collective-permute-start) | collective-permute-done | bytes 163872 | tf_op jit(solution)/shard_map/ppermute | solution.py:448
  7.3 1.6 %collective-permute-done.1.above_ref = f32[5,64,128]{2,1,0:T(8,128)S(1)} collective-permute-done((f32[5,64,128]{2,1,0:T(8,128)S(1)}, f32[5,64,128]{2,1,0:T(8,128)S(1)}, u32[]{:S(2)}, u32[]{:S(2)}) %collective-permute-start.1) | collective-permute-done | bytes 163872 | tf_op jit(solution)/shard_map/ppermute | solution.py:448
  8.9 0.8 %shard_map.132 = (f32[2,5,64,128]{3,2,1,0:T(8,128)S(1)}, f32[5,64,128]{2,1,0:T(8,128)}, f32[5,64,128]{2,1,0:T(8,128)}) custom-call(f32[5,4,64,128]{3,2,1,0:T(8,128)S(1)} %bitcast.26, f32[5,4,64,128]{3,2,1,0:T(8,128)S(1)} %get-tuple-element.25.rate_ref, f32[5,64,128]{2,1,0:T(8,128)S(1)} %collective-permute-done.below_ref, ...), custom_call_target="tpu_custom_call" | custom-call | tf_op jit(solution)/shard_map/pallas_call | solution.py:107
  9.7 0.7 %copy-done.7 = f32[2,5,64,128]{3,2,1,0:T(8,128)} copy-done((f32[2,5,64,128]{3,2,1,0:T(8,128)}, f32[2,5,64,128]{3,2,1,0:T(8,128)S(1)}, u32[]{:S(2)}) %copy-start.7) | copy-done | bytes 327704
  10.4 0.8 %collective-permute-start.2 = (f32[5,64,128]{2,1,0:T(8,128)}, f32[5,64,128]{2,1,0:T(8,128)S(1)}, u32[]{:S(2)}, u32[]{:S(2)}) collective-permute-start(f32[5,64,128]{2,1,0:T(8,128)} %get-tuple-element.30), channel_id=1, source_target_pairs={{0,1},{1,2},{2,3},{3,0},{4,5},{5,6},{6,7},{7,4},{8,9},{9,10},{10,1... | collective-permute-start | bytes 491528 | tf_op jit(solution)/shard_map/ppermute | solution.py:448
  11.3 1.3 %collective-permute-start.3 = (f32[5,64,128]{2,1,0:T(8,128)}, f32[5,64,128]{2,1,0:T(8,128)}, u32[]{:S(2)}, u32[]{:S(2)}) collective-permute-start(f32[5,64,128]{2,1,0:T(8,128)} %get-tuple-element.31), channel_id=1, source_target_pairs={{1,0},{2,1},{3,2},{0,3},{5,4},{6,5},{7,6},{4,7},{9,8},{10,9},{11,1... | collective-permute-start | bytes 491528 | tf_op jit(solution)/shard_map/ppermute | solution.py:448
  12.5 1.3 %collective-permute-start.6 = (f32[40,512]{1,0:T(8,128)}, f32[40,512]{1,0:T(8,128)S(1)}, u32[]{:S(2)}, u32[]{:S(2)}) collective-permute-start(f32[40,512]{1,0:T(8,128)} %get-tuple-element.38), channel_id=1, source_target_pairs={{4,0},{8,4},{12,8},{16,12},{20,16},{24,20},{28,24},{5,1},{9,5},{13... | collective-permute-start | bytes 245768 | tf_op jit(solution)/shard_map/ppermute | solution.py:494
  13.8 0.0 copy-done.1
  13.8 0.0 copy-start.8
  13.9 1.0 %copy-done.8 = f32[2,5,64,128]{3,2,1,0:T(8,128)S(1)} copy-done((f32[2,5,64,128]{3,2,1,0:T(8,128)S(1)}, f32[2,5,64,128]{3,2,1,0:T(8,128)}, u32[]{:S(2)}) %copy-start.8) | copy-done | bytes 327704
  14.8 0.6 %shard_map.133 = (f32[5,4,64,128]{3,2,1,0:T(8,128)S(1)}, f32[5,4,64,128]{3,2,1,0:T(8,128)S(1)}) custom-call(f32[5,4,64,128]{3,2,1,0:T(8,128)S(1)} %bitcast.27, f32[5,4,64,128]{3,2,1,0:T(8,128)S(1)} %get-tuple-element.25.rate_ref, f32[2,5,64,128]{3,2,1,0:T(8,128)S(1)} %copy-done.8, f32[5,4,64,128]{3,2,1,0:T(8,128)S(1)} %copy-done.2, ...), custom_call_target="tpu_custom_call" | custom-call | tf_op jit(solution)/shard_map/pallas_call | solution.py:107
  15.5 0.3 collective-permute-done.2.below_ref
  15.7 1.4 %collective-permute-done.3.above_ref = f32[5,64,128]{2,1,0:T(8,128)} collective-permute-done((f32[5,64,128]{2,1,0:T(8,128)}, f32[5,64,128]{2,1,0:T(8,128)}, u32[]{:S(2)}, u32[]{:S(2)}) %collective-permute-start.3) | collective-permute-done | bytes 163872 | tf_op jit(solution)/shard_map/ppermute | solution.py:448
  17.2 1.7 %shard_map.134 = (f32[2,5,64,128]{3,2,1,0:T(8,128)S(1)}, f32[5,64,128]{2,1,0:T(8,128)}, f32[5,64,128]{2,1,0:T(8,128)}) custom-call(f32[5,4,64,128]{3,2,1,0:T(8,128)S(1)} %bitcast.29, f32[5,4,64,128]{3,2,1,0:T(8,128)S(1)} %get-tuple-element.29.rate_ref, f32[5,64,128]{2,1,0:T(8,128)S(1)} %collective-permute-done.2.below_ref, ...), custom_call_target="tpu_custom_call" | custom-call | tf_op jit(solution)/shard_map/pallas_call | solution.py:107
  18.8 0.7 %copy-done.9 = f32[2,5,64,128]{3,2,1,0:T(8,128)} copy-done((f32[2,5,64,128]{3,2,1,0:T(8,128)}, f32[2,5,64,128]{3,2,1,0:T(8,128)S(1)}, u32[]{:S(2)}) %copy-start.9) | copy-done | bytes 327704
  19.6 0.8 %collective-permute-start.4 = (f32[5,64,128]{2,1,0:T(8,128)}, f32[5,64,128]{2,1,0:T(8,128)S(1)}, u32[]{:S(2)}, u32[]{:S(2)}) collective-permute-start(f32[5,64,128]{2,1,0:T(8,128)} %get-tuple-element.35), channel_id=1, source_target_pairs={{0,1},{1,2},{2,3},{3,0},{4,5},{5,6},{6,7},{7,4},{8,9},{9,10},{10,1... | collective-permute-start | bytes 491528 | tf_op jit(solution)/shard_map/ppermute | solution.py:448
  20.4 1.1 %collective-permute-start.5 = (f32[5,64,128]{2,1,0:T(8,128)}, f32[5,64,128]{2,1,0:T(8,128)}, u32[]{:S(2)}, u32[]{:S(2)}) collective-permute-start(f32[5,64,128]{2,1,0:T(8,128)} %get-tuple-element.36), channel_id=1, source_target_pairs={{1,0},{2,1},{3,2},{0,3},{5,4},{6,5},{7,6},{4,7},{9,8},{10,9},{11,1... | collective-permute-start | bytes 491528 | tf_op jit(solution)/shard_map/ppermute | solution.py:448
  21.5 0.1 pad_add_fusion.place_ref
  21.6 1.0 %copy-done.10 = f32[2,5,64,128]{3,2,1,0:T(8,128)S(1)} copy-done((f32[2,5,64,128]{3,2,1,0:T(8,128)S(1)}, f32[2,5,64,128]{3,2,1,0:T(8,128)}, u32[]{:S(2)}) %copy-start.10) | copy-done | bytes 327704
  22.5 0.6 %shard_map.135 = (f32[5,4,64,128]{3,2,1,0:T(8,128)S(1)}, f32[5,4,64,128]{3,2,1,0:T(8,128)S(1)}) custom-call(f32[5,4,64,128]{3,2,1,0:T(8,128)S(1)} %bitcast.30, f32[5,4,64,128]{3,2,1,0:T(8,128)S(1)} %get-tuple-element.29.rate_ref, f32[2,5,64,128]{3,2,1,0:T(8,128)S(1)} %copy-done.10, f32[5,4,64,128]{3,2,1,0:T(8,128)S(1)} %copy-done.2, ...), custom_call_target="tpu_custom_call" | custom-call | tf_op jit(solution)/shard_map/pallas_call | solution.py:107
  23.2 0.0 collective-permute-done.6.shifted_ref
  23.2 1.5 %collective-permute-done.4.below_ref = f32[5,64,128]{2,1,0:T(8,128)S(1)} collective-permute-done((f32[5,64,128]{2,1,0:T(8,128)}, f32[5,64,128]{2,1,0:T(8,128)S(1)}, u32[]{:S(2)}, u32[]{:S(2)}) %collective-permute-start.4) | collective-permute-done | bytes 163872 | tf_op jit(solution)/shard_map/ppermute | solution.py:448
  24.7 1.3 %collective-permute-done.5.above_ref = f32[5,64,128]{2,1,0:T(8,128)} collective-permute-done((f32[5,64,128]{2,1,0:T(8,128)}, f32[5,64,128]{2,1,0:T(8,128)}, u32[]{:S(2)}, u32[]{:S(2)}) %collective-permute-start.5) | collective-permute-done | bytes 163872 | tf_op jit(solution)/shard_map/ppermute | solution.py:448
  26.0 0.0 copy-done.3
  26.0 2.3 %shard_map.136 = (f32[4,40,128]{2,1,0:T(8,128)S(1)}, f32[5,4,64,128]{3,2,1,0:T(8,128)S(1)}, f32[2,5,64,128]{3,2,1,0:T(8,128)S(1)}) custom-call(s32[2]{0:T(128)S(1)} %pad_add_fusion.place_ref, f32[5,4,64,128]{3,2,1,0:T(8,128)S(1)} %bitcast.31, f32[5,4,64,128]{3,2,1,0:T(8,128)S(1)} %get-tuple-element.34.rate_ref, ...), custom_call_target="tpu_custom_call" | custom-call | tf_op jit(solution)/shard_map/pallas_call | solution.py:107
  28.3 0.9 %collective-permute-start.7 = (f32[40,128]{1,0:T(8,128)S(1)}, f32[40,128]{1,0:T(8,128)S(1)}, u32[]{:S(2)}, u32[]{:S(2)}) collective-permute-start(f32[40,128]{1,0:T(8,128)S(1)} %get-tuple-element.49), channel_id=1, source_target_pairs={{0,1},{1,2},{2,3},{3,0},{4,5},{5,6},{6,7},{7,4},{8,9},{9,10},{10,1... | collective-permute-start | bytes 61448 | tf_op jit(solution)/shard_map/ppermute | solution.py:535
  29.2 1.5 %collective-permute-start.8 = (f32[40,128]{1,0:T(8,128)S(1)}, f32[40,128]{1,0:T(8,128)S(1)}, u32[]{:S(2)}, u32[]{:S(2)}) collective-permute-start(f32[40,128]{1,0:T(8,128)S(1)} %get-tuple-element.51), channel_id=1, source_target_pairs={{0,2},{1,3},{2,0},{3,1},{4,6},{5,7},{6,4},{7,5},{8,10},{9,11},{10,... | collective-permute-start | bytes 61448 | tf_op jit(solution)/shard_map/ppermute | solution.py:535
  30.7 1.1 %collective-permute-start.9 = (f32[40,128]{1,0:T(8,128)S(1)}, f32[40,128]{1,0:T(8,128)S(1)}, u32[]{:S(2)}, u32[]{:S(2)}) collective-permute-start(f32[40,128]{1,0:T(8,128)S(1)} %get-tuple-element.50), channel_id=1, source_target_pairs={{0,3},{1,0},{2,1},{3,2},{4,7},{5,4},{6,5},{7,6},{8,11},{9,8},{10,9... | collective-permute-start | bytes 61448 | tf_op jit(solution)/shard_map/ppermute | solution.py:535
  31.8 0.0 copy-start.5
  31.9 0.0 collective-permute-done.7
  31.9 1.1 %collective-permute-done.8 = f32[40,128]{1,0:T(8,128)S(1)} collective-permute-done((f32[40,128]{1,0:T(8,128)S(1)}, f32[40,128]{1,0:T(8,128)S(1)}, u32[]{:S(2)}, u32[]{:S(2)}) %collective-permute-start.8) | collective-permute-done | bytes 20512 | tf_op jit(solution)/shard_map/ppermute | solution.py:535
  33.0 0.3 collective-permute-done.9
  33.3 1.0 %collective-permute-start.10 = (f32[1,40,128]{2,1,0:T(8,128)S(1)}, f32[1,40,128]{2,1,0:T(8,128)S(1)}, u32[]{:S(2)}, u32[]{:S(2)}) collective-permute-start(f32[1,40,128]{2,1,0:T(8,128)S(1)} %bitcast.32), channel_id=1, source_target_pairs={{0,4},{4,0},{8,12},{12,8},{16,20},{20,16},{24,28},{28,24},{1,5},{5... | collective-permute-start | bytes 61448 | tf_op jit(solution)/shard_map/ppermute | solution.py:553
  34.3 0.2 collective-permute-start.17
  34.5 1.6 %collective-permute-start.18 = (f32[5,64,128]{2,1,0:T(8,128)S(1)}, f32[5,64,128]{2,1,0:T(8,128)S(1)}, u32[]{:S(2)}, u32[]{:S(2)}) collective-permute-start(f32[5,64,128]{2,1,0:T(8,128)S(1)} %get-tuple-element.44), channel_id=1, source_target_pairs={{1,0},{2,1},{3,2},{0,3},{5,4},{6,5},{7,6},{4,7},{9,8},{10,9},{11,1... | collective-permute-start | bytes 491528 | tf_op jit(solution)/shard_map/ppermute | solution.py:448
  36.1 1.0 %collective-permute-done.10 = f32[1,40,128]{2,1,0:T(8,128)S(1)} collective-permute-done((f32[1,40,128]{2,1,0:T(8,128)S(1)}, f32[1,40,128]{2,1,0:T(8,128)S(1)}, u32[]{:S(2)}, u32[]{:S(2)}) %collective-permute-start.10) | collective-permute-done | bytes 20512 | tf_op jit(solution)/shard_map/ppermute | solution.py:553
  37.1 1.0 %collective-permute-start.11 = (f32[2,40,128]{2,1,0:T(8,128)S(1)}, f32[2,40,128]{2,1,0:T(8,128)S(1)}, u32[]{:S(2)}, u32[]{:S(2)}) collective-permute-start(f32[2,40,128]{2,1,0:T(8,128)S(1)} %pad_maximum_fusion), channel_id=1, source_target_pairs={{0,8},{4,12},{8,16},{12,20},{16,24},{20,28},{24,0},{28,4},{1,9},{5... | collective-permute-start | bytes 122888 | tf_op jit(solution)/shard_map/ppermute | solution.py:553
  38.1 2.6 %collective-permute-start.12 = (f32[2,40,128]{2,1,0:T(8,128)S(1)}, f32[2,40,128]{2,1,0:T(8,128)S(1)}, u32[]{:S(2)}, u32[]{:S(2)}) collective-permute-start(f32[2,40,128]{2,1,0:T(8,128)S(1)} %pad_maximum_fusion), channel_id=1, source_target_pairs={{0,16},{4,20},{8,24},{12,28},{16,0},{20,4},{24,8},{28,12},{1,17},{... | collective-permute-start | bytes 122888 | tf_op jit(solution)/shard_map/ppermute | solution.py:553
  40.7 1.3 %collective-permute-start.13 = (f32[2,40,128]{2,1,0:T(8,128)S(1)}, f32[2,40,128]{2,1,0:T(8,128)S(1)}, u32[]{:S(2)}, u32[]{:S(2)}) collective-permute-start(f32[2,40,128]{2,1,0:T(8,128)S(1)} %pad_maximum_fusion), channel_id=1, source_target_pairs={{0,24},{4,28},{8,0},{12,4},{16,8},{20,12},{24,16},{28,20},{1,25},{... | collective-permute-start | bytes 122888 | tf_op jit(solution)/shard_map/ppermute | solution.py:553
  42.0 1.1 %collective-permute-done.11 = f32[2,40,128]{2,1,0:T(8,128)S(1)} collective-permute-done((f32[2,40,128]{2,1,0:T(8,128)S(1)}, f32[2,40,128]{2,1,0:T(8,128)S(1)}, u32[]{:S(2)}, u32[]{:S(2)}) %collective-permute-start.11) | collective-permute-done | bytes 40992 | tf_op jit(solution)/shard_map/ppermute | solution.py:553
  43.1 0.5 collective-permute-done.12
  43.6 1.1 %collective-permute-done.13 = f32[2,40,128]{2,1,0:T(8,128)S(1)} collective-permute-done((f32[2,40,128]{2,1,0:T(8,128)S(1)}, f32[2,40,128]{2,1,0:T(8,128)S(1)}, u32[]{:S(2)}, u32[]{:S(2)}) %collective-permute-start.13) | collective-permute-done | bytes 40992 | tf_op jit(solution)/shard_map/ppermute | solution.py:553
  44.7 0.0 copy-start.14
  44.7 1.1 %shard_map.137.refs_0_ = f32[48,128]{1,0:T(8,128)S(1)} custom-call(s32[2]{0:T(128)S(1)} %pad_add_fusion.place_ref, s32[8]{0:T(128)S(1)} %fusion.2.slot_ref, f32[8,40,128]{2,1,0:T(8,128)S(1)} %constant_dynamic-update-slice_fusion.jump_ref, f32[4,2,8,128]{3,2,1,0:T(8,128)S(1)} %copy-done.13, f32[8,128]{1,0:T(8,128)S(1)} %copy-done.15), custom_call_target="tpu_custom_call" | custom-call | tf_op jit(solution)/shard_map/pallas_call | solution.py:107
  45.8 0.0 collective-permute-start.14
  45.8 1.4 %collective-permute-start.15 = (f32[48,128]{1,0:T(8,128)S(1)}, f32[48,128]{1,0:T(8,128)S(1)}, u32[]{:S(2)}, u32[]{:S(2)}) collective-permute-start(f32[48,128]{1,0:T(8,128)S(1)} %shard_map.137.refs_0_), channel_id=1, source_target_pairs={{0,2},{1,3},{2,0},{3,1},{4,6},{5,7},{6,4},{7,5},{8,10},{9,11},{10,... | collective-permute-start | bytes 73736 | tf_op jit(solution)/shard_map/ppermute | solution.py:567
  47.3 1.4 %collective-permute-start.16 = (f32[48,128]{1,0:T(8,128)S(1)}, f32[48,128]{1,0:T(8,128)S(1)}, u32[]{:S(2)}, u32[]{:S(2)}) collective-permute-start(f32[48,128]{1,0:T(8,128)S(1)} %shard_map.137.refs_0_), channel_id=1, source_target_pairs={{0,3},{1,0},{2,1},{3,2},{4,7},{5,4},{6,5},{7,6},{8,11},{9,8},{10,9... | collective-permute-start | bytes 73736 | tf_op jit(solution)/shard_map/ppermute | solution.py:567
  48.7 0.4 collective-permute-done.14.refs_1_
  49.1 0.6 %collective-permute-done.15.refs_2_ = f32[48,128]{1,0:T(8,128)S(1)} collective-permute-done((f32[48,128]{1,0:T(8,128)S(1)}, f32[48,128]{1,0:T(8,128)S(1)}, u32[]{:S(2)}, u32[]{:S(2)}) %collective-permute-start.15) | collective-permute-done | bytes 24608 | tf_op jit(solution)/shard_map/ppermute | solution.py:567
  49.7 0.5 collective-permute-done.16.refs_3_
  50.2 0.0 collective-permute-done.17.refs_5_
  50.2 0.0 collective-permute-done.18.refs_6_
  50.2 0.0 copy-done.6
  50.2 2.0 %shard_map.138 = (f32[5,4,64,128]{3,2,1,0:T(8,128)}, f32[2,128]{1,0:T(2,128)S(1)}) custom-call(s32[2]{0:T(128)S(1)} %pad_add_fusion.place_ref, f32[48,128]{1,0:T(8,128)S(1)} %shard_map.137.refs_0_, f32[48,128]{1,0:T(8,128)S(1)} %collective-permute-done.14.refs_1_, f32[48,128]{1,0:T(8,128)S(1)} %collective-permute-done.15.refs_2_, ...), custom_call_target="tpu_custom_call" | custom-call | tf_op jit(solution)/shard_map/pallas_call | solution.py:107
  52.2 0.5 fusion.7
  (27 shorter events, 0.1 us)
Async XLA Ops:
  0.6 3.8 %copy-start.12 = (bf16[32,256]{1,0:T(8,128)(2,1)S(1)}, bf16[32,256]{1,0:T(8,128)(2,1)}, u32[]{:S(2)}) copy-start(bf16[32,256]{1,0:T(8,128)(2,1)} %constant.92.clone.table_ref) | copy-start | bytes 49156
  0.6 1.1 %copy-start = (f32[1,5,4,64,128]{4,3,2,1,0:T(8,128)S(1)}, f32[1,5,4,64,128]{4,3,2,1,0:T(8,128)}, u32[]{:S(2)}) copy-start(f32[1,5,4,64,128]{4,3,2,1,0:T(8,128)} %param.11) | copy-start | bytes 1966084
  1.7 2.7 %copy-start.2 = (f32[5,4,64,128]{3,2,1,0:T(8,128)S(1)}, f32[5,4,64,128]{3,2,1,0:T(8,128)}, u32[]{:S(2)}) copy-start(f32[5,4,64,128]{3,2,1,0:T(8,128)} %source_ref.7) | copy-start | bytes 1966084
  1.9 5.5 %collective-permute-start = (f32[5,64,128]{2,1,0:T(8,128)S(1)}, f32[5,64,128]{2,1,0:T(8,128)S(1)}, u32[]{:S(2)}, u32[]{:S(2)}) collective-permute-start(f32[5,64,128]{2,1,0:T(8,128)S(1)} %get-tuple-element.26), channel_id=1, source_target_pairs={{0,1},{1,2},{2,3},{3,0},{4,5},{5,6},{6,7},{7,4},{8,9},{9,10},{10,1... | collective-permute-start | bytes 491528 | tf_op jit(solution)/shard_map/ppermute | solution.py:448
  2.4 6.5 %collective-permute-start.1 = (f32[5,64,128]{2,1,0:T(8,128)S(1)}, f32[5,64,128]{2,1,0:T(8,128)S(1)}, u32[]{:S(2)}, u32[]{:S(2)}) collective-permute-start(f32[5,64,128]{2,1,0:T(8,128)S(1)} %get-tuple-element.27), channel_id=1, source_target_pairs={{1,0},{2,1},{3,2},{0,3},{5,4},{6,5},{7,6},{4,7},{9,8},{10,9},{11,1... | collective-permute-start | bytes 491528 | tf_op jit(solution)/shard_map/ppermute | solution.py:448
  8.9 4.9 %copy-start.1 = (f32[1,5,4,64,128]{4,3,2,1,0:T(8,128)S(1)}, f32[1,5,4,64,128]{4,3,2,1,0:T(8,128)}, u32[]{:S(2)}) copy-start(f32[1,5,4,64,128]{4,3,2,1,0:T(8,128)} %param.11) | copy-start | bytes 1966084
  9.7 0.7 %copy-start.7 = (f32[2,5,64,128]{3,2,1,0:T(8,128)}, f32[2,5,64,128]{3,2,1,0:T(8,128)S(1)}, u32[]{:S(2)}) copy-start(f32[2,5,64,128]{3,2,1,0:T(8,128)S(1)} %get-tuple-element.28.edge_ref) | copy-start | bytes 983044
  10.4 5.3 %collective-permute-start.2 = (f32[5,64,128]{2,1,0:T(8,128)}, f32[5,64,128]{2,1,0:T(8,128)S(1)}, u32[]{:S(2)}, u32[]{:S(2)}) collective-permute-start(f32[5,64,128]{2,1,0:T(8,128)} %get-tuple-element.30), channel_id=1, source_target_pairs={{0,1},{1,2},{2,3},{3,0},{4,5},{5,6},{6,7},{7,4},{8,9},{9,10},{10,1... | collective-permute-start | bytes 491528 | tf_op jit(solution)/shard_map/ppermute | solution.py:448
  11.3 5.9 %collective-permute-start.3 = (f32[5,64,128]{2,1,0:T(8,128)}, f32[5,64,128]{2,1,0:T(8,128)}, u32[]{:S(2)}, u32[]{:S(2)}) collective-permute-start(f32[5,64,128]{2,1,0:T(8,128)} %get-tuple-element.31), channel_id=1, source_target_pairs={{1,0},{2,1},{3,2},{0,3},{5,4},{6,5},{7,6},{4,7},{9,8},{10,9},{11,1... | collective-permute-start | bytes 491528 | tf_op jit(solution)/shard_map/ppermute | solution.py:448
  12.5 10.7 %collective-permute-start.6 = (f32[40,512]{1,0:T(8,128)}, f32[40,512]{1,0:T(8,128)S(1)}, u32[]{:S(2)}, u32[]{:S(2)}) collective-permute-start(f32[40,512]{1,0:T(8,128)} %get-tuple-element.38), channel_id=1, source_target_pairs={{4,0},{8,4},{12,8},{16,12},{20,16},{24,20},{28,24},{5,1},{9,5},{13... | collective-permute-start | bytes 245768 | tf_op jit(solution)/shard_map/ppermute | solution.py:494
  13.8 1.0 %copy-start.8 = (f32[2,5,64,128]{3,2,1,0:T(8,128)S(1)}, f32[2,5,64,128]{3,2,1,0:T(8,128)}, u32[]{:S(2)}) copy-start(f32[2,5,64,128]{3,2,1,0:T(8,128)} %copy-done.7) | copy-start | bytes 983044
  18.8 0.7 %copy-start.9 = (f32[2,5,64,128]{3,2,1,0:T(8,128)}, f32[2,5,64,128]{3,2,1,0:T(8,128)S(1)}, u32[]{:S(2)}) copy-start(f32[2,5,64,128]{3,2,1,0:T(8,128)S(1)} %get-tuple-element.32.edge_ref) | copy-start | bytes 983044
  19.6 5.1 %collective-permute-start.4 = (f32[5,64,128]{2,1,0:T(8,128)}, f32[5,64,128]{2,1,0:T(8,128)S(1)}, u32[]{:S(2)}, u32[]{:S(2)}) collective-permute-start(f32[5,64,128]{2,1,0:T(8,128)} %get-tuple-element.35), channel_id=1, source_target_pairs={{0,1},{1,2},{2,3},{3,0},{4,5},{5,6},{6,7},{7,4},{8,9},{9,10},{10,1... | collective-permute-start | bytes 491528 | tf_op jit(solution)/shard_map/ppermute | solution.py:448
  20.4 5.6 %collective-permute-start.5 = (f32[5,64,128]{2,1,0:T(8,128)}, f32[5,64,128]{2,1,0:T(8,128)}, u32[]{:S(2)}, u32[]{:S(2)}) collective-permute-start(f32[5,64,128]{2,1,0:T(8,128)} %get-tuple-element.36), channel_id=1, source_target_pairs={{1,0},{2,1},{3,2},{0,3},{5,4},{6,5},{7,6},{4,7},{9,8},{10,9},{11,1... | collective-permute-start | bytes 491528 | tf_op jit(solution)/shard_map/ppermute | solution.py:448
  21.6 1.0 %copy-start.10 = (f32[2,5,64,128]{3,2,1,0:T(8,128)S(1)}, f32[2,5,64,128]{3,2,1,0:T(8,128)}, u32[]{:S(2)}) copy-start(f32[2,5,64,128]{3,2,1,0:T(8,128)} %copy-done.9) | copy-start | bytes 983044
  22.5 3.4 %copy-start.3 = (bf16[768,512]{1,0:T(8,128)(2,1)S(1)}, bf16[768,512]{1,0:T(8,128)(2,1)}, u32[]{:S(2)}) copy-start(bf16[768,512]{1,0:T(8,128)(2,1)} %constant.93.clone.high_ref) | copy-start | bytes 2359300
  22.5 3.4 %copy-start.4 = (bf16[768,512]{1,0:T(8,128)(2,1)S(1)}, bf16[768,512]{1,0:T(8,128)(2,1)}, u32[]{:S(2)}) copy-start(bf16[768,512]{1,0:T(8,128)(2,1)} %constant.94.clone.low_ref) | copy-start | bytes 2359300
  22.5 3.4 %copy-start.11 = (f32[4,2,4,128]{3,2,1,0:T(4,128)S(1)}, f32[4,2,4,128]{3,2,1,0:T(4,128)}, u32[]{:S(2)}) copy-start(f32[4,2,4,128]{3,2,1,0:T(4,128)} %constant.95.clone.phase_ref.refs_10_) | copy-start | bytes 49156
  28.3 3.6 %collective-permute-start.7 = (f32[40,128]{1,0:T(8,128)S(1)}, f32[40,128]{1,0:T(8,128)S(1)}, u32[]{:S(2)}, u32[]{:S(2)}) collective-permute-start(f32[40,128]{1,0:T(8,128)S(1)} %get-tuple-element.49), channel_id=1, source_target_pairs={{0,1},{1,2},{2,3},{3,0},{4,5},{5,6},{6,7},{7,4},{8,9},{9,10},{10,1... | collective-permute-start | bytes 61448 | tf_op jit(solution)/shard_map/ppermute | solution.py:535
  29.2 3.8 %collective-permute-start.8 = (f32[40,128]{1,0:T(8,128)S(1)}, f32[40,128]{1,0:T(8,128)S(1)}, u32[]{:S(2)}, u32[]{:S(2)}) collective-permute-start(f32[40,128]{1,0:T(8,128)S(1)} %get-tuple-element.51), channel_id=1, source_target_pairs={{0,2},{1,3},{2,0},{3,1},{4,6},{5,7},{6,4},{7,5},{8,10},{9,11},{10,... | collective-permute-start | bytes 61448 | tf_op jit(solution)/shard_map/ppermute | solution.py:535
  30.7 2.6 %collective-permute-start.9 = (f32[40,128]{1,0:T(8,128)S(1)}, f32[40,128]{1,0:T(8,128)S(1)}, u32[]{:S(2)}, u32[]{:S(2)}) collective-permute-start(f32[40,128]{1,0:T(8,128)S(1)} %get-tuple-element.50), channel_id=1, source_target_pairs={{0,3},{1,0},{2,1},{3,2},{4,7},{5,4},{6,5},{7,6},{8,11},{9,8},{10,9... | collective-permute-start | bytes 61448 | tf_op jit(solution)/shard_map/ppermute | solution.py:535
  31.8 12.9 %copy-start.13 = (f32[4,2,8,128]{3,2,1,0:T(8,128)S(1)}, f32[4,2,8,128]{3,2,1,0:T(8,128)}, u32[]{:S(2)}) copy-start(f32[4,2,8,128]{3,2,1,0:T(8,128)} %constant.96.clone.symbol_ref) | copy-start | bytes 98308
  31.8 12.9 %copy-start.15 = (f32[8,128]{1,0:T(8,128)S(1)}, f32[8,128]{1,0:T(8,128)}, u32[]{:S(2)}) copy-start(f32[8,128]{1,0:T(8,128)} %constant.97.clone.share_ref) | copy-start | bytes 12292
  31.8 18.4 %copy-start.6 = (bf16[512,512]{1,0:T(8,128)(2,1)S(1)}, bf16[512,512]{1,0:T(8,128)(2,1)}, u32[]{:S(2)}) copy-start(bf16[512,512]{1,0:T(8,128)(2,1)} %constant.99.clone.refs_8_) | copy-start | bytes 1572868
  31.8 18.4 %copy-start.5 = (bf16[512,512]{1,0:T(8,128)(2,1)S(1)}, bf16[512,512]{1,0:T(8,128)(2,1)}, u32[]{:S(2)}) copy-start(bf16[512,512]{1,0:T(8,128)(2,1)} %constant.98.clone.refs_7_) | copy-start | bytes 1572868
  33.3 3.8 %collective-permute-start.10 = (f32[1,40,128]{2,1,0:T(8,128)S(1)}, f32[1,40,128]{2,1,0:T(8,128)S(1)}, u32[]{:S(2)}, u32[]{:S(2)}) collective-permute-start(f32[1,40,128]{2,1,0:T(8,128)S(1)} %bitcast.32), channel_id=1, source_target_pairs={{0,4},{4,0},{8,12},{12,8},{16,20},{20,16},{24,28},{28,24},{1,5},{5... | collective-permute-start | bytes 61448 | tf_op jit(solution)/shard_map/ppermute | solution.py:553
  34.3 15.8 %collective-permute-start.17 = (f32[5,64,128]{2,1,0:T(8,128)S(1)}, f32[5,64,128]{2,1,0:T(8,128)S(1)}, u32[]{:S(2)}, u32[]{:S(2)}) collective-permute-start(f32[5,64,128]{2,1,0:T(8,128)S(1)} %get-tuple-element.43), channel_id=1, source_target_pairs={{0,1},{1,2},{2,3},{3,0},{4,5},{5,6},{6,7},{7,4},{8,9},{9,10},{10,1... | collective-permute-start | bytes 491528 | tf_op jit(solution)/shard_map/ppermute | solution.py:448
  34.5 15.7 %collective-permute-start.18 = (f32[5,64,128]{2,1,0:T(8,128)S(1)}, f32[5,64,128]{2,1,0:T(8,128)S(1)}, u32[]{:S(2)}, u32[]{:S(2)}) collective-permute-start(f32[5,64,128]{2,1,0:T(8,128)S(1)} %get-tuple-element.44), channel_id=1, source_target_pairs={{1,0},{2,1},{3,2},{0,3},{5,4},{6,5},{7,6},{4,7},{9,8},{10,9},{11,1... | collective-permute-start | bytes 491528 | tf_op jit(solution)/shard_map/ppermute | solution.py:448
  37.1 6.0 %collective-permute-start.11 = (f32[2,40,128]{2,1,0:T(8,128)S(1)}, f32[2,40,128]{2,1,0:T(8,128)S(1)}, u32[]{:S(2)}, u32[]{:S(2)}) collective-permute-start(f32[2,40,128]{2,1,0:T(8,128)S(1)} %pad_maximum_fusion), channel_id=1, source_target_pairs={{0,8},{4,12},{8,16},{12,20},{16,24},{20,28},{24,0},{28,4},{1,9},{5... | collective-permute-start | bytes 122888 | tf_op jit(solution)/shard_map/ppermute | solution.py:553
  38.1 5.5 %collective-permute-start.12 = (f32[2,40,128]{2,1,0:T(8,128)S(1)}, f32[2,40,128]{2,1,0:T(8,128)S(1)}, u32[]{:S(2)}, u32[]{:S(2)}) collective-permute-start(f32[2,40,128]{2,1,0:T(8,128)S(1)} %pad_maximum_fusion), channel_id=1, source_target_pairs={{0,16},{4,20},{8,24},{12,28},{16,0},{20,4},{24,8},{28,12},{1,17},{... | collective-permute-start | bytes 122888 | tf_op jit(solution)/shard_map/ppermute | solution.py:553
  40.7 4.0 %collective-permute-start.13 = (f32[2,40,128]{2,1,0:T(8,128)S(1)}, f32[2,40,128]{2,1,0:T(8,128)S(1)}, u32[]{:S(2)}, u32[]{:S(2)}) collective-permute-start(f32[2,40,128]{2,1,0:T(8,128)S(1)} %pad_maximum_fusion), channel_id=1, source_target_pairs={{0,24},{4,28},{8,0},{12,4},{16,8},{20,12},{24,16},{28,20},{1,25},{... | collective-permute-start | bytes 122888 | tf_op jit(solution)/shard_map/ppermute | solution.py:553
  44.7 5.5 %copy-start.14 = (bf16[48,128]{1,0:T(8,128)(2,1)S(1)}, bf16[48,128]{1,0:T(8,128)(2,1)}, u32[]{:S(2)}) copy-start(bf16[48,128]{1,0:T(8,128)(2,1)} %constant.100.clone.refs_9_) | copy-start | bytes 36868
  45.8 3.3 %collective-permute-start.14 = (f32[48,128]{1,0:T(8,128)S(1)}, f32[48,128]{1,0:T(8,128)S(1)}, u32[]{:S(2)}, u32[]{:S(2)}) collective-permute-start(f32[48,128]{1,0:T(8,128)S(1)} %shard_map.137.refs_0_), channel_id=1, source_target_pairs={{0,1},{1,2},{2,3},{3,0},{4,5},{5,6},{6,7},{7,4},{8,9},{9,10},{10,1... | collective-permute-start | bytes 73736 | tf_op jit(solution)/shard_map/ppermute | solution.py:567
  45.8 3.9 %collective-permute-start.15 = (f32[48,128]{1,0:T(8,128)S(1)}, f32[48,128]{1,0:T(8,128)S(1)}, u32[]{:S(2)}, u32[]{:S(2)}) collective-permute-start(f32[48,128]{1,0:T(8,128)S(1)} %shard_map.137.refs_0_), channel_id=1, source_target_pairs={{0,2},{1,3},{2,0},{3,1},{4,6},{5,7},{6,4},{7,5},{8,10},{9,11},{10,... | collective-permute-start | bytes 73736 | tf_op jit(solution)/shard_map/ppermute | solution.py:567
  47.3 2.9 %collective-permute-start.16 = (f32[48,128]{1,0:T(8,128)S(1)}, f32[48,128]{1,0:T(8,128)S(1)}, u32[]{:S(2)}, u32[]{:S(2)}) collective-permute-start(f32[48,128]{1,0:T(8,128)S(1)} %shard_map.137.refs_0_), channel_id=1, source_target_pairs={{0,3},{1,0},{2,1},{3,2},{4,7},{5,4},{6,5},{7,6},{8,11},{9,8},{10,9... | collective-permute-start | bytes 73736 | tf_op jit(solution)/shard_map/ppermute | solution.py:567

commit v2 on v1

--- a/solution.py
+++ b/solution.py
@@ -1,5 +1,4 @@
 import functools
-import math
 
 import jax
 import jax.numpy as jnp
@@ -8,6 +7,7 @@
 from jax.experimental import pallas as pl
 from jax.experimental.pallas import tpu as pltpu
 from jax.sharding import PartitionSpec as P
+
 
 viscosity = 0.08
 diffusivity = 0.05
@@ -97,18 +97,22 @@
 
 
 on_chip = pl.BlockSpec(memory_space=pltpu.VMEM)
+off_chip = pl.BlockSpec(memory_space=pltpu.HBM)
 in_scalars = pl.BlockSpec(memory_space=pltpu.SMEM)
 
 
-def local_call(kernel, out_shape, operands, scratch=(), places=None):
+def local_call(kernel, out_shape, operands, scratch=(), places=None, out_specs=None):
     specs = [in_scalars if operand.dtype == jnp.int32 else on_chip for operand in operands]
     for index, spec in (places or {}).items():
         specs[index] = spec
+    if out_specs is None:
+        out_specs = jax.tree.map(lambda _: on_chip, out_shape)
+        out_shape = jax.tree.map(lambda out: pltpu.VMEM(out.shape, out.dtype), out_shape)
     return pl.pallas_call(
         kernel,
         out_shape=out_shape,
         in_specs=specs,
-        out_specs=jax.tree.map(lambda _: on_chip, out_shape),
+        out_specs=out_specs,
         scratch_shapes=list(scratch),
         compiler_params=pltpu.CompilerParams(vmem_limit_bytes=16 * 1024 * 1024),
     )(*operands)
@@ -164,7 +168,7 @@
 
 
 def level_rate(state, source):
-    u, v, w, p, s = state
+    u, v, _, p, _ = state
     rates = list(source)
     rows, cols = u.shape
     for axis, length, speed, velocity, lead in (
@@ -210,19 +214,16 @@
     return [reader(ref, layer) for layer in range(ref.shape[1])]
 
 
-def first_flux_kernel(state_ref, up_ref, down_ref, top_ref, bottom_ref, sems):
-    last = state_ref.shape[1] - 1
-    top = pltpu.make_async_copy(state_ref.at[:, last], top_ref, sems.at[0])
-    bottom = pltpu.make_async_copy(state_ref.at[:, 0], bottom_ref, sems.at[1])
-    top.start()
-    bottom.start()
-    fields = state_ref.shape[0]
-    top.wait()
-    for f, value in enumerate(flux([top_ref[f] for f in range(fields)], 1.0)):
-        up_ref[f] = value
-    bottom.wait()
-    for f, value in enumerate(flux([bottom_ref[f] for f in range(fields)], -1.0)):
-        down_ref[f] = value
+def first_flux_kernel(state_ref, *out_refs):
+    parts = len(out_refs) // 2
+    fields, slab, rows, _ = state_ref.shape
+    count = rows // parts
+    for part in range(parts):
+        span = pl.ds(part * count, count)
+        for side, (layer, sign) in enumerate(((slab - 1, 1.0), (0, -1.0))):
+            values = [state_ref[f, layer, span] for f in range(fields)]
+            for f, value in enumerate(flux(values, sign)):
+                out_refs[2 * part + side][f] = value
 
 
 def first_rate_kernel(state_ref, source_ref, table_ref, rate_ref, waves_ref):
@@ -241,35 +242,42 @@
     waves_ref[:, lanes:] = imag
 
 
-def edge_kernel(state_ref, rate_ref, below_ref, above_ref, edge_ref, up_ref, down_ref, *, step):
+def edge_kernel(
+    state_ref, rate_ref, below_ref, above_ref, edge_ref, up_ref, down_ref, *, step, part
+):
     fields, slab = state_ref.shape[:2]
     last = slab - 1
-    top = [
-        state_ref[f, last] + step * (rate_ref[f, last] + above_ref[f]) for f in range(fields)
-    ]
-    for f, value in enumerate(flux(top, 1.0)):
-        edge_ref[1, f] = top[f]
-        up_ref[f] = value
-    bottom = [state_ref[f, 0] + step * (rate_ref[f, 0] + below_ref[f]) for f in range(fields)]
-    for f, value in enumerate(flux(bottom, -1.0)):
-        edge_ref[0, f] = bottom[f]
-        down_ref[f] = value
-
-
-def fill_stage(state_ref, rate_ref, edge_ref, stage_ref, step):
+    count = below_ref.shape[1]
+    span = pl.ds(part * count, count)
+    for side, layer, came_ref, out_ref, sign in (
+        (1, last, above_ref, up_ref, 1.0),
+        (0, 0, below_ref, down_ref, -1.0),
+    ):
+        values = [
+            state_ref[f, layer, span] + step * (rate_ref[f, layer, span] + came_ref[f])
+            for f in range(fields)
+        ]
+        for f, value in enumerate(flux(values, sign)):
+            edge_ref[side, f] = values[f]
+            out_ref[f] = value
+
+
+def fill_stage(state_ref, rate_ref, edge_refs, stage_ref, step):
     fields, slab = state_ref.shape[:2]
     for f in range(fields):
-        stage_ref[f, 0] = edge_ref[0, f]
+        for part, edge_ref in enumerate(edge_refs):
+            count = edge_ref.shape[2]
+            span = pl.ds(part * count, count)
+            stage_ref[f, 0, span] = edge_ref[0, f]
+            stage_ref[f, slab - 1, span] = edge_ref[1, f]
         for layer in range(1, slab - 1):
             stage_ref[f, layer] = state_ref[f, layer] + step * rate_ref[f, layer]
-        stage_ref[f, slab - 1] = edge_ref[1, f]
-
-
-def rate_kernel(
-    state_ref, rate_ref, edge_ref, source_ref, sum_ref, next_ref, total_ref, stage_ref, *, step, share
-):
+
+
+def rate_kernel(state_ref, rate_ref, source_ref, sum_ref, *refs, step, share):
+    *edge_refs, next_ref, total_ref, stage_ref = refs
     fields = state_ref.shape[0]
-    fill_stage(state_ref, rate_ref, edge_ref, stage_ref, step)
+    fill_stage(state_ref, rate_ref, edge_refs, stage_ref, step)
 
     def put(layer, rates):
         for f in range(fields):
@@ -280,11 +288,8 @@
 
 
 def forward_kernel(
-    place_ref,
     state_ref,
     rate_ref,
-    below_ref,
-    above_ref,
     source_ref,
     sum_ref,
     shifted_ref,
@@ -292,21 +297,26 @@
     high_ref,
     low_ref,
     phase_ref,
-    out_ref,
-    inner_ref,
-    outer_ref,
-    edge_ref,
-    stage_ref,
-    *,
+    *refs,
     step,
     weight,
 ):
+    *came_refs, out_ref, inner_ref, outer_ref, edge_ref, stage_ref = refs
     fields, slab, rows, cols = state_ref.shape
     last = slab - 1
-    for f in range(fields):
-        edge_ref[0, f] = state_ref[f, 0] + step * (rate_ref[f, 0] + below_ref[f])
-        edge_ref[1, f] = state_ref[f, last] + step * (rate_ref[f, last] + above_ref[f])
-    fill_stage(state_ref, rate_ref, edge_ref, stage_ref, step)
+    parts = len(came_refs) // 2
+    count = rows // parts
+    for part in range(parts):
+        span = pl.ds(part * count, count)
+        below_ref, above_ref = came_refs[2 * part : 2 * part + 2]
+        for f in range(fields):
+            edge_ref[0, f, span] = state_ref[f, 0, span] + step * (
+                rate_ref[f, 0, span] + below_ref[f]
+            )
+            edge_ref[1, f, span] = state_ref[f, last, span] + step * (
+                rate_ref[f, last, span] + above_ref[f]
+            )
+    fill_stage(state_ref, rate_ref, [edge_ref], stage_ref, step)
 
     def put(layer, rates):
         for f in range(fields):
@@ -323,7 +333,7 @@
     width = out_ref.shape[0]
     keep = table_ref.shape[0] // 4
     half = out_ref.shape[2] // 2
-    place = place_ref[0]
+    place = lax.axis_index("space")
     table = table_ref[...]
     real, imag = by_field(
         along_x(inner_ref[...].reshape(fields * slab * rows, cols), table), fields, keep
@@ -347,30 +357,42 @@
         out_ref[lax.rem(group - place + width, width)] = turned
 
 
-def coarse_kernel(place_ref, slot_ref, jump_ref, symbol_ref, share_ref, out_ref, kept_ref):
+def slot_of(moment, moment_id, slices):
+    slot, stride = 0, 1
+    for radix in radices(slices):
+        ours = lax.rem(moment // stride, radix)
+        slot = slot + lax.rem(ours + (radix - moment_id // stride % radix), radix) * stride
+        stride *= radix
+    return slot
+
+
+def coarse_kernel(jump_ref, symbol_ref, share_ref, out_ref, kept_ref):
     slices, lines, lanes = jump_ref.shape
     keep = share_ref.shape[0]
     fields = lines // keep
-    place = place_ref[0]
-    moment = place_ref[1]
+    place = lax.axis_index("space")
+    moment = lax.axis_index("tm")
     real = symbol_ref[place, 0]
     imag = symbol_ref[place, 1]
     share = share_ref[...]
-    current = [jnp.zeros((keep, lanes), jnp.float32) for _ in range(fields)]
+    blank = jnp.zeros((keep, lanes), jnp.float32)
+    current = [(blank, blank)] * fields
     sizes = []
     kept_ref[0] = jnp.zeros((lines, lanes), jnp.float32)
     for moment_id in range(slices):
-        total = jnp.zeros((keep, lanes), jnp.float32)
-        for f in range(fields):
-            total = total + current[f] * current[f]
+        total = blank
+        for value, _ in current:
+            total = total + value * value
         sizes.append(jnp.sum(total * share, axis=0, keepdims=True))
         if moment_id == slices - 1:
             break
-        slot = slot_ref[moment_id]
+        slot = slot_of(moment, moment_id, slices)
         for f in range(fields):
-            value = jump_ref[slot, f * keep : (f + 1) * keep, :] + current[f]
-            current[f] = value * real + pltpu.roll(value, lanes // 2, 1) * imag
-            kept_ref[moment_id + 1, f * keep : (f + 1) * keep, :] = current[f]
+            jump = jump_ref[slot, f * keep : (f + 1) * keep, :]
+            value = jump + current[f][0]
+            swapped = pltpu.roll(jump, lanes // 2, 1) + current[f][1]
+            current[f] = (value * real + swapped * imag, swapped * real - value * imag)
+            kept_ref[moment_id + 1, f * keep : (f + 1) * keep, :] = current[f][0]
     out_ref[:lines, :] = kept_ref[moment]
     sums = jnp.sum(jnp.concatenate(sizes), axis=1, keepdims=True)
     spare = out_ref.shape[0] - lines - slices
@@ -379,12 +401,7 @@
     out_ref[lines : lines + slices, :] = jnp.broadcast_to(sums, (slices, lanes))
 
 
-def inverse_kernel(
-    place_ref,
-    *refs,
-    width,
-    scales,
-):
+def inverse_kernel(*refs, width, scales):
     block_refs = refs[:width]
     (
         fine_ref,
@@ -395,12 +412,17 @@
         table_ref,
         phase_ref,
         ends_ref,
-        norm_ref,
+        slice_ref,
+        total_ref,
         order_ref,
+        held_ref,
+        norm_refs,
+        sems,
+        norm_sems,
     ) = refs[width:]
     fields, slab, rows, cols = fine_ref.shape
-    place = place_ref[0]
-    moment = place_ref[1]
+    place = lax.axis_index("space")
+    moment = lax.axis_index("tm")
     lines, lanes = order_ref.shape[1:]
     keep = lines // fields
     sums = None
@@ -413,14 +435,10 @@
         )
         part = block_refs[step][lines:, :]
         sums = part if sums is None else sums + part
-    line = lax.broadcasted_iota(jnp.int32, sums.shape, 0)
-    own = jnp.sum(jnp.where(line == moment, sums, 0.0), axis=0, keepdims=True)
-    whole = jnp.sum(sums, axis=0, keepdims=True)
-    norm_ref[0:1, :] = jnp.sqrt(own * scales[0] + epsilon)
-    norm_ref[1:2, :] = jnp.sqrt(whole * scales[1] + epsilon)
     left = jnp.concatenate([order_ref[group] for group in range(width)], axis=1)
     waves = three_pass(left, high_ref[...], low_ref[...])
     count = slab * rows
+    copies = []
     for f in range(fields):
         both = jnp.concatenate(
             [waves[f * keep : (f + 1) * keep, :count], waves[f * keep : (f + 1) * keep, count:]]
@@ -438,7 +456,19 @@
                 value = value + below_ref[f]
             if layer == slab - 1:
                 value = value + above_ref[f]
-            ends_ref[f, layer] = value
+            held_ref[f, layer] = value
+        copies.append(pltpu.make_async_copy(held_ref.at[f], ends_ref.at[f], sems.at[f]))
+        copies[-1].start()
+    line = lax.broadcasted_iota(jnp.int32, sums.shape, 0)
+    own = jnp.sum(jnp.where(line == moment, sums, 0.0), axis=0, keepdims=True)
+    whole = jnp.sum(sums, axis=0, keepdims=True)
+    norm_refs[0, 0] = jnp.sqrt(own * scales[0] + epsilon)[0, 0]
+    norm_refs[1, 0] = jnp.sqrt(whole * scales[1] + epsilon)[0, 0]
+    for side, out_ref in enumerate((slice_ref, total_ref)):
+        copies.append(pltpu.make_async_copy(norm_refs.at[side], out_ref, norm_sems.at[side]))
+        copies[-1].start()
+    for copy in copies:
+        copy.wait()
 
 
 def halo(up, down):
@@ -467,25 +497,20 @@
     keep_y, keep_x = rows // 8, cols // 16
     lines, lanes = fields * keep_x, 2 * slab * 2 * keep_y
     tables = make_tables(slab, width, rows, cols)
-    place = lax.axis_index("space").astype(jnp.int32)
-    moment = lax.axis_index("tm").astype(jnp.int32)
-    where = jnp.stack([place, moment])
     real = jnp.float32
 
-    layer_shape = jax.ShapeDtypeStruct((fields, rows, cols), real)
-    edge_shape = jax.ShapeDtypeStruct((2, fields, rows, cols), real)
+    parts = 2 if rows % 16 == 0 else 1
+    layer_shape = jax.ShapeDtypeStruct((fields, rows // parts, cols), real)
+    edge_shape = jax.ShapeDtypeStruct((2, fields, rows // parts, cols), real)
     slab_shape = jax.ShapeDtypeStruct((fields, slab, rows, cols), real)
-    layer = pltpu.VMEM((fields, rows, cols), real)
     whole_slab = pltpu.VMEM((fields, slab, rows, cols), real)
 
-    up, down = local_call(
+    given = local_call(
         first_flux_kernel,
-        (layer_shape, layer_shape),
+        (layer_shape,) * (2 * parts),
         [state_now],
-        [layer, layer, pltpu.SemaphoreType.DMA((2,))],
-        {0: pl.BlockSpec(memory_space=pl.ANY)},
-    )
-    below, above = halo(up, down)
+    )
+    came = [halo(*given[2 * part : 2 * part + 2]) for part in range(parts)]
     rates, start_waves = local_call(
         first_rate_kernel,
         (slab_shape, jax.ShapeDtypeStruct((lines, 2 * slab * rows), real)),
@@ -495,17 +520,21 @@
     total = state_now
     for stage in range(2):
         step = 0.5 * time_step
-        edge, up, down = local_call(
-            functools.partial(edge_kernel, step=step),
-            (edge_shape, layer_shape, layer_shape),
-            [state_now, rates, below, above],
-        )
-        below, above = halo(up, down)
+        edges, arrived = [], came
+        came = []
+        for part in range(parts):
+            edge, up, down = local_call(
+                functools.partial(edge_kernel, step=step, part=part),
+                (edge_shape, layer_shape, layer_shape),
+                [state_now, rates, *arrived[part]],
+            )
+            edges.append(edge)
+            came.append(halo(up, down))
         share = ((-1.0 / 3.0, 1.0 / 3.0), (1.0, 2.0 / 3.0))[stage]
         rates, total = local_call(
             functools.partial(rate_kernel, step=step, share=share),
             (slab_shape, slab_shape),
-            [state_now, rates, edge, source, total],
+            [state_now, rates, source, total, *edges],
             [whole_slab],
         )
     waves, fine_inner, fine_outer = local_call(
@@ -513,36 +542,30 @@
         (
             jax.ShapeDtypeStruct((width, lines, lanes), real),
             slab_shape,
-            edge_shape,
+            jax.ShapeDtypeStruct((2, fields, rows, cols), real),
         ),
         [
-            where,
             state_now,
             rates,
-            below,
-            above,
             source,
             total,
             next_waves,
             tables["xforward"],
             *tables["yzforward"],
             tables["phase"],
+            *[array for pair in came for array in pair],
         ],
         [pltpu.VMEM((2, fields, rows, cols), real), whole_slab],
     )
     jump = waves[0]
     for step in range(1, width):
-        jump = jump + lax.ppermute(
-            waves[step], "space", [(i, (i + step) % width) for i in range(width)]
-        )
-
-    up, down, jump = lax.optimization_barrier((fine_outer[1], fine_outer[0], jump))
-    below, above = halo(up, down)
+        part = lax.ppermute(waves[step], "space", [(i, (i + step) % width) for i in range(width)])
+        jump = jump + part
+
+    below, above = halo(fine_outer[1], fine_outer[0])
 
     jumps = jump[None]
     stride = 1
-    slots = jnp.zeros((slices,), jnp.int32)
-    ids = jnp.arange(slices, dtype=jnp.int32)
     for radix in radices(slices):
         parts = [jumps]
         for step in range(1, radix):
@@ -552,13 +575,12 @@
                 pairs.append((i, i + ((digit + step) % radix - digit) * stride))
             parts.append(lax.ppermute(jumps, "tm", pairs))
         jumps = jnp.concatenate(parts)
-        slots = slots + (moment // stride - ids // stride) % radix * stride
         stride *= radix
 
     message = local_call(
         coarse_kernel,
         jax.ShapeDtypeStruct((lines + -(-slices // 8) * 8, lanes), real),
-        [where, slots, jumps, tables["symbol"], tables["share"]],
+        [jumps, tables["symbol"], tables["share"]],
         [pltpu.VMEM((slices, lines, lanes), real)],
     )
     blocks = [message]
@@ -567,16 +589,16 @@
             lax.ppermute(message, "space", [(i, (i + step) % width) for i in range(width)])
         )
     cells = fields * depth * rows * cols
-    ends, norms = local_call(
+    ends, slice_norm, total_norm = local_call(
         functools.partial(
             inverse_kernel, width=width, scales=(1.0 / cells, 1.0 / (cells * slices))
         ),
         (
             jax.ShapeDtypeStruct((fields, slab, rows, cols), real),
-            jax.ShapeDtypeStruct((2, lanes), real),
+            jax.ShapeDtypeStruct((1,), real),
+            jax.ShapeDtypeStruct((1,), real),
         ),
         [
-            where,
             *blocks,
             fine_inner,
             below,
@@ -585,9 +607,16 @@
             tables["xinverse"],
             tables["phase"],
         ],
-        [pltpu.VMEM((width, lines, lanes), real)],
-    )
-    return ends[None], norms[0, :1], norms[1, :1]
+        [
+            pltpu.VMEM((width, lines, lanes), real),
+            whole_slab,
+            pltpu.SMEM((2, 1), real),
+            pltpu.SemaphoreType.DMA((fields,)),
+            pltpu.SemaphoreType.DMA((2,)),
+        ],
+        out_specs=(off_chip, off_chip, off_chip),
+    )
+    return ends[None], slice_norm, total_norm
 
 
 def solution(mesh):

time: 53.3 us -> 49.1 us (0.921)
  starting transfers between devices: 21.9 us -> 28.3 us
  Pallas kernels: 10.6 us -> 5.09 us
  local copies, waits for them, and re-layouts: 5.09 us -> 1.18 us
  waiting for transfers between devices: 14.3 us -> 13.5 us
    ppermute x8 -> x14, waiting for transfers between devices: 7.72 us -> 2.07 us  [halo(): return (lax.ppermute(up, 'space', ups), lax.ppermute(down, 'space', downs))]
    pallas_call x9 -> x11, Pallas kernels: 10.6 us -> 5.09 us  [local_call(): pl.pallas_call(kernel, out_shape=out_shape, in_specs=specs, out_specs=out...]
    ppermute x8 -> x14, starting transfers between devices: 8.3 us -> 12.5 us  [halo(): return (lax.ppermute(up, 'space', ups), lax.ppermute(down, 'space', downs))]
    ppermute x4, starting transfers between devices: 5.95 us -> 9.47 us  [shards(): parts.append(lax.ppermute(jumps, 'tm', pairs))]
    unnamed x36 -> x25, local copies, waits for them, and re-layouts: 4.54 us -> 1.15 us
    ppermute x4, waiting for transfers between devices: 3.64 us -> 5.96 us  [shards(): parts.append(lax.ppermute(jumps, 'tm', pairs))]
    ppermute x3, waiting for transfers between devices: 1.52 us -> 3.08 us  [shards(): lax.ppermute(message, 'space', [(i, (i + step) % width) for i in range(wi...]
    ppermute x3, starting transfers between devices: 2.85 us -> 1.42 us  [shards(): lax.ppermute(message, 'space', [(i, (i + step) % width) for i in range(wi...]
  transfers between devices with their start and end apart: 19 -> 25, of which waited for: 15 -> 9; matrix products, arithmetic and copies ran while one was open for 0% -> 0% of each run, Pallas kernels for 10% -> 5%
where the time goes in v2:
time: 49.1 us; the launch traced here: 48.9 us
  starting transfers between devices  28.3 us (58%)
  waiting for transfers between devices  13.5 us (27%)
  Pallas kernels  5.09 us (10%)
  local copies, waits for them, and re-layouts  1.18 us (2%)
  between operations  0.87 us (2%)
    ppermute x14, starting transfers between devices, halo(): return (lax.ppermute(up, 'space', ups), lax.ppermute(down, 'space', downs))  12.5 us
    ppermute x4, starting transfers between devices, shards(): parts.append(lax.ppermute(jumps, 'tm', pairs))  9.47 us
    ppermute x4, waiting for transfers between devices, shards(): parts.append(lax.ppermute(jumps, 'tm', pairs))  5.96 us
    pallas_call x11, Pallas kernels, local_call(): pl.pallas_call(kernel, out_shape=out_shape, in_specs=specs, out_specs=out...  5.09 us
    ppermute x3, starting transfers between devices, shards(): lax.ppermute(waves[step], 'space', [(i, (i + step) % width) for i in rang...  3.56 us
    ppermute x3, waiting for transfers between devices, shards(): lax.ppermute(message, 'space', [(i, (i + step) % width) for i in range(wi...  3.08 us
    ppermute x14, waiting for transfers between devices, halo(): return (lax.ppermute(up, 'space', ups), lax.ppermute(down, 'space', downs))  2.07 us
    ppermute x3, waiting for transfers between devices, shards(): lax.ppermute(waves[step], 'space', [(i, (i + step) % width) for i in rang...  2.01 us
  transfers between devices with their start and end apart: 25, of which 9 were waited for; matrix products, arithmetic and copies ran while one was open for 0% of the time, Pallas kernels for 5%

profile of v2, /device:TPU:0, one launch (start us, length us, event | category | flops | bytes accessed | tf_op | source)
XLA Modules:
  0.0 48.9 jit_solution(14427081556675285290)
XLA Ops:
  0.6 0.0 copy-start.7
  0.6 0.0 copy-start
  0.7 1.1 %copy-done = f32[1,5,4,64,128]{4,3,2,1,0:T(8,128)S(1)} copy-done((f32[1,5,4,64,128]{4,3,2,1,0:T(8,128)S(1)}, f32[1,5,4,64,128]{4,3,2,1,0:T(8,128)}, u32[]{:S(2)}) %copy-start) | copy-done | bytes 655384
  1.8 0.5 %collective-permute-start.2 = (f32[5,32,128]{2,1,0:T(8,128)S(1)}, f32[5,32,128]{2,1,0:T(8,128)S(1)}, u32[]{:S(2)}, u32[]{:S(2)}) collective-permute-start(f32[5,32,128]{2,1,0:T(8,128)S(1)} %get-tuple-element.35), channel_id=1, source_target_pairs={{0,1},{1,2},{2,3},{3,0},{4,5},{5,6},{6,7},{7,4},{8,9},{9,10},{10,1... | collective-permute-start | bytes 245768 | tf_op jit(solution)/shard_map/ppermute | solution.py:478
  2.3 2.0 %collective-permute-start.3 = (f32[5,32,128]{2,1,0:T(8,128)S(1)}, f32[5,32,128]{2,1,0:T(8,128)S(1)}, u32[]{:S(2)}, u32[]{:S(2)}) collective-permute-start(f32[5,32,128]{2,1,0:T(8,128)S(1)} %get-tuple-element.36), channel_id=1, source_target_pairs={{1,0},{2,1},{3,2},{0,3},{5,4},{6,5},{7,6},{4,7},{9,8},{10,9},{11,1... | collective-permute-start | bytes 245768 | tf_op jit(solution)/shard_map/ppermute | solution.py:478
  4.3 0.6 %collective-permute-start = (f32[5,32,128]{2,1,0:T(8,128)S(1)}, f32[5,32,128]{2,1,0:T(8,128)S(1)}, u32[]{:S(2)}, u32[]{:S(2)}) collective-permute-start(f32[5,32,128]{2,1,0:T(8,128)S(1)} %get-tuple-element.32), channel_id=1, source_target_pairs={{0,1},{1,2},{2,3},{3,0},{4,5},{5,6},{6,7},{7,4},{8,9},{9,10},{10,1... | collective-permute-start | bytes 245768 | tf_op jit(solution)/shard_map/ppermute | solution.py:478
  4.9 1.1 %collective-permute-start.1 = (f32[5,32,128]{2,1,0:T(8,128)S(1)}, f32[5,32,128]{2,1,0:T(8,128)S(1)}, u32[]{:S(2)}, u32[]{:S(2)}) collective-permute-start(f32[5,32,128]{2,1,0:T(8,128)S(1)} %get-tuple-element.33), channel_id=1, source_target_pairs={{1,0},{2,1},{3,2},{0,3},{5,4},{6,5},{7,6},{4,7},{9,8},{10,9},{11,1... | collective-permute-start | bytes 245768 | tf_op jit(solution)/shard_map/ppermute | solution.py:478
  6.0 0.0 copy-done.7
  6.0 0.0 copy-done.1
  6.0 0.6 %shard_map.130 = (f32[5,4,64,128]{3,2,1,0:T(8,128)S(1)}, f32[40,512]{1,0:T(8,128)S(1)}) custom-call(f32[5,4,64,128]{3,2,1,0:T(8,128)S(1)} %bitcast.25, f32[5,4,64,128]{3,2,1,0:T(8,128)S(1)} %copy-done.1, bf16[32,256]{1,0:T(8,128)(2,1)S(1)} %copy-done.7), custom_call_target="tpu_custom_call" | custom-call | tf_op jit(solution)/shard_map/pallas_call | solution.py:111
  6.7 0.0 collective-permute-done.2.below_ref
  6.7 0.4 collective-permute-done.3.above_ref
  7.1 1.9 %collective-permute-start.6 = (f32[5,32,128]{2,1,0:T(8,128)S(1)}, f32[5,32,128]{2,1,0:T(8,128)S(1)}, u32[]{:S(2)}, u32[]{:S(2)}) collective-permute-start(f32[5,32,128]{2,1,0:T(8,128)S(1)} %get-tuple-element.43), channel_id=1, source_target_pairs={{0,1},{1,2},{2,3},{3,0},{4,5},{5,6},{6,7},{7,4},{8,9},{9,10},{10,1... | collective-permute-start | bytes 245768 | tf_op jit(solution)/shard_map/ppermute | solution.py:478
  8.9 0.5 collective-permute-start.7
  9.4 0.0 collective-permute-done.below_ref
  9.4 0.0 collective-permute-done.1.above_ref
  9.5 1.5 %collective-permute-start.4 = (f32[5,32,128]{2,1,0:T(8,128)S(1)}, f32[5,32,128]{2,1,0:T(8,128)S(1)}, u32[]{:S(2)}, u32[]{:S(2)}) collective-permute-start(f32[5,32,128]{2,1,0:T(8,128)S(1)} %get-tuple-element.40), channel_id=1, source_target_pairs={{0,1},{1,2},{2,3},{3,0},{4,5},{5,6},{6,7},{7,4},{8,9},{9,10},{10,1... | collective-permute-start | bytes 245768 | tf_op jit(solution)/shard_map/ppermute | solution.py:478
  11.0 0.3 collective-permute-start.5
  11.3 1.3 %collective-permute-start.8 = (f32[40,512]{1,0:T(8,128)S(1)}, f32[40,512]{1,0:T(8,128)S(1)}, u32[]{:S(2)}, u32[]{:S(2)}) collective-permute-start(f32[40,512]{1,0:T(8,128)S(1)} %get-tuple-element.48), channel_id=1, source_target_pairs={{4,0},{8,4},{12,8},{16,12},{20,16},{24,20},{28,24},{5,1},{9,5},{13... | collective-permute-start | bytes 245768 | tf_op jit(solution)/shard_map/ppermute | solution.py:519
  12.5 0.6 %shard_map.134 = (f32[5,4,64,128]{3,2,1,0:T(8,128)S(1)}, f32[5,4,64,128]{3,2,1,0:T(8,128)S(1)}) custom-call(f32[5,4,64,128]{3,2,1,0:T(8,128)S(1)} %bitcast.28, f32[5,4,64,128]{3,2,1,0:T(8,128)S(1)} %get-tuple-element.31.rate_ref, f32[5,4,64,128]{3,2,1,0:T(8,128)S(1)} %copy-done.1, f32[5,4,64,128]{3,2,1,0:T(8,128)S(1)} %bitcast.29, ...), custom_call_target="tpu_custom_call" | custom-call | tf_op jit(solution)/shard_map/pallas_call | solution.py:111
  13.2 0.0 collective-permute-done.6.below_ref
  13.2 0.0 collective-permute-done.7.above_ref
  13.3 0.9 %collective-permute-start.11 = (f32[5,32,128]{2,1,0:T(8,128)S(1)}, f32[5,32,128]{2,1,0:T(8,128)S(1)}, u32[]{:S(2)}, u32[]{:S(2)}) collective-permute-start(f32[5,32,128]{2,1,0:T(8,128)S(1)} %get-tuple-element.51), channel_id=1, source_target_pairs={{0,1},{1,2},{2,3},{3,0},{4,5},{5,6},{6,7},{7,4},{8,9},{9,10},{10,1... | collective-permute-start | bytes 245768 | tf_op jit(solution)/shard_map/ppermute | solution.py:478
  14.2 0.9 %collective-permute-start.12 = (f32[5,32,128]{2,1,0:T(8,128)S(1)}, f32[5,32,128]{2,1,0:T(8,128)S(1)}, u32[]{:S(2)}, u32[]{:S(2)}) collective-permute-start(f32[5,32,128]{2,1,0:T(8,128)S(1)} %get-tuple-element.52), channel_id=1, source_target_pairs={{1,0},{2,1},{3,2},{0,3},{5,4},{6,5},{7,6},{4,7},{9,8},{10,9},{11,1... | collective-permute-start | bytes 245768 | tf_op jit(solution)/shard_map/ppermute | solution.py:478
  15.1 0.0 collective-permute-done.4.below_ref
  15.1 0.0 collective-permute-done.5.above_ref
  15.1 0.4 collective-permute-start.9
  15.5 1.4 %collective-permute-start.10 = (f32[5,32,128]{2,1,0:T(8,128)S(1)}, f32[5,32,128]{2,1,0:T(8,128)S(1)}, u32[]{:S(2)}, u32[]{:S(2)}) collective-permute-start(f32[5,32,128]{2,1,0:T(8,128)S(1)} %get-tuple-element.50), channel_id=1, source_target_pairs={{1,0},{2,1},{3,2},{0,3},{5,4},{6,5},{7,6},{4,7},{9,8},{10,9},{11,1... | collective-permute-start | bytes 245768 | tf_op jit(solution)/shard_map/ppermute | solution.py:478
  16.9 0.6 %shard_map.137 = (f32[5,4,64,128]{3,2,1,0:T(8,128)S(1)}, f32[5,4,64,128]{3,2,1,0:T(8,128)S(1)}) custom-call(f32[5,4,64,128]{3,2,1,0:T(8,128)S(1)} %bitcast.32, f32[5,4,64,128]{3,2,1,0:T(8,128)S(1)} %get-tuple-element.38.rate_ref, f32[5,4,64,128]{3,2,1,0:T(8,128)S(1)} %copy-done.1, f32[5,4,64,128]{3,2,1,0:T(8,128)S(1)} %get-tuple-element.39.sum_ref, ...), custom_call_target="tpu_custom_call" | custom-call | tf_op jit(solution)/shard_map/pallas_call | solution.py:111
  17.5 0.3 collective-permute-done.8.shifted_ref
  17.9 0.0 collective-permute-done.11.refs_2_
  17.9 0.0 collective-permute-done.12.refs_3_
  17.9 1.7 %collective-permute-done.9.refs_0_ = f32[5,32,128]{2,1,0:T(8,128)S(1)} collective-permute-done((f32[5,32,128]{2,1,0:T(8,128)S(1)}, f32[5,32,128]{2,1,0:T(8,128)S(1)}, u32[]{:S(2)}, u32[]{:S(2)}) %collective-permute-start.9) | collective-permute-done | bytes 81952 | tf_op jit(solution)/shard_map/ppermute | solution.py:478
  19.6 0.0 collective-permute-done.10.refs_1_
  19.6 0.0 copy-done.6
  19.6 1.4 %shard_map.138 = (f32[4,40,128]{2,1,0:T(8,128)S(1)}, f32[5,4,64,128]{3,2,1,0:T(8,128)S(1)}, f32[2,5,64,128]{3,2,1,0:T(8,128)S(1)}) custom-call(f32[5,4,64,128]{3,2,1,0:T(8,128)S(1)} %bitcast.33, f32[5,4,64,128]{3,2,1,0:T(8,128)S(1)} %get-tuple-element.46.rate_ref, f32[5,4,64,128]{3,2,1,0:T(8,128)S(1)} %copy-done.1, ...), custom_call_target="tpu_custom_call" | custom-call | tf_op jit(solution)/shard_map/pallas_call | solution.py:111
  21.0 0.0 copy-start.10
  21.0 1.5 %collective-permute-start.13 = (f32[40,128]{1,0:T(8,128)S(1)}, f32[40,128]{1,0:T(8,128)S(1)}, u32[]{:S(2)}, u32[]{:S(2)}) collective-permute-start(f32[40,128]{1,0:T(8,128)S(1)} %get-tuple-element.63), channel_id=1, source_target_pairs={{0,1},{1,2},{2,3},{3,0},{4,5},{5,6},{6,7},{7,4},{8,9},{9,10},{10,1... | collective-permute-start | bytes 61448 | tf_op jit(solution)/shard_map/ppermute | solution.py:562
  22.5 0.3 collective-permute-start.15
  22.8 1.8 %collective-permute-start.14 = (f32[40,128]{1,0:T(8,128)S(1)}, f32[40,128]{1,0:T(8,128)S(1)}, u32[]{:S(2)}, u32[]{:S(2)}) collective-permute-start(f32[40,128]{1,0:T(8,128)S(1)} %get-tuple-element.65), channel_id=1, source_target_pairs={{0,2},{1,3},{2,0},{3,1},{4,6},{5,7},{6,4},{7,5},{8,10},{9,11},{10,... | collective-permute-start | bytes 61448 | tf_op jit(solution)/shard_map/ppermute | solution.py:562
  24.5 0.0 collective-permute-done.13
  24.6 0.0 collective-permute-done.15
  24.6 2.0 %collective-permute-done.14 = f32[40,128]{1,0:T(8,128)S(1)} collective-permute-done((f32[40,128]{1,0:T(8,128)S(1)}, f32[40,128]{1,0:T(8,128)S(1)}, u32[]{:S(2)}, u32[]{:S(2)}) %collective-permute-start.14) | collective-permute-done | bytes 20512 | tf_op jit(solution)/shard_map/ppermute | solution.py:562
  26.6 2.8 %collective-permute-start.16 = (f32[1,40,128]{2,1,0:T(8,128)S(1)}, f32[1,40,128]{2,1,0:T(8,128)S(1)}, u32[]{:S(2)}, u32[]{:S(2)}) collective-permute-start(f32[1,40,128]{2,1,0:T(8,128)S(1)} %get-tuple-element.60), channel_id=1, source_target_pairs={{0,4},{4,0},{8,12},{12,8},{16,20},{20,16},{24,28},{28,24},{1,5},{5... | collective-permute-start | bytes 61448 | tf_op jit(solution)/shard_map/ppermute | solution.py:576
  29.4 0.1 collective-permute-start.24
  29.5 0.5 %collective-permute-start.23 = (f32[5,64,128]{2,1,0:T(8,128)S(1)}, f32[5,64,128]{2,1,0:T(8,128)S(1)}, u32[]{:S(2)}, u32[]{:S(2)}) collective-permute-start(f32[5,64,128]{2,1,0:T(8,128)S(1)} %get-tuple-element.62), channel_id=1, source_target_pairs={{0,1},{1,2},{2,3},{3,0},{4,5},{5,6},{6,7},{7,4},{8,9},{9,10},{10,1... | collective-permute-start | bytes 491528 | tf_op jit(solution)/shard_map/ppermute | solution.py:478
  30.0 1.2 %collective-permute-done.16 = f32[1,40,128]{2,1,0:T(8,128)S(1)} collective-permute-done((f32[1,40,128]{2,1,0:T(8,128)S(1)}, f32[1,40,128]{2,1,0:T(8,128)S(1)}, u32[]{:S(2)}, u32[]{:S(2)}) %collective-permute-start.16) | collective-permute-done | bytes 20512 | tf_op jit(solution)/shard_map/ppermute | solution.py:576
  31.2 5.6 %collective-permute-start.19 = (f32[2,40,128]{2,1,0:T(8,128)S(1)}, f32[2,40,128]{2,1,0:T(8,128)S(1)}, u32[]{:S(2)}, u32[]{:S(2)}) collective-permute-start(f32[2,40,128]{2,1,0:T(8,128)S(1)} %pad_maximum_fusion), channel_id=1, source_target_pairs={{0,24},{4,28},{8,0},{12,4},{16,8},{20,12},{24,16},{28,20},{1,25},{... | collective-permute-start | bytes 122888 | tf_op jit(solution)/shard_map/ppermute | solution.py:576
  36.8 0.0 collective-permute-start.18
  36.8 1.0 %collective-permute-start.17 = (f32[2,40,128]{2,1,0:T(8,128)S(1)}, f32[2,40,128]{2,1,0:T(8,128)S(1)}, u32[]{:S(2)}, u32[]{:S(2)}) collective-permute-start(f32[2,40,128]{2,1,0:T(8,128)S(1)} %pad_maximum_fusion), channel_id=1, source_target_pairs={{0,8},{4,12},{8,16},{12,20},{16,24},{20,28},{24,0},{28,4},{1,9},{5... | collective-permute-start | bytes 122888 | tf_op jit(solution)/shard_map/ppermute | solution.py:576
  37.8 4.8 %collective-permute-done.17 = f32[2,40,128]{2,1,0:T(8,128)S(1)} collective-permute-done((f32[2,40,128]{2,1,0:T(8,128)S(1)}, f32[2,40,128]{2,1,0:T(8,128)S(1)}, u32[]{:S(2)}, u32[]{:S(2)}) %collective-permute-start.17) | collective-permute-done | bytes 40992 | tf_op jit(solution)/shard_map/ppermute | solution.py:576
  42.6 0.0 collective-permute-done.18
  42.6 0.0 collective-permute-done.19
  42.7 0.0 copy-start.9
  42.7 0.2 shard_map.139.refs_0_
  42.9 0.0 collective-permute-start.22
  42.9 1.2 %collective-permute-start.21 = (f32[48,128]{1,0:T(8,128)S(1)}, f32[48,128]{1,0:T(8,128)S(1)}, u32[]{:S(2)}, u32[]{:S(2)}) collective-permute-start(f32[48,128]{1,0:T(8,128)S(1)} %shard_map.139.refs_0_), channel_id=1, source_target_pairs={{0,2},{1,3},{2,0},{3,1},{4,6},{5,7},{6,4},{7,5},{8,10},{9,11},{10,... | collective-permute-start | bytes 73736 | tf_op jit(solution)/shard_map/ppermute | solution.py:589
  44.2 0.2 collective-permute-start.20
  44.3 0.1 collective-permute-done.22.refs_3_
  44.4 2.4 %collective-permute-done.21.refs_2_ = f32[48,128]{1,0:T(8,128)S(1)} collective-permute-done((f32[48,128]{1,0:T(8,128)S(1)}, f32[48,128]{1,0:T(8,128)S(1)}, u32[]{:S(2)}, u32[]{:S(2)}) %collective-permute-start.21) | collective-permute-done | bytes 24608 | tf_op jit(solution)/shard_map/ppermute | solution.py:589
  46.8 0.6 %collective-permute-done.20.refs_1_ = f32[48,128]{1,0:T(8,128)S(1)} collective-permute-done((f32[48,128]{1,0:T(8,128)S(1)}, f32[48,128]{1,0:T(8,128)S(1)}, u32[]{:S(2)}, u32[]{:S(2)}) %collective-permute-start.20) | collective-permute-done | bytes 24608 | tf_op jit(solution)/shard_map/ppermute | solution.py:589
  47.4 0.0 collective-permute-done.24.refs_6_
  47.4 0.0 collective-permute-done.23.refs_5_
  47.4 1.5 %shard_map.140 = (f32[5,4,64,128]{3,2,1,0:T(8,128)}, f32[1]{0:T(128)}, f32[1]{0:T(128)}) custom-call(f32[48,128]{1,0:T(8,128)S(1)} %shard_map.139.refs_0_, f32[48,128]{1,0:T(8,128)S(1)} %collective-permute-done.20.refs_1_, f32[48,128]{1,0:T(8,128)S(1)} %collective-permute-done.21.refs_2_, f32[48,128]{1,0:T(8,128)S(1)} %collective-permute-done.22.refs_3_, ...), custom_call_target="tpu_custom_call" | custom-call | tf_op jit(solution)/shard_map/pallas_call | solution.py:111
  (27 shorter events, 0.3 us)
Async XLA Ops:
  0.6 5.4 %copy-start.7 = (bf16[32,256]{1,0:T(8,128)(2,1)S(1)}, bf16[32,256]{1,0:T(8,128)(2,1)}, u32[]{:S(2)}) copy-start(bf16[32,256]{1,0:T(8,128)(2,1)} %constant.18.clone.table_ref) | copy-start | bytes 49156
  0.6 1.1 %copy-start = (f32[1,5,4,64,128]{4,3,2,1,0:T(8,128)S(1)}, f32[1,5,4,64,128]{4,3,2,1,0:T(8,128)}, u32[]{:S(2)}) copy-start(f32[1,5,4,64,128]{4,3,2,1,0:T(8,128)} %param.11) | copy-start | bytes 1966084
  1.7 4.3 %copy-start.1 = (f32[5,4,64,128]{3,2,1,0:T(8,128)S(1)}, f32[5,4,64,128]{3,2,1,0:T(8,128)}, u32[]{:S(2)}) copy-start(f32[5,4,64,128]{3,2,1,0:T(8,128)} %source_ref.7) | copy-start | bytes 1966084
  1.8 4.9 %collective-permute-start.2 = (f32[5,32,128]{2,1,0:T(8,128)S(1)}, f32[5,32,128]{2,1,0:T(8,128)S(1)}, u32[]{:S(2)}, u32[]{:S(2)}) collective-permute-start(f32[5,32,128]{2,1,0:T(8,128)S(1)} %get-tuple-element.35), channel_id=1, source_target_pairs={{0,1},{1,2},{2,3},{3,0},{4,5},{5,6},{6,7},{7,4},{8,9},{9,10},{10,1... | collective-permute-start | bytes 245768 | tf_op jit(solution)/shard_map/ppermute | solution.py:478
  2.3 4.7 %collective-permute-start.3 = (f32[5,32,128]{2,1,0:T(8,128)S(1)}, f32[5,32,128]{2,1,0:T(8,128)S(1)}, u32[]{:S(2)}, u32[]{:S(2)}) collective-permute-start(f32[5,32,128]{2,1,0:T(8,128)S(1)} %get-tuple-element.36), channel_id=1, source_target_pairs={{1,0},{2,1},{3,2},{0,3},{5,4},{6,5},{7,6},{4,7},{9,8},{10,9},{11,1... | collective-permute-start | bytes 245768 | tf_op jit(solution)/shard_map/ppermute | solution.py:478
  4.3 5.1 %collective-permute-start = (f32[5,32,128]{2,1,0:T(8,128)S(1)}, f32[5,32,128]{2,1,0:T(8,128)S(1)}, u32[]{:S(2)}, u32[]{:S(2)}) collective-permute-start(f32[5,32,128]{2,1,0:T(8,128)S(1)} %get-tuple-element.32), channel_id=1, source_target_pairs={{0,1},{1,2},{2,3},{3,0},{4,5},{5,6},{6,7},{7,4},{8,9},{9,10},{10,1... | collective-permute-start | bytes 245768 | tf_op jit(solution)/shard_map/ppermute | solution.py:478
  4.9 4.5 %collective-permute-start.1 = (f32[5,32,128]{2,1,0:T(8,128)S(1)}, f32[5,32,128]{2,1,0:T(8,128)S(1)}, u32[]{:S(2)}, u32[]{:S(2)}) collective-permute-start(f32[5,32,128]{2,1,0:T(8,128)S(1)} %get-tuple-element.33), channel_id=1, source_target_pairs={{1,0},{2,1},{3,2},{0,3},{5,4},{6,5},{7,6},{4,7},{9,8},{10,9},{11,1... | collective-permute-start | bytes 245768 | tf_op jit(solution)/shard_map/ppermute | solution.py:478
  7.1 6.1 %collective-permute-start.6 = (f32[5,32,128]{2,1,0:T(8,128)S(1)}, f32[5,32,128]{2,1,0:T(8,128)S(1)}, u32[]{:S(2)}, u32[]{:S(2)}) collective-permute-start(f32[5,32,128]{2,1,0:T(8,128)S(1)} %get-tuple-element.43), channel_id=1, source_target_pairs={{0,1},{1,2},{2,3},{3,0},{4,5},{5,6},{6,7},{7,4},{8,9},{9,10},{10,1... | collective-permute-start | bytes 245768 | tf_op jit(solution)/shard_map/ppermute | solution.py:478
  8.9 4.3 %collective-permute-start.7 = (f32[5,32,128]{2,1,0:T(8,128)S(1)}, f32[5,32,128]{2,1,0:T(8,128)S(1)}, u32[]{:S(2)}, u32[]{:S(2)}) collective-permute-start(f32[5,32,128]{2,1,0:T(8,128)S(1)} %get-tuple-element.44), channel_id=1, source_target_pairs={{1,0},{2,1},{3,2},{0,3},{5,4},{6,5},{7,6},{4,7},{9,8},{10,9},{11,1... | collective-permute-start | bytes 245768 | tf_op jit(solution)/shard_map/ppermute | solution.py:478
  9.5 5.6 %collective-permute-start.4 = (f32[5,32,128]{2,1,0:T(8,128)S(1)}, f32[5,32,128]{2,1,0:T(8,128)S(1)}, u32[]{:S(2)}, u32[]{:S(2)}) collective-permute-start(f32[5,32,128]{2,1,0:T(8,128)S(1)} %get-tuple-element.40), channel_id=1, source_target_pairs={{0,1},{1,2},{2,3},{3,0},{4,5},{5,6},{6,7},{7,4},{8,9},{9,10},{10,1... | collective-permute-start | bytes 245768 | tf_op jit(solution)/shard_map/ppermute | solution.py:478
  11.0 4.1 %collective-permute-start.5 = (f32[5,32,128]{2,1,0:T(8,128)S(1)}, f32[5,32,128]{2,1,0:T(8,128)S(1)}, u32[]{:S(2)}, u32[]{:S(2)}) collective-permute-start(f32[5,32,128]{2,1,0:T(8,128)S(1)} %get-tuple-element.41), channel_id=1, source_target_pairs={{1,0},{2,1},{3,2},{0,3},{5,4},{6,5},{7,6},{4,7},{9,8},{10,9},{11,1... | collective-permute-start | bytes 245768 | tf_op jit(solution)/shard_map/ppermute | solution.py:478
  11.3 6.6 %collective-permute-start.8 = (f32[40,512]{1,0:T(8,128)S(1)}, f32[40,512]{1,0:T(8,128)S(1)}, u32[]{:S(2)}, u32[]{:S(2)}) collective-permute-start(f32[40,512]{1,0:T(8,128)S(1)} %get-tuple-element.48), channel_id=1, source_target_pairs={{4,0},{8,4},{12,8},{16,12},{20,16},{24,20},{28,24},{5,1},{9,5},{13... | collective-permute-start | bytes 245768 | tf_op jit(solution)/shard_map/ppermute | solution.py:519
  13.3 4.6 %collective-permute-start.11 = (f32[5,32,128]{2,1,0:T(8,128)S(1)}, f32[5,32,128]{2,1,0:T(8,128)S(1)}, u32[]{:S(2)}, u32[]{:S(2)}) collective-permute-start(f32[5,32,128]{2,1,0:T(8,128)S(1)} %get-tuple-element.51), channel_id=1, source_target_pairs={{0,1},{1,2},{2,3},{3,0},{4,5},{5,6},{6,7},{7,4},{8,9},{9,10},{10,1... | collective-permute-start | bytes 245768 | tf_op jit(solution)/shard_map/ppermute | solution.py:478
  14.2 3.7 %collective-permute-start.12 = (f32[5,32,128]{2,1,0:T(8,128)S(1)}, f32[5,32,128]{2,1,0:T(8,128)S(1)}, u32[]{:S(2)}, u32[]{:S(2)}) collective-permute-start(f32[5,32,128]{2,1,0:T(8,128)S(1)} %get-tuple-element.52), channel_id=1, source_target_pairs={{1,0},{2,1},{3,2},{0,3},{5,4},{6,5},{7,6},{4,7},{9,8},{10,9},{11,1... | collective-permute-start | bytes 245768 | tf_op jit(solution)/shard_map/ppermute | solution.py:478
  15.1 4.5 %collective-permute-start.9 = (f32[5,32,128]{2,1,0:T(8,128)S(1)}, f32[5,32,128]{2,1,0:T(8,128)S(1)}, u32[]{:S(2)}, u32[]{:S(2)}) collective-permute-start(f32[5,32,128]{2,1,0:T(8,128)S(1)} %get-tuple-element.49), channel_id=1, source_target_pairs={{0,1},{1,2},{2,3},{3,0},{4,5},{5,6},{6,7},{7,4},{8,9},{9,10},{10,1... | collective-permute-start | bytes 245768 | tf_op jit(solution)/shard_map/ppermute | solution.py:478
  15.5 4.1 %collective-permute-start.10 = (f32[5,32,128]{2,1,0:T(8,128)S(1)}, f32[5,32,128]{2,1,0:T(8,128)S(1)}, u32[]{:S(2)}, u32[]{:S(2)}) collective-permute-start(f32[5,32,128]{2,1,0:T(8,128)S(1)} %get-tuple-element.50), channel_id=1, source_target_pairs={{1,0},{2,1},{3,2},{0,3},{5,4},{6,5},{7,6},{4,7},{9,8},{10,9},{11,1... | collective-permute-start | bytes 245768 | tf_op jit(solution)/shard_map/ppermute | solution.py:478
  16.9 2.7 %copy-start.2 = (bf16[768,512]{1,0:T(8,128)(2,1)S(1)}, bf16[768,512]{1,0:T(8,128)(2,1)}, u32[]{:S(2)}) copy-start(bf16[768,512]{1,0:T(8,128)(2,1)} %constant.20.clone.low_ref) | copy-start | bytes 2359300
  16.9 2.7 %copy-start.3 = (bf16[768,512]{1,0:T(8,128)(2,1)S(1)}, bf16[768,512]{1,0:T(8,128)(2,1)}, u32[]{:S(2)}) copy-start(bf16[768,512]{1,0:T(8,128)(2,1)} %constant.19.clone.high_ref) | copy-start | bytes 2359300
  16.9 2.7 %copy-start.6 = (f32[4,2,4,128]{3,2,1,0:T(4,128)S(1)}, f32[4,2,4,128]{3,2,1,0:T(4,128)}, u32[]{:S(2)}) copy-start(f32[4,2,4,128]{3,2,1,0:T(4,128)} %constant.21.clone.phase_ref.refs_10_) | copy-start | bytes 49156
  20.9 21.7 %copy-start.8 = (f32[4,2,8,128]{3,2,1,0:T(8,128)S(1)}, f32[4,2,8,128]{3,2,1,0:T(8,128)}, u32[]{:S(2)}) copy-start(f32[4,2,8,128]{3,2,1,0:T(8,128)} %constant.22.clone.symbol_ref) | copy-start | bytes 98308
  21.0 21.7 %copy-start.10 = (f32[8,128]{1,0:T(8,128)S(1)}, f32[8,128]{1,0:T(8,128)}, u32[]{:S(2)}) copy-start(f32[8,128]{1,0:T(8,128)} %constant.23.clone.share_ref) | copy-start | bytes 12292
  21.0 3.6 %collective-permute-start.13 = (f32[40,128]{1,0:T(8,128)S(1)}, f32[40,128]{1,0:T(8,128)S(1)}, u32[]{:S(2)}, u32[]{:S(2)}) collective-permute-start(f32[40,128]{1,0:T(8,128)S(1)} %get-tuple-element.63), channel_id=1, source_target_pairs={{0,1},{1,2},{2,3},{3,0},{4,5},{5,6},{6,7},{7,4},{8,9},{9,10},{10,1... | collective-permute-start | bytes 61448 | tf_op jit(solution)/shard_map/ppermute | solution.py:562
  22.5 2.1 %collective-permute-start.15 = (f32[40,128]{1,0:T(8,128)S(1)}, f32[40,128]{1,0:T(8,128)S(1)}, u32[]{:S(2)}, u32[]{:S(2)}) collective-permute-start(f32[40,128]{1,0:T(8,128)S(1)} %get-tuple-element.64), channel_id=1, source_target_pairs={{0,3},{1,0},{2,1},{3,2},{4,7},{5,4},{6,5},{7,6},{8,11},{9,8},{10,9... | collective-permute-start | bytes 61448 | tf_op jit(solution)/shard_map/ppermute | solution.py:562
  22.8 3.8 %collective-permute-start.14 = (f32[40,128]{1,0:T(8,128)S(1)}, f32[40,128]{1,0:T(8,128)S(1)}, u32[]{:S(2)}, u32[]{:S(2)}) collective-permute-start(f32[40,128]{1,0:T(8,128)S(1)} %get-tuple-element.65), channel_id=1, source_target_pairs={{0,2},{1,3},{2,0},{3,1},{4,6},{5,7},{6,4},{7,5},{8,10},{9,11},{10,... | collective-permute-start | bytes 61448 | tf_op jit(solution)/shard_map/ppermute | solution.py:562
  26.6 4.6 %collective-permute-start.16 = (f32[1,40,128]{2,1,0:T(8,128)S(1)}, f32[1,40,128]{2,1,0:T(8,128)S(1)}, u32[]{:S(2)}, u32[]{:S(2)}) collective-permute-start(f32[1,40,128]{2,1,0:T(8,128)S(1)} %get-tuple-element.60), channel_id=1, source_target_pairs={{0,4},{4,0},{8,12},{12,8},{16,20},{20,16},{24,28},{28,24},{1,5},{5... | collective-permute-start | bytes 61448 | tf_op jit(solution)/shard_map/ppermute | solution.py:576
  29.4 18.0 %copy-start.4 = (bf16[512,512]{1,0:T(8,128)(2,1)S(1)}, bf16[512,512]{1,0:T(8,128)(2,1)}, u32[]{:S(2)}) copy-start(bf16[512,512]{1,0:T(8,128)(2,1)} %constant.25.clone.refs_8_) | copy-start | bytes 1572868
  29.4 18.0 %copy-start.5 = (bf16[512,512]{1,0:T(8,128)(2,1)S(1)}, bf16[512,512]{1,0:T(8,128)(2,1)}, u32[]{:S(2)}) copy-start(bf16[512,512]{1,0:T(8,128)(2,1)} %constant.24.clone.refs_7_) | copy-start | bytes 1572868
  29.4 18.0 %collective-permute-start.24 = (f32[5,64,128]{2,1,0:T(8,128)S(1)}, f32[5,64,128]{2,1,0:T(8,128)S(1)}, u32[]{:S(2)}, u32[]{:S(2)}) collective-permute-start(f32[5,64,128]{2,1,0:T(8,128)S(1)} %get-tuple-element.61), channel_id=1, source_target_pairs={{1,0},{2,1},{3,2},{0,3},{5,4},{6,5},{7,6},{4,7},{9,8},{10,9},{11,1... | collective-permute-start | bytes 491528 | tf_op jit(solution)/shard_map/ppermute | solution.py:478
  29.5 17.9 %collective-permute-start.23 = (f32[5,64,128]{2,1,0:T(8,128)S(1)}, f32[5,64,128]{2,1,0:T(8,128)S(1)}, u32[]{:S(2)}, u32[]{:S(2)}) collective-permute-start(f32[5,64,128]{2,1,0:T(8,128)S(1)} %get-tuple-element.62), channel_id=1, source_target_pairs={{0,1},{1,2},{2,3},{3,0},{4,5},{5,6},{6,7},{7,4},{8,9},{9,10},{10,1... | collective-permute-start | bytes 491528 | tf_op jit(solution)/shard_map/ppermute | solution.py:478
  31.2 11.5 %collective-permute-start.19 = (f32[2,40,128]{2,1,0:T(8,128)S(1)}, f32[2,40,128]{2,1,0:T(8,128)S(1)}, u32[]{:S(2)}, u32[]{:S(2)}) collective-permute-start(f32[2,40,128]{2,1,0:T(8,128)S(1)} %pad_maximum_fusion), channel_id=1, source_target_pairs={{0,24},{4,28},{8,0},{12,4},{16,8},{20,12},{24,16},{28,20},{1,25},{... | collective-permute-start | bytes 122888 | tf_op jit(solution)/shard_map/ppermute | solution.py:576
  36.8 5.8 %collective-permute-start.18 = (f32[2,40,128]{2,1,0:T(8,128)S(1)}, f32[2,40,128]{2,1,0:T(8,128)S(1)}, u32[]{:S(2)}, u32[]{:S(2)}) collective-permute-start(f32[2,40,128]{2,1,0:T(8,128)S(1)} %pad_maximum_fusion), channel_id=1, source_target_pairs={{0,16},{4,20},{8,24},{12,28},{16,0},{20,4},{24,8},{28,12},{1,17},{... | collective-permute-start | bytes 122888 | tf_op jit(solution)/shard_map/ppermute | solution.py:576
  36.8 5.8 %collective-permute-start.17 = (f32[2,40,128]{2,1,0:T(8,128)S(1)}, f32[2,40,128]{2,1,0:T(8,128)S(1)}, u32[]{:S(2)}, u32[]{:S(2)}) collective-permute-start(f32[2,40,128]{2,1,0:T(8,128)S(1)} %pad_maximum_fusion), channel_id=1, source_target_pairs={{0,8},{4,12},{8,16},{12,20},{16,24},{20,28},{24,0},{28,4},{1,9},{5... | collective-permute-start | bytes 122888 | tf_op jit(solution)/shard_map/ppermute | solution.py:576
  42.7 4.8 %copy-start.9 = (bf16[48,128]{1,0:T(8,128)(2,1)S(1)}, bf16[48,128]{1,0:T(8,128)(2,1)}, u32[]{:S(2)}) copy-start(bf16[48,128]{1,0:T(8,128)(2,1)} %constant.26.clone.refs_9_) | copy-start | bytes 36868
  42.9 1.5 %collective-permute-start.22 = (f32[48,128]{1,0:T(8,128)S(1)}, f32[48,128]{1,0:T(8,128)S(1)}, u32[]{:S(2)}, u32[]{:S(2)}) collective-permute-start(f32[48,128]{1,0:T(8,128)S(1)} %shard_map.139.refs_0_), channel_id=1, source_target_pairs={{0,3},{1,0},{2,1},{3,2},{4,7},{5,4},{6,5},{7,6},{8,11},{9,8},{10,9... | collective-permute-start | bytes 73736 | tf_op jit(solution)/shard_map/ppermute | solution.py:589
  42.9 3.9 %collective-permute-start.21 = (f32[48,128]{1,0:T(8,128)S(1)}, f32[48,128]{1,0:T(8,128)S(1)}, u32[]{:S(2)}, u32[]{:S(2)}) collective-permute-start(f32[48,128]{1,0:T(8,128)S(1)} %shard_map.139.refs_0_), channel_id=1, source_target_pairs={{0,2},{1,3},{2,0},{3,1},{4,6},{5,7},{6,4},{7,5},{8,10},{9,11},{10,... | collective-permute-start | bytes 73736 | tf_op jit(solution)/shard_map/ppermute | solution.py:589
  44.2 3.3 %collective-permute-start.20 = (f32[48,128]{1,0:T(8,128)S(1)}, f32[48,128]{1,0:T(8,128)S(1)}, u32[]{:S(2)}, u32[]{:S(2)}) collective-permute-start(f32[48,128]{1,0:T(8,128)S(1)} %shard_map.139.refs_0_), channel_id=1, source_target_pairs={{0,1},{1,2},{2,3},{3,0},{4,5},{5,6},{6,7},{7,4},{8,9},{9,10},{10,1... | collective-permute-start | bytes 73736 | tf_op jit(solution)/shard_map/ppermute | solution.py:589

commit v3 on v2

--- a/solution.py
+++ b/solution.py
@@ -96,6 +96,22 @@
     return tables
 
 
+def paired(width):
+    return width & (width - 1) == 0
+
+
+def target_of(place, step, width):
+    return place ^ step if paired(width) else (place + step) % width
+
+
+def source_of(place, step, width):
+    return place ^ step if paired(width) else lax.rem(place - step + width, width)
+
+
+def step_between(place, target, width):
+    return place ^ target if paired(width) else lax.rem(target - place + width, width)
+
+
 on_chip = pl.BlockSpec(memory_space=pltpu.VMEM)
 off_chip = pl.BlockSpec(memory_space=pltpu.HBM)
 in_scalars = pl.BlockSpec(memory_space=pltpu.SMEM)
@@ -214,24 +230,44 @@
     return [reader(ref, layer) for layer in range(ref.shape[1])]
 
 
-def first_flux_kernel(state_ref, *out_refs):
-    parts = len(out_refs) // 2
-    fields, slab, rows, _ = state_ref.shape
-    count = rows // parts
-    for part in range(parts):
-        span = pl.ds(part * count, count)
-        for side, (layer, sign) in enumerate(((slab - 1, 1.0), (0, -1.0))):
-            values = [state_ref[f, layer, span] for f in range(fields)]
-            for f, value in enumerate(flux(values, sign)):
-                out_refs[2 * part + side][f] = value
-
-
-def first_rate_kernel(state_ref, source_ref, table_ref, rate_ref, waves_ref):
+def edge_layers_kernel(state_ref, up_ref, down_ref):
+    fields, slab = state_ref.shape[:2]
+    for f in range(fields):
+        up_ref[f] = state_ref[f, slab - 1]
+        down_ref[f] = state_ref[f, 0]
+
+
+def first_rate_kernel(
+    state_ref,
+    source_ref,
+    table_ref,
+    rate_ref,
+    waves_ref,
+    rate_up_ref,
+    rate_down_ref,
+    feed_up_ref,
+    feed_down_ref,
+    *,
+    step,
+):
     fields, slab, rows, cols = state_ref.shape
+    last = slab - 1
 
     def put(layer, rates):
         for f in range(fields):
             rate_ref[f, layer] = rates[f]
+            if layer == last:
+                rate_up_ref[f] = rates[f]
+            if layer == 0:
+                rate_down_ref[f] = rates[f]
+        for inner, edge, out_ref, sign in (
+            (last - 1, last, feed_up_ref, 1.0),
+            (1, 0, feed_down_ref, -1.0),
+        ):
+            if layer == inner:
+                second = [state_ref[f, layer] + step * rates[f] for f in range(fields)]
+                for f, value in enumerate(flux(second, sign)):
+                    out_ref[f] = source_ref[f, edge] + value
 
     slab_rates(readers(state_ref), readers(source_ref), put)
     keep = table_ref.shape[0] // 4
@@ -242,93 +278,147 @@
     waves_ref[:, lanes:] = imag
 
 
-def edge_kernel(
-    state_ref, rate_ref, below_ref, above_ref, edge_ref, up_ref, down_ref, *, step, part
+def second_rate_kernel(
+    state_ref,
+    rate_ref,
+    source_ref,
+    below_ref,
+    above_ref,
+    next_ref,
+    stage_ref,
+    *,
+    step,
 ):
     fields, slab = state_ref.shape[:2]
-    last = slab - 1
-    count = below_ref.shape[1]
-    span = pl.ds(part * count, count)
-    for side, layer, came_ref, out_ref, sign in (
-        (1, last, above_ref, up_ref, 1.0),
-        (0, 0, below_ref, down_ref, -1.0),
-    ):
-        values = [
-            state_ref[f, layer, span] + step * (rate_ref[f, layer, span] + came_ref[f])
-            for f in range(fields)
-        ]
-        for f, value in enumerate(flux(values, sign)):
-            edge_ref[side, f] = values[f]
-            out_ref[f] = value
-
-
-def fill_stage(state_ref, rate_ref, edge_refs, stage_ref, step):
-    fields, slab = state_ref.shape[:2]
-    for f in range(fields):
-        for part, edge_ref in enumerate(edge_refs):
-            count = edge_ref.shape[2]
-            span = pl.ds(part * count, count)
-            stage_ref[f, 0, span] = edge_ref[0, f]
-            stage_ref[f, slab - 1, span] = edge_ref[1, f]
-        for layer in range(1, slab - 1):
-            stage_ref[f, layer] = state_ref[f, layer] + step * rate_ref[f, layer]
-
-
-def rate_kernel(state_ref, rate_ref, source_ref, sum_ref, *refs, step, share):
-    *edge_refs, next_ref, total_ref, stage_ref = refs
-    fields = state_ref.shape[0]
-    fill_stage(state_ref, rate_ref, edge_refs, stage_ref, step)
+    for layer in range(slab):
+        rates = [rate_ref[f, layer] for f in range(fields)]
+        for edge, came_ref, sign in ((0, below_ref, 1.0), (slab - 1, above_ref, -1.0)):
+            if layer == edge:
+                given = flux([came_ref[f] for f in range(fields)], sign)
+                rates = [rate + gift for rate, gift in zip(rates, given)]
+        for f in range(fields):
+            stage_ref[f, layer] = state_ref[f, layer] + step * rates[f]
 
     def put(layer, rates):
         for f in range(fields):
             next_ref[f, layer] = rates[f]
-            total_ref[f, layer] = sum_ref[f, layer] * share[0] + stage_ref[f, layer] * share[1]
 
     slab_rates(readers(stage_ref), readers(source_ref), put)
+
+
+def third_rate_kernel(
+    state_ref,
+    second_ref,
+    rate_ref,
+    source_ref,
+    below_ref,
+    above_ref,
+    below_rate_ref,
+    above_rate_ref,
+    base_ref,
+    edge_rate_ref,
+    edge_sum_ref,
+    inner_sum_ref,
+    third_ref,
+    fourth_ref,
+    *,
+    steps,
+    weight,
+):
+    fields, slab, rows, cols = state_ref.shape
+    last = slab - 1
+    ids = range(fields)
+    blank = [jnp.zeros((rows, cols), jnp.float32)] * fields
+    for layer in range(1, last):
+        for f in ids:
+            third_ref[f, layer] = state_ref[f, layer] + steps[1] * rate_ref[f, layer]
+    for side, edge, came_ref, came_rate_ref, sign in (
+        (0, 0, below_ref, below_rate_ref, 1.0),
+        (1, last, above_ref, above_rate_ref, -1.0),
+    ):
+        outward = flux([state_ref[f, edge] for f in ids], -sign)
+        second = [came_ref[f] + steps[0] * (came_rate_ref[f] + outward[f]) for f in ids]
+        for f, value in enumerate(flux(second, sign)):
+            third_ref[f, edge] = state_ref[f, edge] + steps[1] * (rate_ref[f, edge] + value)
+        outward = flux([second_ref[f, edge] for f in ids], -sign)
+        rates = level_rate(second, outward)
+        for f in ids:
+            base_ref[side, f] = came_ref[f] + steps[1] * rates[f]
+
+    def put(layer, rates):
+        for f in ids:
+            if 0 < layer < last:
+                fourth_ref[f, layer - 1] = state_ref[f, layer] + steps[2] * rates[f]
+            else:
+                edge_rate_ref[0 if layer == 0 else 1, f] = rates[f]
+
+    slab_rates(readers(third_ref), readers(source_ref), put)
+
+    def so_far(f, layer):
+        return (
+            2.0 * third_ref[f, layer] + second_ref[f, layer] - state_ref[f, layer]
+        ) * (1.0 / 3.0)
+
+    def put_inner(index, rates):
+        for f in ids:
+            inner_sum_ref[f, index] = (
+                so_far(f, index + 1) + fourth_ref[f, index] * (1.0 / 3.0) + weight * rates[f]
+            )
+
+    slab_rates(readers(fourth_ref), readers(source_ref)[1:last], put_inner)
+    for side, edge, inner, sign in ((0, 0, 0, -1.0), (1, last, slab - 3, 1.0)):
+        for f, value in enumerate(flux([fourth_ref[f, inner] for f in ids], sign)):
+            edge_sum_ref[side, f] = so_far(f, edge) + weight * (source_ref[f, edge] + value)
 
 
 def forward_kernel(
     state_ref,
-    rate_ref,
-    source_ref,
-    sum_ref,
+    base_ref,
+    edge_rate_ref,
+    edge_sum_ref,
+    inner_sum_ref,
+    below_ref,
+    above_ref,
     shifted_ref,
     table_ref,
     high_ref,
     low_ref,
     phase_ref,
-    *refs,
-    step,
+    out_ref,
+    inner_ref,
+    outer_ref,
+    *,
+    steps,
     weight,
 ):
-    *came_refs, out_ref, inner_ref, outer_ref, edge_ref, stage_ref = refs
     fields, slab, rows, cols = state_ref.shape
     last = slab - 1
-    parts = len(came_refs) // 2
-    count = rows // parts
-    for part in range(parts):
-        span = pl.ds(part * count, count)
-        below_ref, above_ref = came_refs[2 * part : 2 * part + 2]
-        for f in range(fields):
-            edge_ref[0, f, span] = state_ref[f, 0, span] + step * (
-                rate_ref[f, 0, span] + below_ref[f]
+    ids = range(fields)
+    blank = [jnp.zeros((rows, cols), jnp.float32)] * fields
+    inward = {}
+    for side, edge, came_ref, sign in ((0, 0, below_ref, 1.0), (1, last, above_ref, -1.0)):
+        third = [base_ref[side, f] + steps[1] * came_ref[f] for f in ids]
+        given = flux(third, sign)
+        fourth = [
+            state_ref[f, edge] + steps[2] * (edge_rate_ref[side, f] + given[f]) for f in ids
+        ]
+        rates = level_rate(fourth, blank)
+        for f in ids:
+            inner_ref[f, edge] = (
+                edge_sum_ref[side, f] + fourth[f] * (1.0 / 3.0) + weight * rates[f]
             )
-            edge_ref[1, f, span] = state_ref[f, last, span] + step * (
-                rate_ref[f, last, span] + above_ref[f]
-            )
-    fill_stage(state_ref, rate_ref, [edge_ref], stage_ref, step)
-
-    def put(layer, rates):
-        for f in range(fields):
-            inner_ref[f, layer] = (
-                sum_ref[f, layer] + stage_ref[f, layer] * (1.0 / 3.0) + weight * rates[f]
-            )
-
-    slab_rates(readers(stage_ref), readers(source_ref), put)
-    for f, value in enumerate(flux([edge_ref[0, f] for f in range(fields)], -1.0)):
-        outer_ref[0, f] = weight * value
-    for f, value in enumerate(flux([edge_ref[1, f] for f in range(fields)], 1.0)):
-        outer_ref[1, f] = weight * value
+        for f, value in enumerate(flux(fourth, -sign)):
+            outer_ref[side, f] = weight * value
+        inner = 1 if side == 0 else last - 1
+        for f, value in enumerate(flux(fourth, sign)):
+            earlier = inner_ref if inner in inward else inner_sum_ref
+            shift = 0 if inner in inward else 1
+            inner_ref[f, inner] = earlier[f, inner - shift] + weight * value
+        inward[inner] = True
+    for layer in range(1, last):
+        if layer not in inward:
+            for f in ids:
+                inner_ref[f, layer] = inner_sum_ref[f, layer - 1]
 
     width = out_ref.shape[0]
     keep = table_ref.shape[0] // 4
@@ -354,7 +444,7 @@
             block * phase_ref[place, 0, group, :][None, :]
             + pltpu.roll(block, half, 1) * phase_ref[place, 1, group, :][None, :]
         )
-        out_ref[lax.rem(group - place + width, width)] = turned
+        out_ref[step_between(place, group, width)] = turned
 
 
 def slot_of(moment, moment_id, slices):
@@ -427,7 +517,7 @@
     keep = lines // fields
     sums = None
     for step in range(width):
-        group = lax.rem(place - step + width, width)
+        group = source_of(place, step, width)
         block = block_refs[step][:lines, :]
         order_ref[group] = (
             block * phase_ref[place, 0, group, :][None, :]
@@ -499,67 +589,63 @@
     tables = make_tables(slab, width, rows, cols)
     real = jnp.float32
 
-    parts = 2 if rows % 16 == 0 else 1
-    layer_shape = jax.ShapeDtypeStruct((fields, rows // parts, cols), real)
-    edge_shape = jax.ShapeDtypeStruct((2, fields, rows // parts, cols), real)
+    layer_shape = jax.ShapeDtypeStruct((fields, rows, cols), real)
+    edge_shape = jax.ShapeDtypeStruct((2, fields, rows, cols), real)
     slab_shape = jax.ShapeDtypeStruct((fields, slab, rows, cols), real)
-    whole_slab = pltpu.VMEM((fields, slab, rows, cols), real)
-
-    given = local_call(
-        first_flux_kernel,
-        (layer_shape,) * (2 * parts),
-        [state_now],
-    )
-    came = [halo(*given[2 * part : 2 * part + 2]) for part in range(parts)]
-    rates, start_waves = local_call(
-        first_rate_kernel,
-        (slab_shape, jax.ShapeDtypeStruct((lines, 2 * slab * rows), real)),
+    inner_shape = jax.ShapeDtypeStruct((fields, slab - 2, rows, cols), real)
+    steps = (0.5 * time_step, 0.5 * time_step, time_step)
+    weight = time_step / 6.0
+
+    up, down = local_call(edge_layers_kernel, (layer_shape, layer_shape), [state_now])
+    below, above = halo(up, down)
+    rates, start_waves, *given = local_call(
+        functools.partial(first_rate_kernel, step=steps[0]),
+        (
+            slab_shape,
+            jax.ShapeDtypeStruct((lines, 2 * slab * rows), real),
+            *(layer_shape,) * 4,
+        ),
         [state_now, source, tables["xforward"]],
     )
+    below_rate, above_rate = halo(given[0], given[1])
+    below_feed, above_feed = halo(given[2], given[3])
     next_waves = lax.ppermute(start_waves, "tm", [(i + 1, i) for i in range(slices - 1)])
-    total = state_now
-    for stage in range(2):
-        step = 0.5 * time_step
-        edges, arrived = [], came
-        came = []
-        for part in range(parts):
-            edge, up, down = local_call(
-                functools.partial(edge_kernel, step=step, part=part),
-                (edge_shape, layer_shape, layer_shape),
-                [state_now, rates, *arrived[part]],
-            )
-            edges.append(edge)
-            came.append(halo(up, down))
-        share = ((-1.0 / 3.0, 1.0 / 3.0), (1.0, 2.0 / 3.0))[stage]
-        rates, total = local_call(
-            functools.partial(rate_kernel, step=step, share=share),
-            (slab_shape, slab_shape),
-            [state_now, rates, source, total, *edges],
-            [whole_slab],
-        )
+    rates, second = local_call(
+        functools.partial(second_rate_kernel, step=steps[0]),
+        (slab_shape, slab_shape),
+        [state_now, rates, source, below, above],
+    )
+    base, edge_rate, edge_sum, inner_sum = local_call(
+        functools.partial(third_rate_kernel, steps=steps, weight=weight),
+        (edge_shape, edge_shape, edge_shape, inner_shape),
+        [state_now, second, rates, source, below, above, below_rate, above_rate],
+        [
+            pltpu.VMEM((fields, slab, rows, cols), real),
+            pltpu.VMEM((fields, slab - 2, rows, cols), real),
+        ],
+    )
     waves, fine_inner, fine_outer = local_call(
-        functools.partial(forward_kernel, step=time_step, weight=time_step / 6.0),
-        (
-            jax.ShapeDtypeStruct((width, lines, lanes), real),
-            slab_shape,
-            jax.ShapeDtypeStruct((2, fields, rows, cols), real),
-        ),
+        functools.partial(forward_kernel, steps=steps, weight=weight),
+        (jax.ShapeDtypeStruct((width, lines, lanes), real), slab_shape, edge_shape),
         [
             state_now,
-            rates,
-            source,
-            total,
+            base,
+            edge_rate,
+            edge_sum,
+            inner_sum,
+            below_feed,
+            above_feed,
             next_waves,
             tables["xforward"],
             *tables["yzforward"],
             tables["phase"],
-            *[array for pair in came for array in pair],
         ],
-        [pltpu.VMEM((2, fields, rows, cols), real), whole_slab],
     )
     jump = waves[0]
     for step in range(1, width):
-        part = lax.ppermute(waves[step], "space", [(i, (i + step) % width) for i in range(width)])
+        part = lax.ppermute(
+            waves[step], "space", [(i, target_of(i, step, width)) for i in range(width)]
+        )
         jump = jump + part
 
     below, above = halo(fine_outer[1], fine_outer[0])
@@ -586,7 +672,7 @@
     blocks = [message]
     for step in range(1, width):
         blocks.append(
-            lax.ppermute(message, "space", [(i, (i + step) % width) for i in range(width)])
+            lax.ppermute(message, "space", [(i, target_of(i, step, width)) for i in range(width)])
         )
     cells = fields * depth * rows * cols
     ends, slice_norm, total_norm = local_call(
@@ -609,7 +695,7 @@
         ],
         [
             pltpu.VMEM((width, lines, lanes), real),
-            whole_slab,
+            pltpu.VMEM((fields, slab, rows, cols), real),
             pltpu.SMEM((2, 1), real),
             pltpu.SemaphoreType.DMA((fields,)),
             pltpu.SemaphoreType.DMA((2,)),

time: 49.1 us -> 42.2 us (0.86)
  starting transfers between devices: 28.3 us -> 18.9 us
  waiting for transfers between devices: 13.5 us -> 14.9 us
  local copies, waits for them, and re-layouts: 1.18 us -> 1.89 us
    ppermute x14 -> x8, starting transfers between devices: 12.5 us -> 6.62 us  [halo(): return (lax.ppermute(up, 'space', ups), lax.ppermute(down, 'space', downs))]
    ppermute x4, starting transfers between devices: 9.47 us -> 6.82 us  [shards(): parts.append(lax.ppermute(jumps, 'tm', pairs))]
    ppermute x1, waiting for transfers between devices: 0.35 us -> 2.37 us  [shards(): lax.ppermute(start_waves, 'tm', [(i + 1, i) for i in range(slices - 1)])]
    ppermute x14 -> x8, waiting for transfers between devices: 2.07 us -> 1.21 us  [halo(): return (lax.ppermute(up, 'space', ups), lax.ppermute(down, 'space', downs))]
    ppermute x6, starting transfers between devices: 4.98 us -> 4.15 us  [the longest x3 2.29 us: shards(): lax.ppermute(waves[step], 'space', [(i, target_of(i, step, width)) for i...]
    unnamed x25 -> x27, local copies, waits for them, and re-layouts: 1.15 us -> 1.85 us
    ppermute x6, waiting for transfers between devices: 5.09 us -> 5.76 us  [the longest x3 3.72 us: shards(): lax.ppermute(waves[step], 'space', [(i, target_of(i, step, width)) for i...]
    pallas_call x11 -> x7, Pallas kernels: 5.09 us -> 5.43 us  [local_call(): pl.pallas_call(kernel, out_shape=out_shape, in_specs=specs, out_specs=out...]
  transfers between devices with their start and end apart: 25 -> 19, of which waited for: 9 -> 9; matrix products, arithmetic and copies ran while one was open for 0% -> 0% of each run, Pallas kernels for 5% -> 7%
where the time goes in v3:
time: 42.2 us; the launch traced here: 41.9 us
  starting transfers between devices  18.9 us (45%)
  waiting for transfers between devices  14.9 us (35%)
  Pallas kernels  5.43 us (13%)
  local copies, waits for them, and re-layouts  1.89 us (4%)
  between operations  0.83 us (2%)
    ppermute x4, starting transfers between devices, shards(): parts.append(lax.ppermute(jumps, 'tm', pairs))  6.82 us
    ppermute x8, starting transfers between devices, halo(): return (lax.ppermute(up, 'space', ups), lax.ppermute(down, 'space', downs))  6.62 us
    ppermute x4, waiting for transfers between devices, shards(): parts.append(lax.ppermute(jumps, 'tm', pairs))  5.56 us
    pallas_call x7, Pallas kernels, local_call(): pl.pallas_call(kernel, out_shape=out_shape, in_specs=specs, out_specs=out...  5.43 us
    ppermute x3, waiting for transfers between devices, shards(): lax.ppermute(waves[step], 'space', [(i, target_of(i, step, width)) for i...  3.72 us
    ppermute x1, waiting for transfers between devices, shards(): lax.ppermute(start_waves, 'tm', [(i + 1, i) for i in range(slices - 1)])  2.37 us
    ppermute x3, starting transfers between devices, shards(): lax.ppermute(waves[step], 'space', [(i, target_of(i, step, width)) for i...  2.29 us
    ppermute x3, waiting for transfers between devices, shards(): lax.ppermute(message, 'space', [(i, target_of(i, step, width)) for i in r...  2.04 us
  transfers between devices with their start and end apart: 19, of which 9 were waited for; matrix products, arithmetic and copies ran while one was open for 0% of the time, Pallas kernels for 7%

profile of v3, /device:TPU:0, one launch (start us, length us, event | category | flops | bytes accessed | tf_op | source)
XLA Modules:
  0.0 41.9 jit_solution(8332749489535678186)
XLA Ops:
  0.6 0.0 copy-start
  0.6 1.1 %copy-done = f32[1,5,4,64,128]{4,3,2,1,0:T(8,128)S(1)} copy-done((f32[1,5,4,64,128]{4,3,2,1,0:T(8,128)S(1)}, f32[1,5,4,64,128]{4,3,2,1,0:T(8,128)}, u32[]{:S(2)}) %copy-start) | copy-done | bytes 655384
  1.7 0.0 copy-start.1
  1.7 0.5 %collective-permute-start = (f32[5,64,128]{2,1,0:T(8,128)S(1)}, f32[5,64,128]{2,1,0:T(8,128)S(1)}, u32[]{:S(2)}, u32[]{:S(2)}) collective-permute-start(f32[5,64,128]{2,1,0:T(8,128)S(1)} %get-tuple-element.24), channel_id=1, source_target_pairs={{0,1},{1,2},{2,3},{3,0},{4,5},{5,6},{6,7},{7,4},{8,9},{9,10},{10,1... | collective-permute-start | bytes 491528 | tf_op jit(solution)/shard_map/ppermute | solution.py:568
  2.3 2.0 %collective-permute-start.1 = (f32[5,64,128]{2,1,0:T(8,128)S(1)}, f32[5,64,128]{2,1,0:T(8,128)S(1)}, u32[]{:S(2)}, u32[]{:S(2)}) collective-permute-start(f32[5,64,128]{2,1,0:T(8,128)S(1)} %get-tuple-element.25), channel_id=1, source_target_pairs={{1,0},{2,1},{3,2},{0,3},{5,4},{6,5},{7,6},{4,7},{9,8},{10,9},{11,1... | collective-permute-start | bytes 491528 | tf_op jit(solution)/shard_map/ppermute | solution.py:568
  4.3 0.0 copy-done.1
  4.3 0.0 copy-start.7
  4.3 0.7 %copy-done.7 = bf16[32,256]{1,0:T(8,128)(2,1)S(1)} copy-done((bf16[32,256]{1,0:T(8,128)(2,1)S(1)}, bf16[32,256]{1,0:T(8,128)(2,1)}, u32[]{:S(2)}) %copy-start.7) | copy-done | bytes 16408
  5.0 0.7 %shard_map.130 = (f32[5,4,64,128]{3,2,1,0:T(8,128)S(1)}, f32[40,512]{1,0:T(8,128)S(1)}, f32[5,64,128]{2,1,0:T(8,128)S(1)}, f32[5,64,128]{2,1,0:T(8,128)S(1)}, f3...) custom-call(f32[5,4,64,128]{3,2,1,0:T(8,128)S(1)} %bitcast.25, f32[5,4,64,128]{3,2,1,0:T(8,128)S(1)} %copy-done.1, ...), custom_call_target="tpu_custom_call" | custom-call | tf_op jit(solution)/shard_map/pallas_call | solution.py:127
  5.7 0.7 %collective-permute-start.2 = (f32[5,64,128]{2,1,0:T(8,128)S(1)}, f32[5,64,128]{2,1,0:T(8,128)S(1)}, u32[]{:S(2)}, u32[]{:S(2)}) collective-permute-start(f32[5,64,128]{2,1,0:T(8,128)S(1)} %get-tuple-element.28), channel_id=1, source_target_pairs={{0,1},{1,2},{2,3},{3,0},{4,5},{5,6},{6,7},{7,4},{8,9},{9,10},{10,1... | collective-permute-start | bytes 491528 | tf_op jit(solution)/shard_map/ppermute | solution.py:568
  6.3 1.1 %collective-permute-start.3 = (f32[5,64,128]{2,1,0:T(8,128)S(1)}, f32[5,64,128]{2,1,0:T(8,128)S(1)}, u32[]{:S(2)}, u32[]{:S(2)}) collective-permute-start(f32[5,64,128]{2,1,0:T(8,128)S(1)} %get-tuple-element.29), channel_id=1, source_target_pairs={{1,0},{2,1},{3,2},{0,3},{5,4},{6,5},{7,6},{4,7},{9,8},{10,9},{11,1... | collective-permute-start | bytes 491528 | tf_op jit(solution)/shard_map/ppermute | solution.py:568
  7.5 0.6 %collective-permute-start.4 = (f32[5,64,128]{2,1,0:T(8,128)S(1)}, f32[5,64,128]{2,1,0:T(8,128)S(1)}, u32[]{:S(2)}, u32[]{:S(2)}) collective-permute-start(f32[5,64,128]{2,1,0:T(8,128)S(1)} %get-tuple-element.34), channel_id=1, source_target_pairs={{0,1},{1,2},{2,3},{3,0},{4,5},{5,6},{6,7},{7,4},{8,9},{9,10},{10,1... | collective-permute-start | bytes 491528 | tf_op jit(solution)/shard_map/ppermute | solution.py:568
  8.1 0.0 collective-permute-done.below_ref
  8.1 1.1 %collective-permute-start.5 = (f32[5,64,128]{2,1,0:T(8,128)S(1)}, f32[5,64,128]{2,1,0:T(8,128)S(1)}, u32[]{:S(2)}, u32[]{:S(2)}) collective-permute-start(f32[5,64,128]{2,1,0:T(8,128)S(1)} %get-tuple-element.35), channel_id=1, source_target_pairs={{1,0},{2,1},{3,2},{0,3},{5,4},{6,5},{7,6},{4,7},{9,8},{10,9},{11,1... | collective-permute-start | bytes 491528 | tf_op jit(solution)/shard_map/ppermute | solution.py:568
  9.2 0.0 collective-permute-done.1.above_ref
  9.2 1.3 %collective-permute-start.6 = (f32[40,512]{1,0:T(8,128)S(1)}, f32[40,512]{1,0:T(8,128)S(1)}, u32[]{:S(2)}, u32[]{:S(2)}) collective-permute-start(f32[40,512]{1,0:T(8,128)S(1)} %get-tuple-element.36), channel_id=1, source_target_pairs={{4,0},{8,4},{12,8},{16,12},{20,16},{24,20},{28,24},{5,1},{9,5},{13... | collective-permute-start | bytes 245768 | tf_op jit(solution)/shard_map/ppermute | solution.py:612
  10.5 0.6 %shard_map.132 = (f32[5,4,64,128]{3,2,1,0:T(8,128)S(1)}, f32[5,4,64,128]{3,2,1,0:T(8,128)S(1)}) custom-call(f32[5,4,64,128]{3,2,1,0:T(8,128)S(1)} %bitcast.26, f32[5,4,64,128]{3,2,1,0:T(8,128)S(1)} %get-tuple-element.23.rate_ref, f32[5,4,64,128]{3,2,1,0:T(8,128)S(1)} %copy-done.1, f32[5,64,128]{2,1,0:T(8,128)S(1)} %collective-permute-done.below_ref, ...), custom_call_target="tpu_custom_call" | custom-call | tf_op jit(solution)/shard_map/pallas_call | solution.py:127
  11.2 0.7 %collective-permute-done.2.below_rate_ref = f32[5,64,128]{2,1,0:T(8,128)S(1)} collective-permute-done((f32[5,64,128]{2,1,0:T(8,128)S(1)}, f32[5,64,128]{2,1,0:T(8,128)S(1)}, u32[]{:S(2)}, u32[]{:S(2)}) %collective-permute-start.2) | collective-permute-done | bytes 163872 | tf_op jit(solution)/shard_map/ppermute | solution.py:568
  11.9 0.5 %collective-permute-done.3.above_rate_ref = f32[5,64,128]{2,1,0:T(8,128)S(1)} collective-permute-done((f32[5,64,128]{2,1,0:T(8,128)S(1)}, f32[5,64,128]{2,1,0:T(8,128)S(1)}, u32[]{:S(2)}, u32[]{:S(2)}) %collective-permute-start.3) | collective-permute-done | bytes 163872 | tf_op jit(solution)/shard_map/ppermute | solution.py:568
  12.4 0.0 copy-start.2
  12.4 0.0 copy-start.3
  12.4 0.0 copy-start.6
  12.4 0.0 copy-start.8
  12.4 1.4 %shard_map.133 = (f32[2,5,64,128]{3,2,1,0:T(8,128)S(1)}, f32[2,5,64,128]{3,2,1,0:T(8,128)S(1)}, f32[2,5,64,128]{3,2,1,0:T(8,128)S(1)}, f32[5,2,64,128]{3,2,1,0:T(8,128)S(1)}) custom-call(f32[5,4,64,128]{3,2,1,0:T(8,128)S(1)} %bitcast.27, f32[5,4,64,128]{3,2,1,0:T(8,128)S(1)} %get-tuple-element.26.second_ref, ...), custom_call_target="tpu_custom_call" | custom-call | tf_op jit(solution)/shard_map/pallas_call | solution.py:127
  13.8 2.4 %collective-permute-done.6.shifted_ref = f32[40,512]{1,0:T(8,128)S(1)} collective-permute-done((f32[40,512]{1,0:T(8,128)S(1)}, f32[40,512]{1,0:T(8,128)S(1)}, u32[]{:S(2)}, u32[]{:S(2)}) %collective-permute-start.6) | collective-permute-done | bytes 81952 | tf_op jit(solution)/shard_map/ppermute | solution.py:612
  16.1 0.0 collective-permute-done.4.below_ref
  16.2 0.0 collective-permute-done.5.above_ref
  16.2 0.0 copy-done.2
  16.2 0.0 copy-done.3
  16.2 0.0 copy-done.6
  16.2 0.0 copy-done.8
  16.2 1.0 %shard_map.134 = (f32[4,40,128]{2,1,0:T(8,128)S(1)}, f32[5,4,64,128]{3,2,1,0:T(8,128)S(1)}, f32[2,5,64,128]{3,2,1,0:T(8,128)S(1)}) custom-call(f32[5,4,64,128]{3,2,1,0:T(8,128)S(1)} %bitcast.28, f32[2,5,64,128]{3,2,1,0:T(8,128)S(1)} %get-tuple-element.30.base_ref, f32[2,5,64,128]{3,2,1,0:T(8,128)S(1)} %get-tuple-element.31.edge_rate_ref, ...), custom_call_target="tpu_custom_call" | custom-call | tf_op jit(solution)/shard_map/pallas_call | solution.py:127
  17.2 0.5 %collective-permute-start.7 = (f32[40,128]{1,0:T(8,128)S(1)}, f32[40,128]{1,0:T(8,128)S(1)}, u32[]{:S(2)}, u32[]{:S(2)}) collective-permute-start(f32[40,128]{1,0:T(8,128)S(1)} %get-tuple-element.47), channel_id=1, source_target_pairs={{0,1},{1,0},{2,3},{3,2},{4,5},{5,4},{6,7},{7,6},{8,9},{9,8},{10,11... | collective-permute-start | bytes 61448 | tf_op jit(solution)/shard_map/ppermute | solution.py:646
  17.8 1.7 %collective-permute-start.9 = (f32[40,128]{1,0:T(8,128)S(1)}, f32[40,128]{1,0:T(8,128)S(1)}, u32[]{:S(2)}, u32[]{:S(2)}) collective-permute-start(f32[40,128]{1,0:T(8,128)S(1)} %get-tuple-element.48), channel_id=1, source_target_pairs={{0,3},{1,2},{2,1},{3,0},{4,7},{5,6},{6,5},{7,4},{8,11},{9,10},{10,... | collective-permute-start | bytes 61448 | tf_op jit(solution)/shard_map/ppermute | solution.py:646
  19.5 0.1 collective-permute-start.8
  19.5 0.0 collective-permute-done.7
  19.5 1.5 %collective-permute-done.9 = f32[40,128]{1,0:T(8,128)S(1)} collective-permute-done((f32[40,128]{1,0:T(8,128)S(1)}, f32[40,128]{1,0:T(8,128)S(1)}, u32[]{:S(2)}, u32[]{:S(2)}) %collective-permute-start.9) | collective-permute-done | bytes 20512 | tf_op jit(solution)/shard_map/ppermute | solution.py:646
  21.0 2.3 %collective-permute-done.8 = f32[40,128]{1,0:T(8,128)S(1)} collective-permute-done((f32[40,128]{1,0:T(8,128)S(1)}, f32[40,128]{1,0:T(8,128)S(1)}, u32[]{:S(2)}, u32[]{:S(2)}) %collective-permute-start.8) | collective-permute-done | bytes 20512 | tf_op jit(solution)/shard_map/ppermute | solution.py:646
  23.2 2.2 %collective-permute-start.10 = (f32[1,40,128]{2,1,0:T(8,128)S(1)}, f32[1,40,128]{2,1,0:T(8,128)S(1)}, u32[]{:S(2)}, u32[]{:S(2)}) collective-permute-start(f32[1,40,128]{2,1,0:T(8,128)S(1)} %get-tuple-element.44), channel_id=1, source_target_pairs={{0,4},{4,0},{8,12},{12,8},{16,20},{20,16},{24,28},{28,24},{1,5},{5... | collective-permute-start | bytes 61448 | tf_op jit(solution)/shard_map/ppermute | solution.py:662
  25.5 0.1 collective-permute-start.18
  25.5 0.5 %collective-permute-start.17 = (f32[5,64,128]{2,1,0:T(8,128)S(1)}, f32[5,64,128]{2,1,0:T(8,128)S(1)}, u32[]{:S(2)}, u32[]{:S(2)}) collective-permute-start(f32[5,64,128]{2,1,0:T(8,128)S(1)} %get-tuple-element.46), channel_id=1, source_target_pairs={{0,1},{1,2},{2,3},{3,0},{4,5},{5,6},{6,7},{7,4},{8,9},{9,10},{10,1... | collective-permute-start | bytes 491528 | tf_op jit(solution)/shard_map/ppermute | solution.py:568
  26.0 1.2 %collective-permute-done.10 = f32[1,40,128]{2,1,0:T(8,128)S(1)} collective-permute-done((f32[1,40,128]{2,1,0:T(8,128)S(1)}, f32[1,40,128]{2,1,0:T(8,128)S(1)}, u32[]{:S(2)}, u32[]{:S(2)}) %collective-permute-start.10) | collective-permute-done | bytes 20512 | tf_op jit(solution)/shard_map/ppermute | solution.py:662
  27.2 3.2 %collective-permute-start.13 = (f32[2,40,128]{2,1,0:T(8,128)S(1)}, f32[2,40,128]{2,1,0:T(8,128)S(1)}, u32[]{:S(2)}, u32[]{:S(2)}) collective-permute-start(f32[2,40,128]{2,1,0:T(8,128)S(1)} %pad_maximum_fusion), channel_id=1, source_target_pairs={{0,24},{4,28},{8,0},{12,4},{16,8},{20,12},{24,16},{28,20},{1,25},{... | collective-permute-start | bytes 122888 | tf_op jit(solution)/shard_map/ppermute | solution.py:662
  30.4 0.0 collective-permute-start.12
  30.4 1.4 %collective-permute-start.11 = (f32[2,40,128]{2,1,0:T(8,128)S(1)}, f32[2,40,128]{2,1,0:T(8,128)S(1)}, u32[]{:S(2)}, u32[]{:S(2)}) collective-permute-start(f32[2,40,128]{2,1,0:T(8,128)S(1)} %pad_maximum_fusion), channel_id=1, source_target_pairs={{0,8},{4,12},{8,16},{12,20},{16,24},{20,28},{24,0},{28,4},{1,9},{5... | collective-permute-start | bytes 122888 | tf_op jit(solution)/shard_map/ppermute | solution.py:662
  31.8 4.4 %collective-permute-done.11 = f32[2,40,128]{2,1,0:T(8,128)S(1)} collective-permute-done((f32[2,40,128]{2,1,0:T(8,128)S(1)}, f32[2,40,128]{2,1,0:T(8,128)S(1)}, u32[]{:S(2)}, u32[]{:S(2)}) %collective-permute-start.11) | collective-permute-done | bytes 40992 | tf_op jit(solution)/shard_map/ppermute | solution.py:662
  36.2 0.0 collective-permute-done.12
  36.2 0.0 collective-permute-done.13
  36.3 0.0 copy-done.9
  36.3 0.0 copy-done.11
  36.3 0.0 copy-start.10
  36.3 0.2 shard_map.135.refs_0_
  36.5 0.0 collective-permute-start.16
  36.5 0.7 %collective-permute-start.15 = (f32[48,128]{1,0:T(8,128)S(1)}, f32[48,128]{1,0:T(8,128)S(1)}, u32[]{:S(2)}, u32[]{:S(2)}) collective-permute-start(f32[48,128]{1,0:T(8,128)S(1)} %shard_map.135.refs_0_), channel_id=1, source_target_pairs={{0,2},{1,3},{2,0},{3,1},{4,6},{5,7},{6,4},{7,5},{8,10},{9,11},{10,... | collective-permute-start | bytes 73736 | tf_op jit(solution)/shard_map/ppermute | solution.py:675
  37.2 1.2 %collective-permute-start.14 = (f32[48,128]{1,0:T(8,128)S(1)}, f32[48,128]{1,0:T(8,128)S(1)}, u32[]{:S(2)}, u32[]{:S(2)}) collective-permute-start(f32[48,128]{1,0:T(8,128)S(1)} %shard_map.135.refs_0_), channel_id=1, source_target_pairs={{0,1},{1,0},{2,3},{3,2},{4,5},{5,4},{6,7},{7,6},{8,9},{9,8},{10,11... | collective-permute-start | bytes 73736 | tf_op jit(solution)/shard_map/ppermute | solution.py:675
  38.4 1.4 %collective-permute-done.16.refs_3_ = f32[48,128]{1,0:T(8,128)S(1)} collective-permute-done((f32[48,128]{1,0:T(8,128)S(1)}, f32[48,128]{1,0:T(8,128)S(1)}, u32[]{:S(2)}, u32[]{:S(2)}) %collective-permute-start.16) | collective-permute-done | bytes 24608 | tf_op jit(solution)/shard_map/ppermute | solution.py:675
  39.8 0.6 %collective-permute-done.15.refs_2_ = f32[48,128]{1,0:T(8,128)S(1)} collective-permute-done((f32[48,128]{1,0:T(8,128)S(1)}, f32[48,128]{1,0:T(8,128)S(1)}, u32[]{:S(2)}, u32[]{:S(2)}) %collective-permute-start.15) | collective-permute-done | bytes 24608 | tf_op jit(solution)/shard_map/ppermute | solution.py:675
  40.4 0.0 collective-permute-done.14.refs_1_
  40.4 0.0 collective-permute-done.18.refs_6_
  40.4 0.0 collective-permute-done.17.refs_5_
  40.4 0.0 copy-done.4
  40.5 0.0 copy-done.5
  40.5 0.0 copy-done.10
  40.5 1.4 %shard_map.136 = (f32[5,4,64,128]{3,2,1,0:T(8,128)}, f32[1]{0:T(128)}, f32[1]{0:T(128)}) custom-call(f32[48,128]{1,0:T(8,128)S(1)} %shard_map.135.refs_0_, f32[48,128]{1,0:T(8,128)S(1)} %collective-permute-done.14.refs_1_, f32[48,128]{1,0:T(8,128)S(1)} %collective-permute-done.15.refs_2_, f32[48,128]{1,0:T(8,128)S(1)} %collective-permute-done.16.refs_3_, ...), custom_call_target="tpu_custom_call" | custom-call | tf_op jit(solution)/shard_map/pallas_call | solution.py:127
  (13 shorter events, 0.1 us)
Async XLA Ops:
  0.6 1.1 %copy-start = (f32[1,5,4,64,128]{4,3,2,1,0:T(8,128)S(1)}, f32[1,5,4,64,128]{4,3,2,1,0:T(8,128)}, u32[]{:S(2)}) copy-start(f32[1,5,4,64,128]{4,3,2,1,0:T(8,128)} %param.11) | copy-start | bytes 1966084
  1.7 2.6 %copy-start.1 = (f32[5,4,64,128]{3,2,1,0:T(8,128)S(1)}, f32[5,4,64,128]{3,2,1,0:T(8,128)}, u32[]{:S(2)}) copy-start(f32[5,4,64,128]{3,2,1,0:T(8,128)} %source_ref.5) | copy-start | bytes 1966084
  1.7 6.4 %collective-permute-start = (f32[5,64,128]{2,1,0:T(8,128)S(1)}, f32[5,64,128]{2,1,0:T(8,128)S(1)}, u32[]{:S(2)}, u32[]{:S(2)}) collective-permute-start(f32[5,64,128]{2,1,0:T(8,128)S(1)} %get-tuple-element.24), channel_id=1, source_target_pairs={{0,1},{1,2},{2,3},{3,0},{4,5},{5,6},{6,7},{7,4},{8,9},{9,10},{10,1... | collective-permute-start | bytes 491528 | tf_op jit(solution)/shard_map/ppermute | solution.py:568
  2.3 6.9 %collective-permute-start.1 = (f32[5,64,128]{2,1,0:T(8,128)S(1)}, f32[5,64,128]{2,1,0:T(8,128)S(1)}, u32[]{:S(2)}, u32[]{:S(2)}) collective-permute-start(f32[5,64,128]{2,1,0:T(8,128)S(1)} %get-tuple-element.25), channel_id=1, source_target_pairs={{1,0},{2,1},{3,2},{0,3},{5,4},{6,5},{7,6},{4,7},{9,8},{10,9},{11,1... | collective-permute-start | bytes 491528 | tf_op jit(solution)/shard_map/ppermute | solution.py:568
  4.3 0.7 %copy-start.7 = (bf16[32,256]{1,0:T(8,128)(2,1)S(1)}, bf16[32,256]{1,0:T(8,128)(2,1)}, u32[]{:S(2)}) copy-start(bf16[32,256]{1,0:T(8,128)(2,1)} %constant.18.clone.table_ref) | copy-start | bytes 49156
  5.7 6.2 %collective-permute-start.2 = (f32[5,64,128]{2,1,0:T(8,128)S(1)}, f32[5,64,128]{2,1,0:T(8,128)S(1)}, u32[]{:S(2)}, u32[]{:S(2)}) collective-permute-start(f32[5,64,128]{2,1,0:T(8,128)S(1)} %get-tuple-element.28), channel_id=1, source_target_pairs={{0,1},{1,2},{2,3},{3,0},{4,5},{5,6},{6,7},{7,4},{8,9},{9,10},{10,1... | collective-permute-start | bytes 491528 | tf_op jit(solution)/shard_map/ppermute | solution.py:568
  6.3 6.0 %collective-permute-start.3 = (f32[5,64,128]{2,1,0:T(8,128)S(1)}, f32[5,64,128]{2,1,0:T(8,128)S(1)}, u32[]{:S(2)}, u32[]{:S(2)}) collective-permute-start(f32[5,64,128]{2,1,0:T(8,128)S(1)} %get-tuple-element.29), channel_id=1, source_target_pairs={{1,0},{2,1},{3,2},{0,3},{5,4},{6,5},{7,6},{4,7},{9,8},{10,9},{11,1... | collective-permute-start | bytes 491528 | tf_op jit(solution)/shard_map/ppermute | solution.py:568
  7.5 8.7 %collective-permute-start.4 = (f32[5,64,128]{2,1,0:T(8,128)S(1)}, f32[5,64,128]{2,1,0:T(8,128)S(1)}, u32[]{:S(2)}, u32[]{:S(2)}) collective-permute-start(f32[5,64,128]{2,1,0:T(8,128)S(1)} %get-tuple-element.34), channel_id=1, source_target_pairs={{0,1},{1,2},{2,3},{3,0},{4,5},{5,6},{6,7},{7,4},{8,9},{9,10},{10,1... | collective-permute-start | bytes 491528 | tf_op jit(solution)/shard_map/ppermute | solution.py:568
  8.1 8.1 %collective-permute-start.5 = (f32[5,64,128]{2,1,0:T(8,128)S(1)}, f32[5,64,128]{2,1,0:T(8,128)S(1)}, u32[]{:S(2)}, u32[]{:S(2)}) collective-permute-start(f32[5,64,128]{2,1,0:T(8,128)S(1)} %get-tuple-element.35), channel_id=1, source_target_pairs={{1,0},{2,1},{3,2},{0,3},{5,4},{6,5},{7,6},{4,7},{9,8},{10,9},{11,1... | collective-permute-start | bytes 491528 | tf_op jit(solution)/shard_map/ppermute | solution.py:568
  9.2 6.9 %collective-permute-start.6 = (f32[40,512]{1,0:T(8,128)S(1)}, f32[40,512]{1,0:T(8,128)S(1)}, u32[]{:S(2)}, u32[]{:S(2)}) collective-permute-start(f32[40,512]{1,0:T(8,128)S(1)} %get-tuple-element.36), channel_id=1, source_target_pairs={{4,0},{8,4},{12,8},{16,12},{20,16},{24,20},{28,24},{5,1},{9,5},{13... | collective-permute-start | bytes 245768 | tf_op jit(solution)/shard_map/ppermute | solution.py:612
  12.4 3.8 %copy-start.2 = (bf16[768,512]{1,0:T(8,128)(2,1)S(1)}, bf16[768,512]{1,0:T(8,128)(2,1)}, u32[]{:S(2)}) copy-start(bf16[768,512]{1,0:T(8,128)(2,1)} %constant.20.clone.low_ref) | copy-start | bytes 2359300
  12.4 3.8 %copy-start.3 = (bf16[768,512]{1,0:T(8,128)(2,1)S(1)}, bf16[768,512]{1,0:T(8,128)(2,1)}, u32[]{:S(2)}) copy-start(bf16[768,512]{1,0:T(8,128)(2,1)} %constant.19.clone.high_ref) | copy-start | bytes 2359300
  12.4 3.8 %copy-start.6 = (f32[4,2,4,128]{3,2,1,0:T(4,128)S(1)}, f32[4,2,4,128]{3,2,1,0:T(4,128)}, u32[]{:S(2)}) copy-start(f32[4,2,4,128]{3,2,1,0:T(4,128)} %constant.21.clone.phase_ref.refs_10_) | copy-start | bytes 49156
  12.4 3.8 %copy-start.8 = (bf16[32,256]{1,0:T(8,128)(2,1)S(1)}, bf16[32,256]{1,0:T(8,128)(2,1)}, u32[]{:S(2)}) copy-start(bf16[32,256]{1,0:T(8,128)(2,1)} %constant.18.clone.table_ref) | copy-start | bytes 49156
  17.2 2.3 %collective-permute-start.7 = (f32[40,128]{1,0:T(8,128)S(1)}, f32[40,128]{1,0:T(8,128)S(1)}, u32[]{:S(2)}, u32[]{:S(2)}) collective-permute-start(f32[40,128]{1,0:T(8,128)S(1)} %get-tuple-element.47), channel_id=1, source_target_pairs={{0,1},{1,0},{2,3},{3,2},{4,5},{5,4},{6,7},{7,6},{8,9},{9,8},{10,11... | collective-permute-start | bytes 61448 | tf_op jit(solution)/shard_map/ppermute | solution.py:646
  17.8 3.2 %collective-permute-start.9 = (f32[40,128]{1,0:T(8,128)S(1)}, f32[40,128]{1,0:T(8,128)S(1)}, u32[]{:S(2)}, u32[]{:S(2)}) collective-permute-start(f32[40,128]{1,0:T(8,128)S(1)} %get-tuple-element.48), channel_id=1, source_target_pairs={{0,3},{1,2},{2,1},{3,0},{4,7},{5,6},{6,5},{7,4},{8,11},{9,10},{10,... | collective-permute-start | bytes 61448 | tf_op jit(solution)/shard_map/ppermute | solution.py:646
  19.4 16.8 %copy-start.9 = (f32[4,2,8,128]{3,2,1,0:T(8,128)S(1)}, f32[4,2,8,128]{3,2,1,0:T(8,128)}, u32[]{:S(2)}) copy-start(f32[4,2,8,128]{3,2,1,0:T(8,128)} %constant.22.clone.symbol_ref) | copy-start | bytes 98308
  19.5 16.8 %copy-start.11 = (f32[8,128]{1,0:T(8,128)S(1)}, f32[8,128]{1,0:T(8,128)}, u32[]{:S(2)}) copy-start(f32[8,128]{1,0:T(8,128)} %constant.23.clone.share_ref) | copy-start | bytes 12292
  19.5 3.8 %collective-permute-start.8 = (f32[40,128]{1,0:T(8,128)S(1)}, f32[40,128]{1,0:T(8,128)S(1)}, u32[]{:S(2)}, u32[]{:S(2)}) collective-permute-start(f32[40,128]{1,0:T(8,128)S(1)} %get-tuple-element.49), channel_id=1, source_target_pairs={{0,2},{1,3},{2,0},{3,1},{4,6},{5,7},{6,4},{7,5},{8,10},{9,11},{10,... | collective-permute-start | bytes 61448 | tf_op jit(solution)/shard_map/ppermute | solution.py:646
  23.2 4.0 %collective-permute-start.10 = (f32[1,40,128]{2,1,0:T(8,128)S(1)}, f32[1,40,128]{2,1,0:T(8,128)S(1)}, u32[]{:S(2)}, u32[]{:S(2)}) collective-permute-start(f32[1,40,128]{2,1,0:T(8,128)S(1)} %get-tuple-element.44), channel_id=1, source_target_pairs={{0,4},{4,0},{8,12},{12,8},{16,20},{20,16},{24,28},{28,24},{1,5},{5... | collective-permute-start | bytes 61448 | tf_op jit(solution)/shard_map/ppermute | solution.py:662
  25.4 15.0 %copy-start.4 = (bf16[512,512]{1,0:T(8,128)(2,1)S(1)}, bf16[512,512]{1,0:T(8,128)(2,1)}, u32[]{:S(2)}) copy-start(bf16[512,512]{1,0:T(8,128)(2,1)} %constant.25.clone.refs_8_) | copy-start | bytes 1572868
  25.4 15.0 %copy-start.5 = (bf16[512,512]{1,0:T(8,128)(2,1)S(1)}, bf16[512,512]{1,0:T(8,128)(2,1)}, u32[]{:S(2)}) copy-start(bf16[512,512]{1,0:T(8,128)(2,1)} %constant.24.clone.refs_7_) | copy-start | bytes 1572868
  25.5 15.0 %collective-permute-start.18 = (f32[5,64,128]{2,1,0:T(8,128)S(1)}, f32[5,64,128]{2,1,0:T(8,128)S(1)}, u32[]{:S(2)}, u32[]{:S(2)}) collective-permute-start(f32[5,64,128]{2,1,0:T(8,128)S(1)} %get-tuple-element.45), channel_id=1, source_target_pairs={{1,0},{2,1},{3,2},{0,3},{5,4},{6,5},{7,6},{4,7},{9,8},{10,9},{11,1... | collective-permute-start | bytes 491528 | tf_op jit(solution)/shard_map/ppermute | solution.py:568
  25.5 14.9 %collective-permute-start.17 = (f32[5,64,128]{2,1,0:T(8,128)S(1)}, f32[5,64,128]{2,1,0:T(8,128)S(1)}, u32[]{:S(2)}, u32[]{:S(2)}) collective-permute-start(f32[5,64,128]{2,1,0:T(8,128)S(1)} %get-tuple-element.46), channel_id=1, source_target_pairs={{0,1},{1,2},{2,3},{3,0},{4,5},{5,6},{6,7},{7,4},{8,9},{9,10},{10,1... | collective-permute-start | bytes 491528 | tf_op jit(solution)/shard_map/ppermute | solution.py:568
  27.2 9.0 %collective-permute-start.13 = (f32[2,40,128]{2,1,0:T(8,128)S(1)}, f32[2,40,128]{2,1,0:T(8,128)S(1)}, u32[]{:S(2)}, u32[]{:S(2)}) collective-permute-start(f32[2,40,128]{2,1,0:T(8,128)S(1)} %pad_maximum_fusion), channel_id=1, source_target_pairs={{0,24},{4,28},{8,0},{12,4},{16,8},{20,12},{24,16},{28,20},{1,25},{... | collective-permute-start | bytes 122888 | tf_op jit(solution)/shard_map/ppermute | solution.py:662
  30.4 5.8 %collective-permute-start.12 = (f32[2,40,128]{2,1,0:T(8,128)S(1)}, f32[2,40,128]{2,1,0:T(8,128)S(1)}, u32[]{:S(2)}, u32[]{:S(2)}) collective-permute-start(f32[2,40,128]{2,1,0:T(8,128)S(1)} %pad_maximum_fusion), channel_id=1, source_target_pairs={{0,16},{4,20},{8,24},{12,28},{16,0},{20,4},{24,8},{28,12},{1,17},{... | collective-permute-start | bytes 122888 | tf_op jit(solution)/shard_map/ppermute | solution.py:662
  30.4 5.8 %collective-permute-start.11 = (f32[2,40,128]{2,1,0:T(8,128)S(1)}, f32[2,40,128]{2,1,0:T(8,128)S(1)}, u32[]{:S(2)}, u32[]{:S(2)}) collective-permute-start(f32[2,40,128]{2,1,0:T(8,128)S(1)} %pad_maximum_fusion), channel_id=1, source_target_pairs={{0,8},{4,12},{8,16},{12,20},{16,24},{20,28},{24,0},{28,4},{1,9},{5... | collective-permute-start | bytes 122888 | tf_op jit(solution)/shard_map/ppermute | solution.py:662
  36.3 4.2 %copy-start.10 = (bf16[48,128]{1,0:T(8,128)(2,1)S(1)}, bf16[48,128]{1,0:T(8,128)(2,1)}, u32[]{:S(2)}) copy-start(bf16[48,128]{1,0:T(8,128)(2,1)} %constant.26.clone.refs_9_) | copy-start | bytes 36868
  36.5 3.3 %collective-permute-start.16 = (f32[48,128]{1,0:T(8,128)S(1)}, f32[48,128]{1,0:T(8,128)S(1)}, u32[]{:S(2)}, u32[]{:S(2)}) collective-permute-start(f32[48,128]{1,0:T(8,128)S(1)} %shard_map.135.refs_0_), channel_id=1, source_target_pairs={{0,3},{1,2},{2,1},{3,0},{4,7},{5,6},{6,5},{7,4},{8,11},{9,10},{10,... | collective-permute-start | bytes 73736 | tf_op jit(solution)/shard_map/ppermute | solution.py:675
  36.5 3.9 %collective-permute-start.15 = (f32[48,128]{1,0:T(8,128)S(1)}, f32[48,128]{1,0:T(8,128)S(1)}, u32[]{:S(2)}, u32[]{:S(2)}) collective-permute-start(f32[48,128]{1,0:T(8,128)S(1)} %shard_map.135.refs_0_), channel_id=1, source_target_pairs={{0,2},{1,3},{2,0},{3,1},{4,6},{5,7},{6,4},{7,5},{8,10},{9,11},{10,... | collective-permute-start | bytes 73736 | tf_op jit(solution)/shard_map/ppermute | solution.py:675
  37.2 3.2 %collective-permute-start.14 = (f32[48,128]{1,0:T(8,128)S(1)}, f32[48,128]{1,0:T(8,128)S(1)}, u32[]{:S(2)}, u32[]{:S(2)}) collective-permute-start(f32[48,128]{1,0:T(8,128)S(1)} %shard_map.135.refs_0_), channel_id=1, source_target_pairs={{0,1},{1,0},{2,3},{3,2},{4,5},{5,4},{6,7},{7,6},{8,9},{9,8},{10,11... | collective-permute-start | bytes 73736 | tf_op jit(solution)/shard_map/ppermute | solution.py:675

commit v4 on v3

--- a/solution.py
+++ b/solution.py
@@ -447,15 +447,6 @@
         out_ref[step_between(place, group, width)] = turned
 
 
-def slot_of(moment, moment_id, slices):
-    slot, stride = 0, 1
-    for radix in radices(slices):
-        ours = lax.rem(moment // stride, radix)
-        slot = slot + lax.rem(ours + (radix - moment_id // stride % radix), radix) * stride
-        stride *= radix
-    return slot
-
-
 def coarse_kernel(jump_ref, symbol_ref, share_ref, out_ref, kept_ref):
     slices, lines, lanes = jump_ref.shape
     keep = share_ref.shape[0]
@@ -476,9 +467,8 @@
         sizes.append(jnp.sum(total * share, axis=0, keepdims=True))
         if moment_id == slices - 1:
             break
-        slot = slot_of(moment, moment_id, slices)
         for f in range(fields):
-            jump = jump_ref[slot, f * keep : (f + 1) * keep, :]
+            jump = jump_ref[moment_id, f * keep : (f + 1) * keep, :]
             value = jump + current[f][0]
             swapped = pltpu.roll(jump, lanes // 2, 1) + current[f][1]
             current[f] = (value * real + swapped * imag, swapped * real - value * imag)
@@ -568,16 +558,6 @@
     return lax.ppermute(up, "space", ups), lax.ppermute(down, "space", downs)
 
 
-def radices(count):
-    parts = []
-    while count % 4 == 0 and count > 4:
-        parts.append(4)
-        count //= 4
-    if count > 1:
-        parts.append(count)
-    return sorted(parts)
-
-
 def shards(starts, source):
     state_now = starts[0]
     fields, slab, rows, cols = state_now.shape
@@ -650,18 +630,7 @@
 
     below, above = halo(fine_outer[1], fine_outer[0])
 
-    jumps = jump[None]
-    stride = 1
-    for radix in radices(slices):
-        parts = [jumps]
-        for step in range(1, radix):
-            pairs = []
-            for i in range(slices):
-                digit = i // stride % radix
-                pairs.append((i, i + ((digit + step) % radix - digit) * stride))
-            parts.append(lax.ppermute(jumps, "tm", pairs))
-        jumps = jnp.concatenate(parts)
-        stride *= radix
+    jumps = lax.all_to_all(jnp.broadcast_to(jump, (slices, lines, lanes)), "tm", 0, 0, tiled=True)
 
     message = local_call(
         coarse_kernel,

time: 42.2 us -> 43 us (1.019)
  waiting for transfers between devices: 14.9 us -> 16.3 us
  starting transfers between devices: 18.9 us -> 17.6 us
  local copies, waits for them, and re-layouts: 1.89 us -> 2.55 us
    all_to_all x0 -> x1, waiting for transfers between devices: none -> 6.96 us  [shards(): lax.all_to_all(jnp.broadcast_to(jump, (slices, lines, lanes)), 'tm', 0, 0...]
    ppermute x4 -> x0, starting transfers between devices: 6.82 us -> none  [shards(): parts.append(lax.ppermute(jumps, 'tm', pairs))]
    all_to_all x0 -> x1, starting transfers between devices: none -> 5.57 us  [shards(): lax.all_to_all(jnp.broadcast_to(jump, (slices, lines, lanes)), 'tm', 0, 0...]
    ppermute x4 -> x0, waiting for transfers between devices: 5.56 us -> none  [shards(): parts.append(lax.ppermute(jumps, 'tm', pairs))]
    broadcast_in_dim x0 -> x1, local copies, waits for them, and re-layouts: none -> 0.68 us  [shards(): jnp.broadcast_to(jump, (slices, lines, lanes))]
    unnamed x27 -> x24, local copies, waits for them, and re-layouts: 1.85 us -> 1.84 us
  transfers between devices with their start and end apart: 19 -> 16, of which waited for: 9 -> 8; matrix products, arithmetic and copies ran while one was open for 0% -> 0% of each run, Pallas kernels for 7% -> 7%
where the time goes in v4:
time: 43 us; the launch traced here: 42.6 us
  starting transfers between devices  17.6 us (41%)
  waiting for transfers between devices  16.3 us (38%)
  Pallas kernels  5.41 us (13%)
  local copies, waits for them, and re-layouts  2.55 us (6%)
  between operations  0.77 us (2%)
    all_to_all x1, waiting for transfers between devices, shards(): lax.all_to_all(jnp.broadcast_to(jump, (slices, lines, lanes)), 'tm', 0, 0...  6.96 us
    ppermute x8, starting transfers between devices, halo(): return (lax.ppermute(up, 'space', ups), lax.ppermute(down, 'space', downs))  6.61 us
    all_to_all x1, starting transfers between devices, shards(): lax.all_to_all(jnp.broadcast_to(jump, (slices, lines, lanes)), 'tm', 0, 0...  5.57 us
    pallas_call x7, Pallas kernels, local_call(): pl.pallas_call(kernel, out_shape=out_shape, in_specs=specs, out_specs=out...  5.41 us
    ppermute x3, waiting for transfers between devices, shards(): lax.ppermute(waves[step], 'space', [(i, target_of(i, step, width)) for i...  3.74 us
    ppermute x1, waiting for transfers between devices, shards(): lax.ppermute(start_waves, 'tm', [(i + 1, i) for i in range(slices - 1)])  2.37 us
    ppermute x3, starting transfers between devices, shards(): lax.ppermute(waves[step], 'space', [(i, target_of(i, step, width)) for i...  2.27 us
    ppermute x3, waiting for transfers between devices, shards(): lax.ppermute(message, 'space', [(i, target_of(i, step, width)) for i in r...  2.03 us
  transfers between devices with their start and end apart: 16, of which 8 were waited for; matrix products, arithmetic and copies ran while one was open for 0% of the time, Pallas kernels for 7%

profile of v4, /device:TPU:0, one launch (start us, length us, event | category | flops | bytes accessed | tf_op | source)
XLA Modules:
  0.0 42.6 jit_solution(6282922333739470649)
XLA Ops:
  0.6 0.0 copy-start
  0.6 1.1 %copy-done = f32[1,5,4,64,128]{4,3,2,1,0:T(8,128)S(1)} copy-done((f32[1,5,4,64,128]{4,3,2,1,0:T(8,128)S(1)}, f32[1,5,4,64,128]{4,3,2,1,0:T(8,128)}, u32[]{:S(2)}) %copy-start) | copy-done | bytes 655384
  1.7 0.0 copy-start.1
  1.7 0.5 %collective-permute-start = (f32[5,64,128]{2,1,0:T(8,128)S(1)}, f32[5,64,128]{2,1,0:T(8,128)S(1)}, u32[]{:S(2)}, u32[]{:S(2)}) collective-permute-start(f32[5,64,128]{2,1,0:T(8,128)S(1)} %get-tuple-element.24), channel_id=1, source_target_pairs={{0,1},{1,2},{2,3},{3,0},{4,5},{5,6},{6,7},{7,4},{8,9},{9,10},{10,1... | collective-permute-start | bytes 491528 | tf_op jit(solution)/shard_map/ppermute | solution.py:558
  2.3 2.0 %collective-permute-start.1 = (f32[5,64,128]{2,1,0:T(8,128)S(1)}, f32[5,64,128]{2,1,0:T(8,128)S(1)}, u32[]{:S(2)}, u32[]{:S(2)}) collective-permute-start(f32[5,64,128]{2,1,0:T(8,128)S(1)} %get-tuple-element.25), channel_id=1, source_target_pairs={{1,0},{2,1},{3,2},{0,3},{5,4},{6,5},{7,6},{4,7},{9,8},{10,9},{11,1... | collective-permute-start | bytes 491528 | tf_op jit(solution)/shard_map/ppermute | solution.py:558
  4.3 0.0 copy-done.1
  4.3 0.0 copy-start.7
  4.3 0.7 %copy-done.7 = bf16[32,256]{1,0:T(8,128)(2,1)S(1)} copy-done((bf16[32,256]{1,0:T(8,128)(2,1)S(1)}, bf16[32,256]{1,0:T(8,128)(2,1)}, u32[]{:S(2)}) %copy-start.7) | copy-done | bytes 16408
  5.0 0.7 %shard_map.130 = (f32[5,4,64,128]{3,2,1,0:T(8,128)S(1)}, f32[40,512]{1,0:T(8,128)S(1)}, f32[5,64,128]{2,1,0:T(8,128)S(1)}, f32[5,64,128]{2,1,0:T(8,128)S(1)}, f3...) custom-call(f32[5,4,64,128]{3,2,1,0:T(8,128)S(1)} %bitcast.19, f32[5,4,64,128]{3,2,1,0:T(8,128)S(1)} %copy-done.1, ...), custom_call_target="tpu_custom_call" | custom-call | tf_op jit(solution)/shard_map/pallas_call | solution.py:127
  5.7 0.7 %collective-permute-start.2 = (f32[5,64,128]{2,1,0:T(8,128)S(1)}, f32[5,64,128]{2,1,0:T(8,128)S(1)}, u32[]{:S(2)}, u32[]{:S(2)}) collective-permute-start(f32[5,64,128]{2,1,0:T(8,128)S(1)} %get-tuple-element.28), channel_id=1, source_target_pairs={{0,1},{1,2},{2,3},{3,0},{4,5},{5,6},{6,7},{7,4},{8,9},{9,10},{10,1... | collective-permute-start | bytes 491528 | tf_op jit(solution)/shard_map/ppermute | solution.py:558
  6.3 1.1 %collective-permute-start.3 = (f32[5,64,128]{2,1,0:T(8,128)S(1)}, f32[5,64,128]{2,1,0:T(8,128)S(1)}, u32[]{:S(2)}, u32[]{:S(2)}) collective-permute-start(f32[5,64,128]{2,1,0:T(8,128)S(1)} %get-tuple-element.29), channel_id=1, source_target_pairs={{1,0},{2,1},{3,2},{0,3},{5,4},{6,5},{7,6},{4,7},{9,8},{10,9},{11,1... | collective-permute-start | bytes 491528 | tf_op jit(solution)/shard_map/ppermute | solution.py:558
  7.5 0.6 %collective-permute-start.4 = (f32[5,64,128]{2,1,0:T(8,128)S(1)}, f32[5,64,128]{2,1,0:T(8,128)S(1)}, u32[]{:S(2)}, u32[]{:S(2)}) collective-permute-start(f32[5,64,128]{2,1,0:T(8,128)S(1)} %get-tuple-element.34), channel_id=1, source_target_pairs={{0,1},{1,2},{2,3},{3,0},{4,5},{5,6},{6,7},{7,4},{8,9},{9,10},{10,1... | collective-permute-start | bytes 491528 | tf_op jit(solution)/shard_map/ppermute | solution.py:558
  8.1 0.0 collective-permute-done.below_ref
  8.1 1.1 %collective-permute-start.5 = (f32[5,64,128]{2,1,0:T(8,128)S(1)}, f32[5,64,128]{2,1,0:T(8,128)S(1)}, u32[]{:S(2)}, u32[]{:S(2)}) collective-permute-start(f32[5,64,128]{2,1,0:T(8,128)S(1)} %get-tuple-element.35), channel_id=1, source_target_pairs={{1,0},{2,1},{3,2},{0,3},{5,4},{6,5},{7,6},{4,7},{9,8},{10,9},{11,1... | collective-permute-start | bytes 491528 | tf_op jit(solution)/shard_map/ppermute | solution.py:558
  9.2 0.0 collective-permute-done.1.above_ref
  9.2 1.3 %collective-permute-start.6 = (f32[40,512]{1,0:T(8,128)S(1)}, f32[40,512]{1,0:T(8,128)S(1)}, u32[]{:S(2)}, u32[]{:S(2)}) collective-permute-start(f32[40,512]{1,0:T(8,128)S(1)} %get-tuple-element.36), channel_id=1, source_target_pairs={{4,0},{8,4},{12,8},{16,12},{20,16},{24,20},{28,24},{5,1},{9,5},{13... | collective-permute-start | bytes 245768 | tf_op jit(solution)/shard_map/ppermute | solution.py:592
  10.5 0.6 %shard_map.132 = (f32[5,4,64,128]{3,2,1,0:T(8,128)S(1)}, f32[5,4,64,128]{3,2,1,0:T(8,128)S(1)}) custom-call(f32[5,4,64,128]{3,2,1,0:T(8,128)S(1)} %bitcast.20, f32[5,4,64,128]{3,2,1,0:T(8,128)S(1)} %get-tuple-element.23.rate_ref, f32[5,4,64,128]{3,2,1,0:T(8,128)S(1)} %copy-done.1, f32[5,64,128]{2,1,0:T(8,128)S(1)} %collective-permute-done.below_ref, ...), custom_call_target="tpu_custom_call" | custom-call | tf_op jit(solution)/shard_map/pallas_call | solution.py:127
  11.2 0.7 %collective-permute-done.2.below_rate_ref = f32[5,64,128]{2,1,0:T(8,128)S(1)} collective-permute-done((f32[5,64,128]{2,1,0:T(8,128)S(1)}, f32[5,64,128]{2,1,0:T(8,128)S(1)}, u32[]{:S(2)}, u32[]{:S(2)}) %collective-permute-start.2) | collective-permute-done | bytes 163872 | tf_op jit(solution)/shard_map/ppermute | solution.py:558
  11.9 0.5 %collective-permute-done.3.above_rate_ref = f32[5,64,128]{2,1,0:T(8,128)S(1)} collective-permute-done((f32[5,64,128]{2,1,0:T(8,128)S(1)}, f32[5,64,128]{2,1,0:T(8,128)S(1)}, u32[]{:S(2)}, u32[]{:S(2)}) %collective-permute-start.3) | collective-permute-done | bytes 163872 | tf_op jit(solution)/shard_map/ppermute | solution.py:558
  12.4 0.0 copy-start.2
  12.4 0.0 copy-start.3
  12.4 0.0 copy-start.6
  12.4 0.0 copy-start.8
  12.4 1.4 %shard_map.133 = (f32[2,5,64,128]{3,2,1,0:T(8,128)S(1)}, f32[2,5,64,128]{3,2,1,0:T(8,128)S(1)}, f32[2,5,64,128]{3,2,1,0:T(8,128)S(1)}, f32[5,2,64,128]{3,2,1,0:T(8,128)S(1)}) custom-call(f32[5,4,64,128]{3,2,1,0:T(8,128)S(1)} %bitcast.21, f32[5,4,64,128]{3,2,1,0:T(8,128)S(1)} %get-tuple-element.26.second_ref, ...), custom_call_target="tpu_custom_call" | custom-call | tf_op jit(solution)/shard_map/pallas_call | solution.py:127
  13.8 2.4 %collective-permute-done.6.shifted_ref = f32[40,512]{1,0:T(8,128)S(1)} collective-permute-done((f32[40,512]{1,0:T(8,128)S(1)}, f32[40,512]{1,0:T(8,128)S(1)}, u32[]{:S(2)}, u32[]{:S(2)}) %collective-permute-start.6) | collective-permute-done | bytes 81952 | tf_op jit(solution)/shard_map/ppermute | solution.py:592
  16.1 0.0 collective-permute-done.4.below_ref
  16.2 0.0 collective-permute-done.5.above_ref
  16.2 0.0 copy-done.2
  16.2 0.0 copy-done.3
  16.2 0.0 copy-done.6
  16.2 0.0 copy-done.8
  16.2 1.0 %shard_map.134 = (f32[4,40,128]{2,1,0:T(8,128)S(1)}, f32[5,4,64,128]{3,2,1,0:T(8,128)S(1)}, f32[2,5,64,128]{3,2,1,0:T(8,128)S(1)}) custom-call(f32[5,4,64,128]{3,2,1,0:T(8,128)S(1)} %bitcast.22, f32[2,5,64,128]{3,2,1,0:T(8,128)S(1)} %get-tuple-element.30.base_ref, f32[2,5,64,128]{3,2,1,0:T(8,128)S(1)} %get-tuple-element.31.edge_rate_ref, ...), custom_call_target="tpu_custom_call" | custom-call | tf_op jit(solution)/shard_map/pallas_call | solution.py:127
  17.2 0.5 %collective-permute-start.7 = (f32[40,128]{1,0:T(8,128)S(1)}, f32[40,128]{1,0:T(8,128)S(1)}, u32[]{:S(2)}, u32[]{:S(2)}) collective-permute-start(f32[40,128]{1,0:T(8,128)S(1)} %get-tuple-element.45), channel_id=1, source_target_pairs={{0,1},{1,0},{2,3},{3,2},{4,5},{5,4},{6,7},{7,6},{8,9},{9,8},{10,11... | collective-permute-start | bytes 61448 | tf_op jit(solution)/shard_map/ppermute | solution.py:626
  17.8 1.7 %collective-permute-start.9 = (f32[40,128]{1,0:T(8,128)S(1)}, f32[40,128]{1,0:T(8,128)S(1)}, u32[]{:S(2)}, u32[]{:S(2)}) collective-permute-start(f32[40,128]{1,0:T(8,128)S(1)} %get-tuple-element.46), channel_id=1, source_target_pairs={{0,3},{1,2},{2,1},{3,0},{4,7},{5,6},{6,5},{7,4},{8,11},{9,10},{10,... | collective-permute-start | bytes 61448 | tf_op jit(solution)/shard_map/ppermute | solution.py:626
  19.4 0.0 collective-permute-start.8
  19.5 0.0 collective-permute-done.7
  19.5 1.5 %collective-permute-done.9 = f32[40,128]{1,0:T(8,128)S(1)} collective-permute-done((f32[40,128]{1,0:T(8,128)S(1)}, f32[40,128]{1,0:T(8,128)S(1)}, u32[]{:S(2)}, u32[]{:S(2)}) %collective-permute-start.9) | collective-permute-done | bytes 20512 | tf_op jit(solution)/shard_map/ppermute | solution.py:626
  21.0 2.3 %collective-permute-done.8 = f32[40,128]{1,0:T(8,128)S(1)} collective-permute-done((f32[40,128]{1,0:T(8,128)S(1)}, f32[40,128]{1,0:T(8,128)S(1)}, u32[]{:S(2)}, u32[]{:S(2)}) %collective-permute-start.8) | collective-permute-done | bytes 20512 | tf_op jit(solution)/shard_map/ppermute | solution.py:626
  23.2 0.7 %broadcast_in_dim.6 = f32[8,40,128]{2,1,0:T(8,128)} broadcast(f32[40,128]{1,0:T(8,128)S(1)} %fusion.1), dimensions={1,2} | broadcast | bytes 184320 | tf_op jit(solution)/shard_map/broadcast_in_dim | solution.py:633
  23.9 0.0 copy-start.9
  23.9 0.0 copy-start.11
  23.9 0.0 copy-start.5
  23.9 5.6 %all-to-all-start = ((f32[8,40,128]{2,1,0:T(8,128)}), f32[8,40,128]{2,1,0:T(8,128)S(1)}, u32[]{:S(2)}, u32[]{:S(2)}) async-start(f32[8,40,128]{2,1,0:T(8,128)} %broadcast_in_dim.6), calls=%async_computation | async-start | bytes 327680 | tf_op jit(solution)/shard_map/all_to_all | solution.py:633
  29.5 0.0 copy-start.4
  29.5 0.1 collective-permute-start.14
  29.6 0.0 copy-start.10
  29.6 0.5 %collective-permute-start.13 = (f32[5,64,128]{2,1,0:T(8,128)S(1)}, f32[5,64,128]{2,1,0:T(8,128)S(1)}, u32[]{:S(2)}, u32[]{:S(2)}) collective-permute-start(f32[5,64,128]{2,1,0:T(8,128)S(1)} %get-tuple-element.44), channel_id=1, source_target_pairs={{0,1},{1,2},{2,3},{3,0},{4,5},{5,6},{6,7},{7,4},{8,9},{9,10},{10,1... | collective-permute-start | bytes 491528 | tf_op jit(solution)/shard_map/ppermute | solution.py:558
  30.1 7.0 %all-to-all-done.jump_ref = f32[8,40,128]{2,1,0:T(8,128)S(1)} async-done(((f32[8,40,128]{2,1,0:T(8,128)}), f32[8,40,128]{2,1,0:T(8,128)S(1)}, u32[]{:S(2)}, u32[]{:S(2)}) %all-to-all-start) | async-done | bytes 163872 | tf_op jit(solution)/shard_map/all_to_all | solution.py:633
  37.1 0.0 copy-done.9
  37.1 0.0 copy-done.11
  37.1 0.2 shard_map.135.refs_0_
  37.3 0.0 collective-permute-start.12
  37.3 0.7 %collective-permute-start.11 = (f32[48,128]{1,0:T(8,128)S(1)}, f32[48,128]{1,0:T(8,128)S(1)}, u32[]{:S(2)}, u32[]{:S(2)}) collective-permute-start(f32[48,128]{1,0:T(8,128)S(1)} %shard_map.135.refs_0_), channel_id=1, source_target_pairs={{0,2},{1,3},{2,0},{3,1},{4,6},{5,7},{6,4},{7,5},{8,10},{9,11},{10,... | collective-permute-start | bytes 73736 | tf_op jit(solution)/shard_map/ppermute | solution.py:644
  37.9 1.2 %collective-permute-start.10 = (f32[48,128]{1,0:T(8,128)S(1)}, f32[48,128]{1,0:T(8,128)S(1)}, u32[]{:S(2)}, u32[]{:S(2)}) collective-permute-start(f32[48,128]{1,0:T(8,128)S(1)} %shard_map.135.refs_0_), channel_id=1, source_target_pairs={{0,1},{1,0},{2,3},{3,2},{4,5},{5,4},{6,7},{7,6},{8,9},{9,8},{10,11... | collective-permute-start | bytes 73736 | tf_op jit(solution)/shard_map/ppermute | solution.py:644
  39.1 0.0 collective-permute-done.14.refs_6_
  39.1 0.0 collective-permute-done.13.refs_5_
  39.1 1.4 %collective-permute-done.12.refs_3_ = f32[48,128]{1,0:T(8,128)S(1)} collective-permute-done((f32[48,128]{1,0:T(8,128)S(1)}, f32[48,128]{1,0:T(8,128)S(1)}, u32[]{:S(2)}, u32[]{:S(2)}) %collective-permute-start.12) | collective-permute-done | bytes 24608 | tf_op jit(solution)/shard_map/ppermute | solution.py:644
  40.5 0.6 %collective-permute-done.11.refs_2_ = f32[48,128]{1,0:T(8,128)S(1)} collective-permute-done((f32[48,128]{1,0:T(8,128)S(1)}, f32[48,128]{1,0:T(8,128)S(1)}, u32[]{:S(2)}, u32[]{:S(2)}) %collective-permute-start.11) | collective-permute-done | bytes 24608 | tf_op jit(solution)/shard_map/ppermute | solution.py:644
  41.2 0.0 collective-permute-done.10.refs_1_
  41.2 0.0 copy-done.5
  41.2 0.0 copy-done.4
  41.2 0.0 copy-done.10
  41.2 1.4 %shard_map.136 = (f32[5,4,64,128]{3,2,1,0:T(8,128)}, f32[1]{0:T(128)}, f32[1]{0:T(128)}) custom-call(f32[48,128]{1,0:T(8,128)S(1)} %shard_map.135.refs_0_, f32[48,128]{1,0:T(8,128)S(1)} %collective-permute-done.10.refs_1_, f32[48,128]{1,0:T(8,128)S(1)} %collective-permute-done.11.refs_2_, f32[48,128]{1,0:T(8,128)S(1)} %collective-permute-done.12.refs_3_, ...), custom_call_target="tpu_custom_call" | custom-call | tf_op jit(solution)/shard_map/pallas_call | solution.py:127
  (4 shorter events, 0.1 us)
Async XLA Ops:
  0.6 1.1 %copy-start = (f32[1,5,4,64,128]{4,3,2,1,0:T(8,128)S(1)}, f32[1,5,4,64,128]{4,3,2,1,0:T(8,128)}, u32[]{:S(2)}) copy-start(f32[1,5,4,64,128]{4,3,2,1,0:T(8,128)} %param.11) | copy-start | bytes 1966084
  1.7 2.6 %copy-start.1 = (f32[5,4,64,128]{3,2,1,0:T(8,128)S(1)}, f32[5,4,64,128]{3,2,1,0:T(8,128)}, u32[]{:S(2)}) copy-start(f32[5,4,64,128]{3,2,1,0:T(8,128)} %source_ref.5) | copy-start | bytes 1966084
  1.7 6.4 %collective-permute-start = (f32[5,64,128]{2,1,0:T(8,128)S(1)}, f32[5,64,128]{2,1,0:T(8,128)S(1)}, u32[]{:S(2)}, u32[]{:S(2)}) collective-permute-start(f32[5,64,128]{2,1,0:T(8,128)S(1)} %get-tuple-element.24), channel_id=1, source_target_pairs={{0,1},{1,2},{2,3},{3,0},{4,5},{5,6},{6,7},{7,4},{8,9},{9,10},{10,1... | collective-permute-start | bytes 491528 | tf_op jit(solution)/shard_map/ppermute | solution.py:558
  2.3 6.9 %collective-permute-start.1 = (f32[5,64,128]{2,1,0:T(8,128)S(1)}, f32[5,64,128]{2,1,0:T(8,128)S(1)}, u32[]{:S(2)}, u32[]{:S(2)}) collective-permute-start(f32[5,64,128]{2,1,0:T(8,128)S(1)} %get-tuple-element.25), channel_id=1, source_target_pairs={{1,0},{2,1},{3,2},{0,3},{5,4},{6,5},{7,6},{4,7},{9,8},{10,9},{11,1... | collective-permute-start | bytes 491528 | tf_op jit(solution)/shard_map/ppermute | solution.py:558
  4.3 0.7 %copy-start.7 = (bf16[32,256]{1,0:T(8,128)(2,1)S(1)}, bf16[32,256]{1,0:T(8,128)(2,1)}, u32[]{:S(2)}) copy-start(bf16[32,256]{1,0:T(8,128)(2,1)} %constant.18.clone.table_ref) | copy-start | bytes 49156
  5.7 6.2 %collective-permute-start.2 = (f32[5,64,128]{2,1,0:T(8,128)S(1)}, f32[5,64,128]{2,1,0:T(8,128)S(1)}, u32[]{:S(2)}, u32[]{:S(2)}) collective-permute-start(f32[5,64,128]{2,1,0:T(8,128)S(1)} %get-tuple-element.28), channel_id=1, source_target_pairs={{0,1},{1,2},{2,3},{3,0},{4,5},{5,6},{6,7},{7,4},{8,9},{9,10},{10,1... | collective-permute-start | bytes 491528 | tf_op jit(solution)/shard_map/ppermute | solution.py:558
  6.3 6.0 %collective-permute-start.3 = (f32[5,64,128]{2,1,0:T(8,128)S(1)}, f32[5,64,128]{2,1,0:T(8,128)S(1)}, u32[]{:S(2)}, u32[]{:S(2)}) collective-permute-start(f32[5,64,128]{2,1,0:T(8,128)S(1)} %get-tuple-element.29), channel_id=1, source_target_pairs={{1,0},{2,1},{3,2},{0,3},{5,4},{6,5},{7,6},{4,7},{9,8},{10,9},{11,1... | collective-permute-start | bytes 491528 | tf_op jit(solution)/shard_map/ppermute | solution.py:558
  7.5 8.7 %collective-permute-start.4 = (f32[5,64,128]{2,1,0:T(8,128)S(1)}, f32[5,64,128]{2,1,0:T(8,128)S(1)}, u32[]{:S(2)}, u32[]{:S(2)}) collective-permute-start(f32[5,64,128]{2,1,0:T(8,128)S(1)} %get-tuple-element.34), channel_id=1, source_target_pairs={{0,1},{1,2},{2,3},{3,0},{4,5},{5,6},{6,7},{7,4},{8,9},{9,10},{10,1... | collective-permute-start | bytes 491528 | tf_op jit(solution)/shard_map/ppermute | solution.py:558
  8.1 8.1 %collective-permute-start.5 = (f32[5,64,128]{2,1,0:T(8,128)S(1)}, f32[5,64,128]{2,1,0:T(8,128)S(1)}, u32[]{:S(2)}, u32[]{:S(2)}) collective-permute-start(f32[5,64,128]{2,1,0:T(8,128)S(1)} %get-tuple-element.35), channel_id=1, source_target_pairs={{1,0},{2,1},{3,2},{0,3},{5,4},{6,5},{7,6},{4,7},{9,8},{10,9},{11,1... | collective-permute-start | bytes 491528 | tf_op jit(solution)/shard_map/ppermute | solution.py:558
  9.2 6.9 %collective-permute-start.6 = (f32[40,512]{1,0:T(8,128)S(1)}, f32[40,512]{1,0:T(8,128)S(1)}, u32[]{:S(2)}, u32[]{:S(2)}) collective-permute-start(f32[40,512]{1,0:T(8,128)S(1)} %get-tuple-element.36), channel_id=1, source_target_pairs={{4,0},{8,4},{12,8},{16,12},{20,16},{24,20},{28,24},{5,1},{9,5},{13... | collective-permute-start | bytes 245768 | tf_op jit(solution)/shard_map/ppermute | solution.py:592
  12.4 3.8 %copy-start.2 = (bf16[768,512]{1,0:T(8,128)(2,1)S(1)}, bf16[768,512]{1,0:T(8,128)(2,1)}, u32[]{:S(2)}) copy-start(bf16[768,512]{1,0:T(8,128)(2,1)} %constant.20.clone.low_ref) | copy-start | bytes 2359300
  12.4 3.8 %copy-start.3 = (bf16[768,512]{1,0:T(8,128)(2,1)S(1)}, bf16[768,512]{1,0:T(8,128)(2,1)}, u32[]{:S(2)}) copy-start(bf16[768,512]{1,0:T(8,128)(2,1)} %constant.19.clone.high_ref) | copy-start | bytes 2359300
  12.4 3.8 %copy-start.6 = (f32[4,2,4,128]{3,2,1,0:T(4,128)S(1)}, f32[4,2,4,128]{3,2,1,0:T(4,128)}, u32[]{:S(2)}) copy-start(f32[4,2,4,128]{3,2,1,0:T(4,128)} %constant.21.clone.phase_ref.refs_10_) | copy-start | bytes 49156
  12.4 3.8 %copy-start.8 = (bf16[32,256]{1,0:T(8,128)(2,1)S(1)}, bf16[32,256]{1,0:T(8,128)(2,1)}, u32[]{:S(2)}) copy-start(bf16[32,256]{1,0:T(8,128)(2,1)} %constant.18.clone.table_ref) | copy-start | bytes 49156
  17.2 2.3 %collective-permute-start.7 = (f32[40,128]{1,0:T(8,128)S(1)}, f32[40,128]{1,0:T(8,128)S(1)}, u32[]{:S(2)}, u32[]{:S(2)}) collective-permute-start(f32[40,128]{1,0:T(8,128)S(1)} %get-tuple-element.45), channel_id=1, source_target_pairs={{0,1},{1,0},{2,3},{3,2},{4,5},{5,4},{6,7},{7,6},{8,9},{9,8},{10,11... | collective-permute-start | bytes 61448 | tf_op jit(solution)/shard_map/ppermute | solution.py:626
  17.8 3.2 %collective-permute-start.9 = (f32[40,128]{1,0:T(8,128)S(1)}, f32[40,128]{1,0:T(8,128)S(1)}, u32[]{:S(2)}, u32[]{:S(2)}) collective-permute-start(f32[40,128]{1,0:T(8,128)S(1)} %get-tuple-element.46), channel_id=1, source_target_pairs={{0,3},{1,2},{2,1},{3,0},{4,7},{5,6},{6,5},{7,4},{8,11},{9,10},{10,... | collective-permute-start | bytes 61448 | tf_op jit(solution)/shard_map/ppermute | solution.py:626
  19.4 3.8 %collective-permute-start.8 = (f32[40,128]{1,0:T(8,128)S(1)}, f32[40,128]{1,0:T(8,128)S(1)}, u32[]{:S(2)}, u32[]{:S(2)}) collective-permute-start(f32[40,128]{1,0:T(8,128)S(1)} %get-tuple-element.47), channel_id=1, source_target_pairs={{0,2},{1,3},{2,0},{3,1},{4,6},{5,7},{6,4},{7,5},{8,10},{9,11},{10,... | collective-permute-start | bytes 61448 | tf_op jit(solution)/shard_map/ppermute | solution.py:626
  23.9 13.1 %copy-start.9 = (f32[4,2,8,128]{3,2,1,0:T(8,128)S(1)}, f32[4,2,8,128]{3,2,1,0:T(8,128)}, u32[]{:S(2)}) copy-start(f32[4,2,8,128]{3,2,1,0:T(8,128)} %constant.22.clone.symbol_ref) | copy-start | bytes 98308
  23.9 13.1 %copy-start.11 = (f32[8,128]{1,0:T(8,128)S(1)}, f32[8,128]{1,0:T(8,128)}, u32[]{:S(2)}) copy-start(f32[8,128]{1,0:T(8,128)} %constant.23.clone.share_ref) | copy-start | bytes 12292
  23.9 17.2 %copy-start.5 = (bf16[512,512]{1,0:T(8,128)(2,1)S(1)}, bf16[512,512]{1,0:T(8,128)(2,1)}, u32[]{:S(2)}) copy-start(bf16[512,512]{1,0:T(8,128)(2,1)} %constant.24.clone.refs_7_) | copy-start | bytes 1572868
  23.9 13.1 %all-to-all-start = ((f32[8,40,128]{2,1,0:T(8,128)}), f32[8,40,128]{2,1,0:T(8,128)S(1)}, u32[]{:S(2)}, u32[]{:S(2)}) async-start(f32[8,40,128]{2,1,0:T(8,128)} %broadcast_in_dim.6), calls=%async_computation | async-start | bytes 327680 | tf_op jit(solution)/shard_map/all_to_all | solution.py:633
  29.5 11.7 %copy-start.4 = (bf16[512,512]{1,0:T(8,128)(2,1)S(1)}, bf16[512,512]{1,0:T(8,128)(2,1)}, u32[]{:S(2)}) copy-start(bf16[512,512]{1,0:T(8,128)(2,1)} %constant.25.clone.refs_8_) | copy-start | bytes 1572868
  29.5 9.6 %collective-permute-start.14 = (f32[5,64,128]{2,1,0:T(8,128)S(1)}, f32[5,64,128]{2,1,0:T(8,128)S(1)}, u32[]{:S(2)}, u32[]{:S(2)}) collective-permute-start(f32[5,64,128]{2,1,0:T(8,128)S(1)} %get-tuple-element.43), channel_id=1, source_target_pairs={{1,0},{2,1},{3,2},{0,3},{5,4},{6,5},{7,6},{4,7},{9,8},{10,9},{11,1... | collective-permute-start | bytes 491528 | tf_op jit(solution)/shard_map/ppermute | solution.py:558
  29.6 11.6 %copy-start.10 = (bf16[48,128]{1,0:T(8,128)(2,1)S(1)}, bf16[48,128]{1,0:T(8,128)(2,1)}, u32[]{:S(2)}) copy-start(bf16[48,128]{1,0:T(8,128)(2,1)} %constant.26.clone.refs_9_) | copy-start | bytes 36868
  29.6 9.5 %collective-permute-start.13 = (f32[5,64,128]{2,1,0:T(8,128)S(1)}, f32[5,64,128]{2,1,0:T(8,128)S(1)}, u32[]{:S(2)}, u32[]{:S(2)}) collective-permute-start(f32[5,64,128]{2,1,0:T(8,128)S(1)} %get-tuple-element.44), channel_id=1, source_target_pairs={{0,1},{1,2},{2,3},{3,0},{4,5},{5,6},{6,7},{7,4},{8,9},{9,10},{10,1... | collective-permute-start | bytes 491528 | tf_op jit(solution)/shard_map/ppermute | solution.py:558
  37.3 3.3 %collective-permute-start.12 = (f32[48,128]{1,0:T(8,128)S(1)}, f32[48,128]{1,0:T(8,128)S(1)}, u32[]{:S(2)}, u32[]{:S(2)}) collective-permute-start(f32[48,128]{1,0:T(8,128)S(1)} %shard_map.135.refs_0_), channel_id=1, source_target_pairs={{0,3},{1,2},{2,1},{3,0},{4,7},{5,6},{6,5},{7,4},{8,11},{9,10},{10,... | collective-permute-start | bytes 73736 | tf_op jit(solution)/shard_map/ppermute | solution.py:644
  37.3 3.9 %collective-permute-start.11 = (f32[48,128]{1,0:T(8,128)S(1)}, f32[48,128]{1,0:T(8,128)S(1)}, u32[]{:S(2)}, u32[]{:S(2)}) collective-permute-start(f32[48,128]{1,0:T(8,128)S(1)} %shard_map.135.refs_0_), channel_id=1, source_target_pairs={{0,2},{1,3},{2,0},{3,1},{4,6},{5,7},{6,4},{7,5},{8,10},{9,11},{10,... | collective-permute-start | bytes 73736 | tf_op jit(solution)/shard_map/ppermute | solution.py:644
  37.9 3.2 %collective-permute-start.10 = (f32[48,128]{1,0:T(8,128)S(1)}, f32[48,128]{1,0:T(8,128)S(1)}, u32[]{:S(2)}, u32[]{:S(2)}) collective-permute-start(f32[48,128]{1,0:T(8,128)S(1)} %shard_map.135.refs_0_), channel_id=1, source_target_pairs={{0,1},{1,0},{2,3},{3,2},{4,5},{5,4},{6,7},{7,6},{8,9},{9,8},{10,11... | collective-permute-start | bytes 73736 | tf_op jit(solution)/shard_map/ppermute | solution.py:644

commit v5 on v4

--- a/solution.py
+++ b/solution.py
@@ -117,7 +117,9 @@
 in_scalars = pl.BlockSpec(memory_space=pltpu.SMEM)
 
 
-def local_call(kernel, out_shape, operands, scratch=(), places=None, out_specs=None):
+def local_call(
+    kernel, out_shape, operands, scratch=(), places=None, out_specs=None, aliases=None
+):
     specs = [in_scalars if operand.dtype == jnp.int32 else on_chip for operand in operands]
     for index, spec in (places or {}).items():
         specs[index] = spec
@@ -130,6 +132,7 @@
         in_specs=specs,
         out_specs=out_specs,
         scratch_shapes=list(scratch),
+        input_output_aliases=aliases or {},
         compiler_params=pltpu.CompilerParams(vmem_limit_bytes=16 * 1024 * 1024),
     )(*operands)
 
@@ -481,6 +484,26 @@
     out_ref[lines : lines + slices, :] = jnp.broadcast_to(sums, (slices, lanes))
 
 
+def uncorrected_kernel(fine_ref, below_ref, above_ref, ends_ref, held_ref, sems):
+    fields, slab = fine_ref.shape[:2]
+
+    @pl.when(lax.axis_index("tm") == 0)
+    def _():
+        copies = []
+        for f in range(fields):
+            for layer in range(slab):
+                value = fine_ref[f, layer]
+                if layer == 0:
+                    value = value + below_ref[f]
+                if layer == slab - 1:
+                    value = value + above_ref[f]
+                held_ref[f, layer] = value
+            copies.append(pltpu.make_async_copy(held_ref.at[f], ends_ref.at[f], sems.at[f]))
+            copies[-1].start()
+        for copy in copies:
+            copy.wait()
+
+
 def inverse_kernel(*refs, width, scales):
     block_refs = refs[:width]
     (
@@ -491,6 +514,7 @@
         low_ref,
         table_ref,
         phase_ref,
+        _,
         ends_ref,
         slice_ref,
         total_ref,
@@ -505,49 +529,57 @@
     moment = lax.axis_index("tm")
     lines, lanes = order_ref.shape[1:]
     keep = lines // fields
-    sums = None
-    for step in range(width):
-        group = source_of(place, step, width)
-        block = block_refs[step][:lines, :]
-        order_ref[group] = (
-            block * phase_ref[place, 0, group, :][None, :]
-            - pltpu.roll(block, lanes // 2, 1) * phase_ref[place, 1, group, :][None, :]
-        )
-        part = block_refs[step][lines:, :]
-        sums = part if sums is None else sums + part
-    left = jnp.concatenate([order_ref[group] for group in range(width)], axis=1)
-    waves = three_pass(left, high_ref[...], low_ref[...])
-    count = slab * rows
-    copies = []
-    for f in range(fields):
-        both = jnp.concatenate(
-            [waves[f * keep : (f + 1) * keep, :count], waves[f * keep : (f + 1) * keep, count:]]
-        )
-        high, low = split(both)
-        change = lax.dot_general(
-            jnp.concatenate([high, low, high]),
-            table_ref[...],
-            (((0,), (0,)), ((), ())),
-            preferred_element_type=jnp.float32,
-        ).reshape(slab, rows, cols)
-        for layer in range(slab):
-            value = fine_ref[f, layer] + change[layer]
-            if layer == 0:
-                value = value + below_ref[f]
-            if layer == slab - 1:
-                value = value + above_ref[f]
-            held_ref[f, layer] = value
-        copies.append(pltpu.make_async_copy(held_ref.at[f], ends_ref.at[f], sems.at[f]))
-        copies[-1].start()
+
+    sums = block_refs[0][lines:, :]
+    for step in range(1, width):
+        sums = sums + block_refs[step][lines:, :]
     line = lax.broadcasted_iota(jnp.int32, sums.shape, 0)
     own = jnp.sum(jnp.where(line == moment, sums, 0.0), axis=0, keepdims=True)
     whole = jnp.sum(sums, axis=0, keepdims=True)
     norm_refs[0, 0] = jnp.sqrt(own * scales[0] + epsilon)[0, 0]
     norm_refs[1, 0] = jnp.sqrt(whole * scales[1] + epsilon)[0, 0]
-    for side, out_ref in enumerate((slice_ref, total_ref)):
-        copies.append(pltpu.make_async_copy(norm_refs.at[side], out_ref, norm_sems.at[side]))
-        copies[-1].start()
-    for copy in copies:
+    norms = [
+        pltpu.make_async_copy(norm_refs.at[side], out_ref, norm_sems.at[side])
+        for side, out_ref in enumerate((slice_ref, total_ref))
+    ]
+    for copy in norms:
+        copy.start()
+
+    @pl.when(moment != 0)
+    def _():
+        for step in range(width):
+            group = source_of(place, step, width)
+            block = block_refs[step][:lines, :]
+            order_ref[group] = (
+                block * phase_ref[place, 0, group, :][None, :]
+                - pltpu.roll(block, lanes // 2, 1) * phase_ref[place, 1, group, :][None, :]
+            )
+        left = jnp.concatenate([order_ref[group] for group in range(width)], axis=1)
+        waves = three_pass(left, high_ref[...], low_ref[...])
+        count = slab * rows
+        copies = []
+        for f in range(fields):
+            own_waves = waves[f * keep : (f + 1) * keep]
+            high, low = split(jnp.concatenate([own_waves[:, :count], own_waves[:, count:]]))
+            change = lax.dot_general(
+                jnp.concatenate([high, low, high]),
+                table_ref[...],
+                (((0,), (0,)), ((), ())),
+                preferred_element_type=jnp.float32,
+            ).reshape(slab, rows, cols)
+            for layer in range(slab):
+                value = fine_ref[f, layer] + change[layer]
+                if layer == 0:
+                    value = value + below_ref[f]
+                if layer == slab - 1:
+                    value = value + above_ref[f]
+                held_ref[f, layer] = value
+            copies.append(pltpu.make_async_copy(held_ref.at[f], ends_ref.at[f], sems.at[f]))
+            copies[-1].start()
+        for copy in copies:
+            copy.wait()
+
+    for copy in norms:
         copy.wait()
 
 
@@ -640,9 +672,18 @@
     )
     blocks = [message]
     for step in range(1, width):
-        blocks.append(
-            lax.ppermute(message, "space", [(i, target_of(i, step, width)) for i in range(width)])
+        block = lax.ppermute(
+            message, "space", [(i, target_of(i, step, width)) for i in range(width)]
         )
+        blocks.append(block)
+    whole_slab = pltpu.VMEM((fields, slab, rows, cols), real)
+    ends = local_call(
+        uncorrected_kernel,
+        jax.ShapeDtypeStruct((fields, slab, rows, cols), real),
+        [fine_inner, below, above],
+        [whole_slab, pltpu.SemaphoreType.DMA((fields,))],
+        out_specs=off_chip,
+    )
     cells = fields * depth * rows * cols
     ends, slice_norm, total_norm = local_call(
         functools.partial(
@@ -661,15 +702,18 @@
             *tables["yzinverse"],
             tables["xinverse"],
             tables["phase"],
+            ends,
         ],
         [
             pltpu.VMEM((width, lines, lanes), real),
-            pltpu.VMEM((fields, slab, rows, cols), real),
+            whole_slab,
             pltpu.SMEM((2, 1), real),
             pltpu.SemaphoreType.DMA((fields,)),
             pltpu.SemaphoreType.DMA((2,)),
         ],
+        places={width + 7: off_chip},
         out_specs=(off_chip, off_chip, off_chip),
+        aliases={width + 7: 0},
     )
     return ends[None], slice_norm, total_norm
 

time: 43 us -> 42 us (0.977)
  waiting for transfers between devices: 16.3 us -> 15.4 us
    ppermute x3, waiting for transfers between devices: 2.03 us -> 1.1 us  [shards(): lax.ppermute(message, 'space', [(i, target_of(i, step, width)) for i in r...]
    pallas_call x7 -> x8, Pallas kernels: 5.41 us -> 5.51 us  [local_call(): pl.pallas_call(kernel, out_shape=out_shape, in_specs=specs, out_specs=out...]
  transfers between devices with their start and end apart: 16 -> 16, of which waited for: 8 -> 8; matrix products, arithmetic and copies ran while one was open for 0% -> 0% of each run, Pallas kernels for 7% -> 9%
where the time goes in v5:
time: 42 us; the launch traced here: 41.7 us
  starting transfers between devices  17.5 us (42%)
  waiting for transfers between devices  15.4 us (37%)
  Pallas kernels  5.51 us (13%)
  local copies, waits for them, and re-layouts  2.55 us (6%)
  between operations  0.8 us (2%)
    all_to_all x1, waiting for transfers between devices, shards(): lax.all_to_all(jnp.broadcast_to(jump, (slices, lines, lanes)), 'tm', 0, 0...  6.95 us
    ppermute x8, starting transfers between devices, halo(): return (lax.ppermute(up, 'space', ups), lax.ppermute(down, 'space', downs))  6.62 us
    pallas_call x8, Pallas kernels, local_call(): pl.pallas_call(kernel, out_shape=out_shape, in_specs=specs, out_specs=out...  5.51 us
    all_to_all x1, starting transfers between devices, shards(): lax.all_to_all(jnp.broadcast_to(jump, (slices, lines, lanes)), 'tm', 0, 0...  5.44 us
    ppermute x3, waiting for transfers between devices, shards(): lax.ppermute(waves[step], 'space', [(i, target_of(i, step, width)) for i...  3.74 us
    ppermute x1, waiting for transfers between devices, shards(): lax.ppermute(start_waves, 'tm', [(i + 1, i) for i in range(slices - 1)])  2.37 us
    ppermute x3, starting transfers between devices, shards(): lax.ppermute(waves[step], 'space', [(i, target_of(i, step, width)) for i...  2.27 us
    ppermute x3, starting transfers between devices, shards(): lax.ppermute(message, 'space', [(i, target_of(i, step, width)) for i in r...  1.86 us
  transfers between devices with their start and end apart: 16, of which 8 were waited for; matrix products, arithmetic and copies ran while one was open for 0% of the time, Pallas kernels for 9%

profile of v5, /device:TPU:0, one launch (start us, length us, event | category | flops | bytes accessed | tf_op | source)
XLA Modules:
  0.0 41.7 jit_solution(341869887167183105)
XLA Ops:
  0.6 0.0 copy-start
  0.6 1.1 %copy-done = f32[1,5,4,64,128]{4,3,2,1,0:T(8,128)S(1)} copy-done((f32[1,5,4,64,128]{4,3,2,1,0:T(8,128)S(1)}, f32[1,5,4,64,128]{4,3,2,1,0:T(8,128)}, u32[]{:S(2)}) %copy-start) | copy-done | bytes 655384
  1.7 0.0 copy-start.1
  1.7 0.5 %collective-permute-start = (f32[5,64,128]{2,1,0:T(8,128)S(1)}, f32[5,64,128]{2,1,0:T(8,128)S(1)}, u32[]{:S(2)}, u32[]{:S(2)}) collective-permute-start(f32[5,64,128]{2,1,0:T(8,128)S(1)} %get-tuple-element.24), channel_id=1, source_target_pairs={{0,1},{1,2},{2,3},{3,0},{4,5},{5,6},{6,7},{7,4},{8,9},{9,10},{10,1... | collective-permute-start | bytes 491528 | tf_op jit(solution)/shard_map/ppermute | solution.py:590
  2.3 2.0 %collective-permute-start.1 = (f32[5,64,128]{2,1,0:T(8,128)S(1)}, f32[5,64,128]{2,1,0:T(8,128)S(1)}, u32[]{:S(2)}, u32[]{:S(2)}) collective-permute-start(f32[5,64,128]{2,1,0:T(8,128)S(1)} %get-tuple-element.25), channel_id=1, source_target_pairs={{1,0},{2,1},{3,2},{0,3},{5,4},{6,5},{7,6},{4,7},{9,8},{10,9},{11,1... | collective-permute-start | bytes 491528 | tf_op jit(solution)/shard_map/ppermute | solution.py:590
  4.3 0.0 copy-done.1
  4.3 0.0 copy-start.7
  4.3 0.7 %copy-done.7 = bf16[32,256]{1,0:T(8,128)(2,1)S(1)} copy-done((bf16[32,256]{1,0:T(8,128)(2,1)S(1)}, bf16[32,256]{1,0:T(8,128)(2,1)}, u32[]{:S(2)}) %copy-start.7) | copy-done | bytes 16408
  5.0 0.7 %shard_map.130 = (f32[5,4,64,128]{3,2,1,0:T(8,128)S(1)}, f32[40,512]{1,0:T(8,128)S(1)}, f32[5,64,128]{2,1,0:T(8,128)S(1)}, f32[5,64,128]{2,1,0:T(8,128)S(1)}, f3...) custom-call(f32[5,4,64,128]{3,2,1,0:T(8,128)S(1)} %bitcast.19, f32[5,4,64,128]{3,2,1,0:T(8,128)S(1)} %copy-done.1, ...), custom_call_target="tpu_custom_call" | custom-call | tf_op jit(solution)/shard_map/pallas_call | solution.py:129
  5.7 0.7 %collective-permute-start.2 = (f32[5,64,128]{2,1,0:T(8,128)S(1)}, f32[5,64,128]{2,1,0:T(8,128)S(1)}, u32[]{:S(2)}, u32[]{:S(2)}) collective-permute-start(f32[5,64,128]{2,1,0:T(8,128)S(1)} %get-tuple-element.28), channel_id=1, source_target_pairs={{0,1},{1,2},{2,3},{3,0},{4,5},{5,6},{6,7},{7,4},{8,9},{9,10},{10,1... | collective-permute-start | bytes 491528 | tf_op jit(solution)/shard_map/ppermute | solution.py:590
  6.3 1.1 %collective-permute-start.3 = (f32[5,64,128]{2,1,0:T(8,128)S(1)}, f32[5,64,128]{2,1,0:T(8,128)S(1)}, u32[]{:S(2)}, u32[]{:S(2)}) collective-permute-start(f32[5,64,128]{2,1,0:T(8,128)S(1)} %get-tuple-element.29), channel_id=1, source_target_pairs={{1,0},{2,1},{3,2},{0,3},{5,4},{6,5},{7,6},{4,7},{9,8},{10,9},{11,1... | collective-permute-start | bytes 491528 | tf_op jit(solution)/shard_map/ppermute | solution.py:590
  7.5 0.6 %collective-permute-start.4 = (f32[5,64,128]{2,1,0:T(8,128)S(1)}, f32[5,64,128]{2,1,0:T(8,128)S(1)}, u32[]{:S(2)}, u32[]{:S(2)}) collective-permute-start(f32[5,64,128]{2,1,0:T(8,128)S(1)} %get-tuple-element.34), channel_id=1, source_target_pairs={{0,1},{1,2},{2,3},{3,0},{4,5},{5,6},{6,7},{7,4},{8,9},{9,10},{10,1... | collective-permute-start | bytes 491528 | tf_op jit(solution)/shard_map/ppermute | solution.py:590
  8.1 0.0 collective-permute-done.below_ref
  8.1 1.1 %collective-permute-start.5 = (f32[5,64,128]{2,1,0:T(8,128)S(1)}, f32[5,64,128]{2,1,0:T(8,128)S(1)}, u32[]{:S(2)}, u32[]{:S(2)}) collective-permute-start(f32[5,64,128]{2,1,0:T(8,128)S(1)} %get-tuple-element.35), channel_id=1, source_target_pairs={{1,0},{2,1},{3,2},{0,3},{5,4},{6,5},{7,6},{4,7},{9,8},{10,9},{11,1... | collective-permute-start | bytes 491528 | tf_op jit(solution)/shard_map/ppermute | solution.py:590
  9.2 0.0 collective-permute-done.1.above_ref
  9.2 1.3 %collective-permute-start.6 = (f32[40,512]{1,0:T(8,128)S(1)}, f32[40,512]{1,0:T(8,128)S(1)}, u32[]{:S(2)}, u32[]{:S(2)}) collective-permute-start(f32[40,512]{1,0:T(8,128)S(1)} %get-tuple-element.36), channel_id=1, source_target_pairs={{4,0},{8,4},{12,8},{16,12},{20,16},{24,20},{28,24},{5,1},{9,5},{13... | collective-permute-start | bytes 245768 | tf_op jit(solution)/shard_map/ppermute | solution.py:624
  10.5 0.6 %shard_map.132 = (f32[5,4,64,128]{3,2,1,0:T(8,128)S(1)}, f32[5,4,64,128]{3,2,1,0:T(8,128)S(1)}) custom-call(f32[5,4,64,128]{3,2,1,0:T(8,128)S(1)} %bitcast.20, f32[5,4,64,128]{3,2,1,0:T(8,128)S(1)} %get-tuple-element.23.rate_ref, f32[5,4,64,128]{3,2,1,0:T(8,128)S(1)} %copy-done.1, f32[5,64,128]{2,1,0:T(8,128)S(1)} %collective-permute-done.below_ref, ...), custom_call_target="tpu_custom_call" | custom-call | tf_op jit(solution)/shard_map/pallas_call | solution.py:129
  11.2 0.7 %collective-permute-done.2.below_rate_ref = f32[5,64,128]{2,1,0:T(8,128)S(1)} collective-permute-done((f32[5,64,128]{2,1,0:T(8,128)S(1)}, f32[5,64,128]{2,1,0:T(8,128)S(1)}, u32[]{:S(2)}, u32[]{:S(2)}) %collective-permute-start.2) | collective-permute-done | bytes 163872 | tf_op jit(solution)/shard_map/ppermute | solution.py:590
  11.9 0.5 %collective-permute-done.3.above_rate_ref = f32[5,64,128]{2,1,0:T(8,128)S(1)} collective-permute-done((f32[5,64,128]{2,1,0:T(8,128)S(1)}, f32[5,64,128]{2,1,0:T(8,128)S(1)}, u32[]{:S(2)}, u32[]{:S(2)}) %collective-permute-start.3) | collective-permute-done | bytes 163872 | tf_op jit(solution)/shard_map/ppermute | solution.py:590
  12.4 0.0 copy-start.2
  12.4 0.0 copy-start.3
  12.4 0.0 copy-start.6
  12.4 0.0 copy-start.8
  12.4 1.4 %shard_map.133 = (f32[2,5,64,128]{3,2,1,0:T(8,128)S(1)}, f32[2,5,64,128]{3,2,1,0:T(8,128)S(1)}, f32[2,5,64,128]{3,2,1,0:T(8,128)S(1)}, f32[5,2,64,128]{3,2,1,0:T(8,128)S(1)}) custom-call(f32[5,4,64,128]{3,2,1,0:T(8,128)S(1)} %bitcast.21, f32[5,4,64,128]{3,2,1,0:T(8,128)S(1)} %get-tuple-element.26.second_ref, ...), custom_call_target="tpu_custom_call" | custom-call | tf_op jit(solution)/shard_map/pallas_call | solution.py:129
  13.8 2.4 %collective-permute-done.6.shifted_ref = f32[40,512]{1,0:T(8,128)S(1)} collective-permute-done((f32[40,512]{1,0:T(8,128)S(1)}, f32[40,512]{1,0:T(8,128)S(1)}, u32[]{:S(2)}, u32[]{:S(2)}) %collective-permute-start.6) | collective-permute-done | bytes 81952 | tf_op jit(solution)/shard_map/ppermute | solution.py:624
  16.1 0.0 collective-permute-done.4.below_ref
  16.2 0.0 collective-permute-done.5.above_ref
  16.2 0.0 copy-done.2
  16.2 0.0 copy-done.3
  16.2 0.0 copy-done.6
  16.2 0.0 copy-done.8
  16.2 1.0 %shard_map.134 = (f32[4,40,128]{2,1,0:T(8,128)S(1)}, f32[5,4,64,128]{3,2,1,0:T(8,128)S(1)}, f32[2,5,64,128]{3,2,1,0:T(8,128)S(1)}) custom-call(f32[5,4,64,128]{3,2,1,0:T(8,128)S(1)} %bitcast.22, f32[2,5,64,128]{3,2,1,0:T(8,128)S(1)} %get-tuple-element.30.base_ref, f32[2,5,64,128]{3,2,1,0:T(8,128)S(1)} %get-tuple-element.31.edge_rate_ref, ...), custom_call_target="tpu_custom_call" | custom-call | tf_op jit(solution)/shard_map/pallas_call | solution.py:129
  17.2 0.5 %collective-permute-start.7 = (f32[40,128]{1,0:T(8,128)S(1)}, f32[40,128]{1,0:T(8,128)S(1)}, u32[]{:S(2)}, u32[]{:S(2)}) collective-permute-start(f32[40,128]{1,0:T(8,128)S(1)} %get-tuple-element.45), channel_id=1, source_target_pairs={{0,1},{1,0},{2,3},{3,2},{4,5},{5,4},{6,7},{7,6},{8,9},{9,8},{10,11... | collective-permute-start | bytes 61448 | tf_op jit(solution)/shard_map/ppermute | solution.py:658
  17.8 1.7 %collective-permute-start.9 = (f32[40,128]{1,0:T(8,128)S(1)}, f32[40,128]{1,0:T(8,128)S(1)}, u32[]{:S(2)}, u32[]{:S(2)}) collective-permute-start(f32[40,128]{1,0:T(8,128)S(1)} %get-tuple-element.46), channel_id=1, source_target_pairs={{0,3},{1,2},{2,1},{3,0},{4,7},{5,6},{6,5},{7,4},{8,11},{9,10},{10,... | collective-permute-start | bytes 61448 | tf_op jit(solution)/shard_map/ppermute | solution.py:658
  19.4 0.0 collective-permute-start.8
  19.5 0.0 collective-permute-done.7
  19.5 1.5 %collective-permute-done.9 = f32[40,128]{1,0:T(8,128)S(1)} collective-permute-done((f32[40,128]{1,0:T(8,128)S(1)}, f32[40,128]{1,0:T(8,128)S(1)}, u32[]{:S(2)}, u32[]{:S(2)}) %collective-permute-start.9) | collective-permute-done | bytes 20512 | tf_op jit(solution)/shard_map/ppermute | solution.py:658
  21.0 2.3 %collective-permute-done.8 = f32[40,128]{1,0:T(8,128)S(1)} collective-permute-done((f32[40,128]{1,0:T(8,128)S(1)}, f32[40,128]{1,0:T(8,128)S(1)}, u32[]{:S(2)}, u32[]{:S(2)}) %collective-permute-start.8) | collective-permute-done | bytes 20512 | tf_op jit(solution)/shard_map/ppermute | solution.py:658
  23.2 0.7 %broadcast_in_dim.6 = f32[8,40,128]{2,1,0:T(8,128)} broadcast(f32[40,128]{1,0:T(8,128)S(1)} %fusion.1), dimensions={1,2} | broadcast | bytes 184320 | tf_op jit(solution)/shard_map/broadcast_in_dim | solution.py:665
  23.9 5.4 %all-to-all-start = ((f32[8,40,128]{2,1,0:T(8,128)}), f32[8,40,128]{2,1,0:T(8,128)S(1)}, u32[]{:S(2)}, u32[]{:S(2)}) async-start(f32[8,40,128]{2,1,0:T(8,128)} %broadcast_in_dim.6), calls=%async_computation | async-start | bytes 327680 | tf_op jit(solution)/shard_map/all_to_all | solution.py:665
  29.4 0.0 copy-start.9
  29.4 0.0 copy-start.11
  29.4 0.1 collective-permute-start.14
  29.5 0.5 %collective-permute-start.13 = (f32[5,64,128]{2,1,0:T(8,128)S(1)}, f32[5,64,128]{2,1,0:T(8,128)S(1)}, u32[]{:S(2)}, u32[]{:S(2)}) collective-permute-start(f32[5,64,128]{2,1,0:T(8,128)S(1)} %get-tuple-element.44), channel_id=1, source_target_pairs={{0,1},{1,2},{2,3},{3,0},{4,5},{5,6},{6,7},{7,4},{8,9},{9,10},{10,1... | collective-permute-start | bytes 491528 | tf_op jit(solution)/shard_map/ppermute | solution.py:590
  30.0 7.0 %all-to-all-done.jump_ref = f32[8,40,128]{2,1,0:T(8,128)S(1)} async-done(((f32[8,40,128]{2,1,0:T(8,128)}), f32[8,40,128]{2,1,0:T(8,128)S(1)}, u32[]{:S(2)}, u32[]{:S(2)}) %all-to-all-start) | async-done | bytes 163872 | tf_op jit(solution)/shard_map/all_to_all | solution.py:665
  36.9 0.0 copy-done.9
  36.9 0.0 copy-done.11
  36.9 0.2 shard_map.135.refs_0_
  37.1 0.0 collective-permute-start.12
  37.1 0.7 %collective-permute-start.11 = (f32[48,128]{1,0:T(8,128)S(1)}, f32[48,128]{1,0:T(8,128)S(1)}, u32[]{:S(2)}, u32[]{:S(2)}) collective-permute-start(f32[48,128]{1,0:T(8,128)S(1)} %shard_map.135.refs_0_), channel_id=1, source_target_pairs={{0,2},{1,3},{2,0},{3,1},{4,6},{5,7},{6,4},{7,5},{8,10},{9,11},{10,... | collective-permute-start | bytes 73736 | tf_op jit(solution)/shard_map/ppermute | solution.py:675
  37.8 1.2 %collective-permute-start.10 = (f32[48,128]{1,0:T(8,128)S(1)}, f32[48,128]{1,0:T(8,128)S(1)}, u32[]{:S(2)}, u32[]{:S(2)}) collective-permute-start(f32[48,128]{1,0:T(8,128)S(1)} %shard_map.135.refs_0_), channel_id=1, source_target_pairs={{0,1},{1,0},{2,3},{3,2},{4,5},{5,4},{6,7},{7,6},{8,9},{9,8},{10,11... | collective-permute-start | bytes 73736 | tf_op jit(solution)/shard_map/ppermute | solution.py:675
  39.0 0.0 collective-permute-done.14.above_ref.refs_6_
  39.0 0.0 collective-permute-done.13.below_ref.refs_5_
  39.0 0.0 copy-start.4
  39.0 0.0 copy-start.5
  39.0 0.0 copy-start.10
  39.0 0.9 %shard_map.136.refs_11_ = f32[5,4,64,128]{3,2,1,0:T(8,128)} custom-call(f32[5,4,64,128]{3,2,1,0:T(8,128)S(1)} %get-tuple-element.38.fine_ref.refs_4_, f32[5,64,128]{2,1,0:T(8,128)S(1)} %collective-permute-done.13.below_ref.refs_5_, f32[5,64,128]{2,1,0:T(8,128)S(1)} %collective-permute-done.14.above_ref.refs_6_), custom_call_target="tpu_custom_call" | custom-call | tf_op jit(solution)/shard_map/pallas_call | solution.py:129
  39.9 0.5 %collective-permute-done.12.refs_3_ = f32[48,128]{1,0:T(8,128)S(1)} collective-permute-done((f32[48,128]{1,0:T(8,128)S(1)}, f32[48,128]{1,0:T(8,128)S(1)}, u32[]{:S(2)}, u32[]{:S(2)}) %collective-permute-start.12) | collective-permute-done | bytes 24608 | tf_op jit(solution)/shard_map/ppermute | solution.py:675
  40.4 0.6 %collective-permute-done.11.refs_2_ = f32[48,128]{1,0:T(8,128)S(1)} collective-permute-done((f32[48,128]{1,0:T(8,128)S(1)}, f32[48,128]{1,0:T(8,128)S(1)}, u32[]{:S(2)}, u32[]{:S(2)}) %collective-permute-start.11) | collective-permute-done | bytes 24608 | tf_op jit(solution)/shard_map/ppermute | solution.py:675
  41.0 0.0 collective-permute-done.10.refs_1_
  41.0 0.0 copy-done.4
  41.0 0.0 copy-done.5
  41.0 0.0 copy-done.10
  41.1 0.7 %shard_map.137 = (f32[5,4,64,128]{3,2,1,0:T(8,128)}, f32[1]{0:T(128)}, f32[1]{0:T(128)}) custom-call(f32[48,128]{1,0:T(8,128)S(1)} %shard_map.135.refs_0_, f32[48,128]{1,0:T(8,128)S(1)} %collective-permute-done.10.refs_1_, f32[48,128]{1,0:T(8,128)S(1)} %collective-permute-done.11.refs_2_, ...), custom_call_target="tpu_custom_call", output_to_operand_aliasing={{0}: (11, {})} | custom-call | tf_op jit(solution)/shard_map/pallas_call | solution.py:129
  (4 shorter events, 0.1 us)
Async XLA Ops:
  0.6 1.1 %copy-start = (f32[1,5,4,64,128]{4,3,2,1,0:T(8,128)S(1)}, f32[1,5,4,64,128]{4,3,2,1,0:T(8,128)}, u32[]{:S(2)}) copy-start(f32[1,5,4,64,128]{4,3,2,1,0:T(8,128)} %param.11) | copy-start | bytes 1966084
  1.7 2.6 %copy-start.1 = (f32[5,4,64,128]{3,2,1,0:T(8,128)S(1)}, f32[5,4,64,128]{3,2,1,0:T(8,128)}, u32[]{:S(2)}) copy-start(f32[5,4,64,128]{3,2,1,0:T(8,128)} %source_ref.5) | copy-start | bytes 1966084
  1.7 6.4 %collective-permute-start = (f32[5,64,128]{2,1,0:T(8,128)S(1)}, f32[5,64,128]{2,1,0:T(8,128)S(1)}, u32[]{:S(2)}, u32[]{:S(2)}) collective-permute-start(f32[5,64,128]{2,1,0:T(8,128)S(1)} %get-tuple-element.24), channel_id=1, source_target_pairs={{0,1},{1,2},{2,3},{3,0},{4,5},{5,6},{6,7},{7,4},{8,9},{9,10},{10,1... | collective-permute-start | bytes 491528 | tf_op jit(solution)/shard_map/ppermute | solution.py:590
  2.3 6.9 %collective-permute-start.1 = (f32[5,64,128]{2,1,0:T(8,128)S(1)}, f32[5,64,128]{2,1,0:T(8,128)S(1)}, u32[]{:S(2)}, u32[]{:S(2)}) collective-permute-start(f32[5,64,128]{2,1,0:T(8,128)S(1)} %get-tuple-element.25), channel_id=1, source_target_pairs={{1,0},{2,1},{3,2},{0,3},{5,4},{6,5},{7,6},{4,7},{9,8},{10,9},{11,1... | collective-permute-start | bytes 491528 | tf_op jit(solution)/shard_map/ppermute | solution.py:590
  4.3 0.7 %copy-start.7 = (bf16[32,256]{1,0:T(8,128)(2,1)S(1)}, bf16[32,256]{1,0:T(8,128)(2,1)}, u32[]{:S(2)}) copy-start(bf16[32,256]{1,0:T(8,128)(2,1)} %constant.18.clone.table_ref) | copy-start | bytes 49156
  5.7 6.2 %collective-permute-start.2 = (f32[5,64,128]{2,1,0:T(8,128)S(1)}, f32[5,64,128]{2,1,0:T(8,128)S(1)}, u32[]{:S(2)}, u32[]{:S(2)}) collective-permute-start(f32[5,64,128]{2,1,0:T(8,128)S(1)} %get-tuple-element.28), channel_id=1, source_target_pairs={{0,1},{1,2},{2,3},{3,0},{4,5},{5,6},{6,7},{7,4},{8,9},{9,10},{10,1... | collective-permute-start | bytes 491528 | tf_op jit(solution)/shard_map/ppermute | solution.py:590
  6.3 6.0 %collective-permute-start.3 = (f32[5,64,128]{2,1,0:T(8,128)S(1)}, f32[5,64,128]{2,1,0:T(8,128)S(1)}, u32[]{:S(2)}, u32[]{:S(2)}) collective-permute-start(f32[5,64,128]{2,1,0:T(8,128)S(1)} %get-tuple-element.29), channel_id=1, source_target_pairs={{1,0},{2,1},{3,2},{0,3},{5,4},{6,5},{7,6},{4,7},{9,8},{10,9},{11,1... | collective-permute-start | bytes 491528 | tf_op jit(solution)/shard_map/ppermute | solution.py:590
  7.5 8.7 %collective-permute-start.4 = (f32[5,64,128]{2,1,0:T(8,128)S(1)}, f32[5,64,128]{2,1,0:T(8,128)S(1)}, u32[]{:S(2)}, u32[]{:S(2)}) collective-permute-start(f32[5,64,128]{2,1,0:T(8,128)S(1)} %get-tuple-element.34), channel_id=1, source_target_pairs={{0,1},{1,2},{2,3},{3,0},{4,5},{5,6},{6,7},{7,4},{8,9},{9,10},{10,1... | collective-permute-start | bytes 491528 | tf_op jit(solution)/shard_map/ppermute | solution.py:590
  8.1 8.1 %collective-permute-start.5 = (f32[5,64,128]{2,1,0:T(8,128)S(1)}, f32[5,64,128]{2,1,0:T(8,128)S(1)}, u32[]{:S(2)}, u32[]{:S(2)}) collective-permute-start(f32[5,64,128]{2,1,0:T(8,128)S(1)} %get-tuple-element.35), channel_id=1, source_target_pairs={{1,0},{2,1},{3,2},{0,3},{5,4},{6,5},{7,6},{4,7},{9,8},{10,9},{11,1... | collective-permute-start | bytes 491528 | tf_op jit(solution)/shard_map/ppermute | solution.py:590
  9.2 6.9 %collective-permute-start.6 = (f32[40,512]{1,0:T(8,128)S(1)}, f32[40,512]{1,0:T(8,128)S(1)}, u32[]{:S(2)}, u32[]{:S(2)}) collective-permute-start(f32[40,512]{1,0:T(8,128)S(1)} %get-tuple-element.36), channel_id=1, source_target_pairs={{4,0},{8,4},{12,8},{16,12},{20,16},{24,20},{28,24},{5,1},{9,5},{13... | collective-permute-start | bytes 245768 | tf_op jit(solution)/shard_map/ppermute | solution.py:624
  12.4 3.8 %copy-start.2 = (bf16[768,512]{1,0:T(8,128)(2,1)S(1)}, bf16[768,512]{1,0:T(8,128)(2,1)}, u32[]{:S(2)}) copy-start(bf16[768,512]{1,0:T(8,128)(2,1)} %constant.20.clone.low_ref) | copy-start | bytes 2359300
  12.4 3.8 %copy-start.3 = (bf16[768,512]{1,0:T(8,128)(2,1)S(1)}, bf16[768,512]{1,0:T(8,128)(2,1)}, u32[]{:S(2)}) copy-start(bf16[768,512]{1,0:T(8,128)(2,1)} %constant.19.clone.high_ref) | copy-start | bytes 2359300
  12.4 3.8 %copy-start.6 = (f32[4,2,4,128]{3,2,1,0:T(4,128)S(1)}, f32[4,2,4,128]{3,2,1,0:T(4,128)}, u32[]{:S(2)}) copy-start(f32[4,2,4,128]{3,2,1,0:T(4,128)} %constant.21.clone.phase_ref.refs_10_) | copy-start | bytes 49156
  12.4 3.8 %copy-start.8 = (bf16[32,256]{1,0:T(8,128)(2,1)S(1)}, bf16[32,256]{1,0:T(8,128)(2,1)}, u32[]{:S(2)}) copy-start(bf16[32,256]{1,0:T(8,128)(2,1)} %constant.18.clone.table_ref) | copy-start | bytes 49156
  17.2 2.3 %collective-permute-start.7 = (f32[40,128]{1,0:T(8,128)S(1)}, f32[40,128]{1,0:T(8,128)S(1)}, u32[]{:S(2)}, u32[]{:S(2)}) collective-permute-start(f32[40,128]{1,0:T(8,128)S(1)} %get-tuple-element.45), channel_id=1, source_target_pairs={{0,1},{1,0},{2,3},{3,2},{4,5},{5,4},{6,7},{7,6},{8,9},{9,8},{10,11... | collective-permute-start | bytes 61448 | tf_op jit(solution)/shard_map/ppermute | solution.py:658
  17.8 3.2 %collective-permute-start.9 = (f32[40,128]{1,0:T(8,128)S(1)}, f32[40,128]{1,0:T(8,128)S(1)}, u32[]{:S(2)}, u32[]{:S(2)}) collective-permute-start(f32[40,128]{1,0:T(8,128)S(1)} %get-tuple-element.46), channel_id=1, source_target_pairs={{0,3},{1,2},{2,1},{3,0},{4,7},{5,6},{6,5},{7,4},{8,11},{9,10},{10,... | collective-permute-start | bytes 61448 | tf_op jit(solution)/shard_map/ppermute | solution.py:658
  19.4 3.8 %collective-permute-start.8 = (f32[40,128]{1,0:T(8,128)S(1)}, f32[40,128]{1,0:T(8,128)S(1)}, u32[]{:S(2)}, u32[]{:S(2)}) collective-permute-start(f32[40,128]{1,0:T(8,128)S(1)} %get-tuple-element.47), channel_id=1, source_target_pairs={{0,2},{1,3},{2,0},{3,1},{4,6},{5,7},{6,4},{7,5},{8,10},{9,11},{10,... | collective-permute-start | bytes 61448 | tf_op jit(solution)/shard_map/ppermute | solution.py:658
  23.9 13.0 %all-to-all-start = ((f32[8,40,128]{2,1,0:T(8,128)}), f32[8,40,128]{2,1,0:T(8,128)S(1)}, u32[]{:S(2)}, u32[]{:S(2)}) async-start(f32[8,40,128]{2,1,0:T(8,128)} %broadcast_in_dim.6), calls=%async_computation | async-start | bytes 327680 | tf_op jit(solution)/shard_map/all_to_all | solution.py:665
  29.4 7.6 %copy-start.9 = (f32[4,2,8,128]{3,2,1,0:T(8,128)S(1)}, f32[4,2,8,128]{3,2,1,0:T(8,128)}, u32[]{:S(2)}) copy-start(f32[4,2,8,128]{3,2,1,0:T(8,128)} %constant.22.clone.symbol_ref) | copy-start | bytes 98308
  29.4 7.6 %copy-start.11 = (f32[8,128]{1,0:T(8,128)S(1)}, f32[8,128]{1,0:T(8,128)}, u32[]{:S(2)}) copy-start(f32[8,128]{1,0:T(8,128)} %constant.23.clone.share_ref) | copy-start | bytes 12292
  29.4 9.6 %collective-permute-start.14 = (f32[5,64,128]{2,1,0:T(8,128)S(1)}, f32[5,64,128]{2,1,0:T(8,128)S(1)}, u32[]{:S(2)}, u32[]{:S(2)}) collective-permute-start(f32[5,64,128]{2,1,0:T(8,128)S(1)} %get-tuple-element.43), channel_id=1, source_target_pairs={{1,0},{2,1},{3,2},{0,3},{5,4},{6,5},{7,6},{4,7},{9,8},{10,9},{11,1... | collective-permute-start | bytes 491528 | tf_op jit(solution)/shard_map/ppermute | solution.py:590
  29.5 9.5 %collective-permute-start.13 = (f32[5,64,128]{2,1,0:T(8,128)S(1)}, f32[5,64,128]{2,1,0:T(8,128)S(1)}, u32[]{:S(2)}, u32[]{:S(2)}) collective-permute-start(f32[5,64,128]{2,1,0:T(8,128)S(1)} %get-tuple-element.44), channel_id=1, source_target_pairs={{0,1},{1,2},{2,3},{3,0},{4,5},{5,6},{6,7},{7,4},{8,9},{9,10},{10,1... | collective-permute-start | bytes 491528 | tf_op jit(solution)/shard_map/ppermute | solution.py:590
  37.1 3.3 %collective-permute-start.12 = (f32[48,128]{1,0:T(8,128)S(1)}, f32[48,128]{1,0:T(8,128)S(1)}, u32[]{:S(2)}, u32[]{:S(2)}) collective-permute-start(f32[48,128]{1,0:T(8,128)S(1)} %shard_map.135.refs_0_), channel_id=1, source_target_pairs={{0,3},{1,2},{2,1},{3,0},{4,7},{5,6},{6,5},{7,4},{8,11},{9,10},{10,... | collective-permute-start | bytes 73736 | tf_op jit(solution)/shard_map/ppermute | solution.py:675
  37.1 3.9 %collective-permute-start.11 = (f32[48,128]{1,0:T(8,128)S(1)}, f32[48,128]{1,0:T(8,128)S(1)}, u32[]{:S(2)}, u32[]{:S(2)}) collective-permute-start(f32[48,128]{1,0:T(8,128)S(1)} %shard_map.135.refs_0_), channel_id=1, source_target_pairs={{0,2},{1,3},{2,0},{3,1},{4,6},{5,7},{6,4},{7,5},{8,10},{9,11},{10,... | collective-permute-start | bytes 73736 | tf_op jit(solution)/shard_map/ppermute | solution.py:675
  37.8 3.2 %collective-permute-start.10 = (f32[48,128]{1,0:T(8,128)S(1)}, f32[48,128]{1,0:T(8,128)S(1)}, u32[]{:S(2)}, u32[]{:S(2)}) collective-permute-start(f32[48,128]{1,0:T(8,128)S(1)} %shard_map.135.refs_0_), channel_id=1, source_target_pairs={{0,1},{1,0},{2,3},{3,2},{4,5},{5,4},{6,7},{7,6},{8,9},{9,8},{10,11... | collective-permute-start | bytes 73736 | tf_op jit(solution)/shard_map/ppermute | solution.py:675
  39.0 2.0 %copy-start.4 = (bf16[512,512]{1,0:T(8,128)(2,1)S(1)}, bf16[512,512]{1,0:T(8,128)(2,1)}, u32[]{:S(2)}) copy-start(bf16[512,512]{1,0:T(8,128)(2,1)} %constant.25.clone.refs_8_) | copy-start | bytes 1572868
  39.0 2.0 %copy-start.5 = (bf16[512,512]{1,0:T(8,128)(2,1)S(1)}, bf16[512,512]{1,0:T(8,128)(2,1)}, u32[]{:S(2)}) copy-start(bf16[512,512]{1,0:T(8,128)(2,1)} %constant.24.clone.refs_7_) | copy-start | bytes 1572868
  39.0 2.0 %copy-start.10 = (bf16[48,128]{1,0:T(8,128)(2,1)S(1)}, bf16[48,128]{1,0:T(8,128)(2,1)}, u32[]{:S(2)}) copy-start(bf16[48,128]{1,0:T(8,128)(2,1)} %constant.26.clone.refs_9_) | copy-start | bytes 36868

commit v6 on v5

--- a/solution.py
+++ b/solution.py
@@ -66,6 +66,24 @@
     inner = forward(range(slab))
     outer = forward([-1, slab])
     tables["yzforward"] = hi_lo(np.concatenate([inner[0], inner[1], outer[0], outer[1]]))
+    theta = turn * ky[None, :] * np.arange(rows)[:, None] / rows
+    c, s = np.cos(theta), np.sin(theta)
+    layers = np.eye(slab)
+
+    def planes(block):
+        return np.einsum("ab,yk->aybk", layers, block).reshape(slab * rows, -1)
+
+    tables["yforward"] = hi_lo(np.block([[planes(c), -planes(s)], [planes(s), planes(c)]]))
+    theta = turn * kz.reshape(1, width, slab) * np.arange(slab).reshape(-1, 1, 1) / depth
+    c, s = np.cos(theta), np.sin(theta)
+    modes = np.eye(2 * keep_y)
+
+    def spread(real, imag):
+        return np.einsum("zgrk,jl->zjgrkl", np.stack([real, imag], axis=2), modes).reshape(
+            slab * 2 * keep_y, -1
+        )
+
+    tables["zforward"] = hi_lo(np.concatenate([spread(c, -s), spread(s, c)]))
     theta = joint(range(slab))
     count = theta.shape[0]
     c, s = np.cos(theta), np.sin(theta)
@@ -279,6 +297,10 @@
     lanes = real.shape[1]
     waves_ref[:, :lanes] = real
     waves_ref[:, lanes:] = imag
+
+
+def start_planes_kernel(waves_ref, high_ref, low_ref, out_ref):
+    out_ref[...] = three_pass(waves_ref[...], high_ref[...], low_ref[...])
 
 
 def second_rate_kernel(
@@ -386,6 +408,8 @@
     table_ref,
     high_ref,
     low_ref,
+    shift_high_ref,
+    shift_low_ref,
     phase_ref,
     out_ref,
     inner_ref,
@@ -435,12 +459,10 @@
         [outer_ref[side, f] for f in range(fields) for side in range(2)]
     )
     outer_real, outer_imag = by_field(along_x(outer_cells, table), fields, keep)
-    shifted = shifted_ref[...]
-    lanes = real.shape[1]
-    left = jnp.concatenate(
-        [real - shifted[:, :lanes], imag - shifted[:, lanes:], outer_real, outer_imag], axis=1
-    )
-    waves = three_pass(left, high_ref[...], low_ref[...])
+    left = jnp.concatenate([real, imag, outer_real, outer_imag], axis=1)
+    waves = three_pass(left, high_ref[...], low_ref[...]) - three_pass(
+        shifted_ref[...], shift_high_ref[...], shift_low_ref[...]
+    )
     for group in range(width):
         block = waves[:, group * 2 * half : (group + 1) * 2 * half]
         turned = (
@@ -520,7 +542,8 @@
         total_ref,
         order_ref,
         held_ref,
-        norm_refs,
+        own_norm_ref,
+        whole_norm_ref,
         sems,
         norm_sems,
     ) = refs[width:]
@@ -536,11 +559,11 @@
     line = lax.broadcasted_iota(jnp.int32, sums.shape, 0)
     own = jnp.sum(jnp.where(line == moment, sums, 0.0), axis=0, keepdims=True)
     whole = jnp.sum(sums, axis=0, keepdims=True)
-    norm_refs[0, 0] = jnp.sqrt(own * scales[0] + epsilon)[0, 0]
-    norm_refs[1, 0] = jnp.sqrt(whole * scales[1] + epsilon)[0, 0]
+    own_norm_ref[...] = jnp.sqrt(own * scales[0] + epsilon)[:, :1]
+    whole_norm_ref[...] = jnp.sqrt(whole * scales[1] + epsilon)[:, :1]
     norms = [
-        pltpu.make_async_copy(norm_refs.at[side], out_ref, norm_sems.at[side])
-        for side, out_ref in enumerate((slice_ref, total_ref))
+        pltpu.make_async_copy(own_norm_ref, slice_ref, norm_sems.at[0]),
+        pltpu.make_async_copy(whole_norm_ref, total_ref, norm_sems.at[1]),
     ]
     for copy in norms:
         copy.start()
@@ -587,7 +610,9 @@
     count = lax.axis_size("space")
     ups = [(i, (i + 1) % count) for i in range(count)]
     downs = [((i + 1) % count, i) for i in range(count)]
-    return lax.ppermute(up, "space", ups), lax.ppermute(down, "space", downs)
+    below = lax.ppermute(up, "space", ups)
+    above = lax.ppermute(down, "space", downs)
+    return below, above
 
 
 def shards(starts, source):
@@ -621,7 +646,12 @@
     )
     below_rate, above_rate = halo(given[0], given[1])
     below_feed, above_feed = halo(given[2], given[3])
-    next_waves = lax.ppermute(start_waves, "tm", [(i + 1, i) for i in range(slices - 1)])
+    start_planes = local_call(
+        start_planes_kernel,
+        jax.ShapeDtypeStruct((lines, lanes), real),
+        [start_waves, *tables["yforward"]],
+    )
+    next_waves = lax.ppermute(start_planes, "tm", [(i + 1, i) for i in range(slices - 1)])
     rates, second = local_call(
         functools.partial(second_rate_kernel, step=steps[0]),
         (slab_shape, slab_shape),
@@ -650,6 +680,7 @@
             next_waves,
             tables["xforward"],
             *tables["yzforward"],
+            *tables["zforward"],
             tables["phase"],
         ],
     )
@@ -691,8 +722,8 @@
         ),
         (
             jax.ShapeDtypeStruct((fields, slab, rows, cols), real),
-            jax.ShapeDtypeStruct((1,), real),
-            jax.ShapeDtypeStruct((1,), real),
+            jax.ShapeDtypeStruct((1, 1), real),
+            jax.ShapeDtypeStruct((1, 1), real),
         ),
         [
             *blocks,
@@ -707,7 +738,8 @@
         [
             pltpu.VMEM((width, lines, lanes), real),
             whole_slab,
-            pltpu.SMEM((2, 1), real),
+            pltpu.VMEM((1, 1), real),
+            pltpu.VMEM((1, 1), real),
             pltpu.SemaphoreType.DMA((fields,)),
             pltpu.SemaphoreType.DMA((2,)),
         ],
@@ -715,7 +747,7 @@
         out_specs=(off_chip, off_chip, off_chip),
         aliases={width + 7: 0},
     )
-    return ends[None], slice_norm, total_norm
+    return ends[None], slice_norm[0], total_norm[0]
 
 
 def solution(mesh):

time: 42 us -> 41.9 us (level)
  local copies, waits for them, and re-layouts: 2.55 us -> 1.86 us
    unnamed x24 -> x32, local copies, waits for them, and re-layouts: 1.84 us -> 1.15 us
    pallas_call x8 -> x9, Pallas kernels: 5.51 us -> 5.76 us  [local_call(): pl.pallas_call(kernel, out_shape=out_shape, in_specs=specs, out_specs=out...]
  transfers between devices with their start and end apart: 16 -> 16, of which waited for: 8 -> 11; matrix products, arithmetic and copies ran while one was open for 0% -> 0% of each run, Pallas kernels for 9% -> 10%
where the time goes in v6:
time: 41.9 us; the launch traced here: 41.6 us
  starting transfers between devices  17.8 us (42%)
  waiting for transfers between devices  15.4 us (37%)
  Pallas kernels  5.76 us (14%)
  local copies, waits for them, and re-layouts  1.86 us (4%)
  between operations  0.82 us (2%)
    all_to_all x1, waiting for transfers between devices, shards(): lax.all_to_all(jnp.broadcast_to(jump, (slices, lines, lanes)), 'tm', 0, 0...  6.95 us
    pallas_call x9, Pallas kernels, local_call(): pl.pallas_call(kernel, out_shape=out_shape, in_specs=specs, out_specs=out...  5.76 us
    all_to_all x1, starting transfers between devices, shards(): lax.all_to_all(jnp.broadcast_to(jump, (slices, lines, lanes)), 'tm', 0, 0...  5.33 us
    ppermute x4, starting transfers between devices, halo(): above = lax.ppermute(down, 'space', downs)  4.37 us
    ppermute x3, waiting for transfers between devices, shards(): lax.ppermute(waves[step], 'space', [(i, target_of(i, step, width)) for i...  3.67 us
    ppermute x3, starting transfers between devices, shards(): lax.ppermute(waves[step], 'space', [(i, target_of(i, step, width)) for i...  2.67 us
    ppermute x4, starting transfers between devices, halo(): below = lax.ppermute(up, 'space', ups)  2.28 us
    ppermute x3, starting transfers between devices, shards(): lax.ppermute(message, 'space', [(i, target_of(i, step, width)) for i in r...  1.86 us
  transfers between devices with their start and end apart: 16, of which 11 were waited for; matrix products, arithmetic and copies ran while one was open for 0% of the time, Pallas kernels for 10%

profile of v6, /device:TPU:0, one launch (start us, length us, event | category | flops | bytes accessed | tf_op | source)
XLA Modules:
  0.0 41.6 jit_solution(10153021314587822941)
XLA Ops:
  0.6 0.0 copy-start.12
  0.6 0.0 copy-start
  0.7 1.1 %copy-done = f32[1,5,4,64,128]{4,3,2,1,0:T(8,128)S(1)} copy-done((f32[1,5,4,64,128]{4,3,2,1,0:T(8,128)S(1)}, f32[1,5,4,64,128]{4,3,2,1,0:T(8,128)}, u32[]{:S(2)}) %copy-start) | copy-done | bytes 655384
  1.7 0.0 copy-start.2
  1.8 0.5 %collective-permute-start = (f32[5,64,128]{2,1,0:T(8,128)S(1)}, f32[5,64,128]{2,1,0:T(8,128)S(1)}, u32[]{:S(2)}, u32[]{:S(2)}) collective-permute-start(f32[5,64,128]{2,1,0:T(8,128)S(1)} %get-tuple-element.24), channel_id=1, source_target_pairs={{0,1},{1,2},{2,3},{3,0},{4,5},{5,6},{6,7},{7,4},{8,9},{9,10},{10,1... | collective-permute-start | bytes 491528 | tf_op jit(solution)/shard_map/ppermute | solution.py:613
  2.3 0.0 copy-start.9
  2.3 2.0 %collective-permute-start.1 = (f32[5,64,128]{2,1,0:T(8,128)S(1)}, f32[5,64,128]{2,1,0:T(8,128)S(1)}, u32[]{:S(2)}, u32[]{:S(2)}) collective-permute-start(f32[5,64,128]{2,1,0:T(8,128)S(1)} %get-tuple-element.25), channel_id=1, source_target_pairs={{1,0},{2,1},{3,2},{0,3},{5,4},{6,5},{7,6},{4,7},{9,8},{10,9},{11,1... | collective-permute-start | bytes 491528 | tf_op jit(solution)/shard_map/ppermute | solution.py:614
  4.3 0.0 copy-done.12
  4.3 0.0 copy-done.2
  4.3 0.7 %shard_map.166 = (f32[5,4,64,128]{3,2,1,0:T(8,128)S(1)}, f32[40,512]{1,0:T(8,128)S(1)}, f32[5,64,128]{2,1,0:T(8,128)S(1)}, f32[5,64,128]{2,1,0:T(8,128)S(1)}, f3...) custom-call(f32[5,4,64,128]{3,2,1,0:T(8,128)S(1)} %bitcast.21, f32[5,4,64,128]{3,2,1,0:T(8,128)S(1)} %copy-done.2, ...), custom_call_target="tpu_custom_call" | custom-call | tf_op jit(solution)/shard_map/pallas_call | solution.py:147
  5.0 0.7 %collective-permute-start.2 = (f32[5,64,128]{2,1,0:T(8,128)S(1)}, f32[5,64,128]{2,1,0:T(8,128)S(1)}, u32[]{:S(2)}, u32[]{:S(2)}) collective-permute-start(f32[5,64,128]{2,1,0:T(8,128)S(1)} %get-tuple-element.28), channel_id=1, source_target_pairs={{0,1},{1,2},{2,3},{3,0},{4,5},{5,6},{6,7},{7,4},{8,9},{9,10},{10,1... | collective-permute-start | bytes 491528 | tf_op jit(solution)/shard_map/ppermute | solution.py:613
  5.7 1.1 %collective-permute-start.3 = (f32[5,64,128]{2,1,0:T(8,128)S(1)}, f32[5,64,128]{2,1,0:T(8,128)S(1)}, u32[]{:S(2)}, u32[]{:S(2)}) collective-permute-start(f32[5,64,128]{2,1,0:T(8,128)S(1)} %get-tuple-element.29), channel_id=1, source_target_pairs={{1,0},{2,1},{3,2},{0,3},{5,4},{6,5},{7,6},{4,7},{9,8},{10,9},{11,1... | collective-permute-start | bytes 491528 | tf_op jit(solution)/shard_map/ppermute | solution.py:614
  6.8 0.6 %collective-permute-start.4 = (f32[5,64,128]{2,1,0:T(8,128)S(1)}, f32[5,64,128]{2,1,0:T(8,128)S(1)}, u32[]{:S(2)}, u32[]{:S(2)}) collective-permute-start(f32[5,64,128]{2,1,0:T(8,128)S(1)} %get-tuple-element.34), channel_id=1, source_target_pairs={{0,1},{1,2},{2,3},{3,0},{4,5},{5,6},{6,7},{7,4},{8,9},{9,10},{10,1... | collective-permute-start | bytes 491528 | tf_op jit(solution)/shard_map/ppermute | solution.py:613
  7.4 0.0 collective-permute-done.below_ref
  7.4 1.2 %collective-permute-start.5 = (f32[5,64,128]{2,1,0:T(8,128)S(1)}, f32[5,64,128]{2,1,0:T(8,128)S(1)}, u32[]{:S(2)}, u32[]{:S(2)}) collective-permute-start(f32[5,64,128]{2,1,0:T(8,128)S(1)} %get-tuple-element.35), channel_id=1, source_target_pairs={{1,0},{2,1},{3,2},{0,3},{5,4},{6,5},{7,6},{4,7},{9,8},{10,9},{11,1... | collective-permute-start | bytes 491528 | tf_op jit(solution)/shard_map/ppermute | solution.py:614
  8.6 0.0 copy-done.9
  8.6 0.0 copy-done.10
  8.6 0.2 shard_map.170
  8.8 0.2 collective-permute-done.1.above_ref
  8.9 1.3 %collective-permute-start.6 = (f32[40,128]{1,0:T(8,128)S(1)}, f32[40,128]{1,0:T(8,128)S(1)}, u32[]{:S(2)}, u32[]{:S(2)}) collective-permute-start(f32[40,128]{1,0:T(8,128)S(1)} %shard_map.170), channel_id=1, source_target_pairs={{4,0},{8,4},{12,8},{16,12},{20,16},{24,20},{28,24},{5,1},{9,5},{13... | collective-permute-start | bytes 61448 | tf_op jit(solution)/shard_map/ppermute | solution.py:654
  10.2 0.0 copy-done.1
  10.2 0.7 %shard_map.168 = (f32[5,4,64,128]{3,2,1,0:T(8,128)S(1)}, f32[5,4,64,128]{3,2,1,0:T(8,128)S(1)}) custom-call(f32[5,4,64,128]{3,2,1,0:T(8,128)S(1)} %bitcast.22, f32[5,4,64,128]{3,2,1,0:T(8,128)S(1)} %get-tuple-element.23.rate_ref, f32[5,4,64,128]{3,2,1,0:T(8,128)S(1)} %copy-done.2, f32[5,64,128]{2,1,0:T(8,128)S(1)} %collective-permute-done.below_ref, ...), custom_call_target="tpu_custom_call" | custom-call | tf_op jit(solution)/shard_map/pallas_call | solution.py:147
  10.9 0.7 %collective-permute-done.2.below_rate_ref = f32[5,64,128]{2,1,0:T(8,128)S(1)} collective-permute-done((f32[5,64,128]{2,1,0:T(8,128)S(1)}, f32[5,64,128]{2,1,0:T(8,128)S(1)}, u32[]{:S(2)}, u32[]{:S(2)}) %collective-permute-start.2) | collective-permute-done | bytes 163872 | tf_op jit(solution)/shard_map/ppermute | solution.py:613
  11.6 0.9 %collective-permute-done.3.above_rate_ref = f32[5,64,128]{2,1,0:T(8,128)S(1)} collective-permute-done((f32[5,64,128]{2,1,0:T(8,128)S(1)}, f32[5,64,128]{2,1,0:T(8,128)S(1)}, u32[]{:S(2)}, u32[]{:S(2)}) %collective-permute-start.3) | collective-permute-done | bytes 163872 | tf_op jit(solution)/shard_map/ppermute | solution.py:614
  12.4 1.4 %shard_map.169 = (f32[2,5,64,128]{3,2,1,0:T(8,128)S(1)}, f32[2,5,64,128]{3,2,1,0:T(8,128)S(1)}, f32[2,5,64,128]{3,2,1,0:T(8,128)S(1)}, f32[5,2,64,128]{3,2,1,0:T(8,128)S(1)}) custom-call(f32[5,4,64,128]{3,2,1,0:T(8,128)S(1)} %bitcast.23, f32[5,4,64,128]{3,2,1,0:T(8,128)S(1)} %get-tuple-element.26.second_ref, ...), custom_call_target="tpu_custom_call" | custom-call | tf_op jit(solution)/shard_map/pallas_call | solution.py:147
  13.9 0.9 %collective-permute-done.6.shifted_ref = f32[40,128]{1,0:T(8,128)S(1)} collective-permute-done((f32[40,128]{1,0:T(8,128)S(1)}, f32[40,128]{1,0:T(8,128)S(1)}, u32[]{:S(2)}, u32[]{:S(2)}) %collective-permute-start.6) | collective-permute-done | bytes 20512 | tf_op jit(solution)/shard_map/ppermute | solution.py:654
  14.8 0.3 collective-permute-done.4.below_ref
  15.1 0.7 %collective-permute-done.5.above_ref = f32[5,64,128]{2,1,0:T(8,128)S(1)} collective-permute-done((f32[5,64,128]{2,1,0:T(8,128)S(1)}, f32[5,64,128]{2,1,0:T(8,128)S(1)}, u32[]{:S(2)}, u32[]{:S(2)}) %collective-permute-start.5) | collective-permute-done | bytes 163872 | tf_op jit(solution)/shard_map/ppermute | solution.py:614
  15.8 0.0 copy-done.3
  15.8 0.0 copy-done.4
  15.8 0.0 copy-done.7
  15.8 0.0 copy-done.8
  15.8 0.0 copy-done.11
  15.8 1.1 %shard_map.171 = (f32[4,40,128]{2,1,0:T(8,128)S(1)}, f32[5,4,64,128]{3,2,1,0:T(8,128)S(1)}, f32[2,5,64,128]{3,2,1,0:T(8,128)S(1)}) custom-call(f32[5,4,64,128]{3,2,1,0:T(8,128)S(1)} %bitcast.24, f32[2,5,64,128]{3,2,1,0:T(8,128)S(1)} %get-tuple-element.30.base_ref, f32[2,5,64,128]{3,2,1,0:T(8,128)S(1)} %get-tuple-element.31.edge_rate_ref, ...), custom_call_target="tpu_custom_call" | custom-call | tf_op jit(solution)/shard_map/pallas_call | solution.py:147
  16.9 1.0 %collective-permute-start.7 = (f32[40,128]{1,0:T(8,128)S(1)}, f32[40,128]{1,0:T(8,128)S(1)}, u32[]{:S(2)}, u32[]{:S(2)}) collective-permute-start(f32[40,128]{1,0:T(8,128)S(1)} %get-tuple-element.45), channel_id=1, source_target_pairs={{0,1},{1,0},{2,3},{3,2},{4,5},{5,4},{6,7},{7,6},{8,9},{9,8},{10,11... | collective-permute-start | bytes 61448 | tf_op jit(solution)/shard_map/ppermute | solution.py:689
  17.9 1.6 %collective-permute-start.9 = (f32[40,128]{1,0:T(8,128)S(1)}, f32[40,128]{1,0:T(8,128)S(1)}, u32[]{:S(2)}, u32[]{:S(2)}) collective-permute-start(f32[40,128]{1,0:T(8,128)S(1)} %get-tuple-element.46), channel_id=1, source_target_pairs={{0,3},{1,2},{2,1},{3,0},{4,7},{5,6},{6,5},{7,4},{8,11},{9,10},{10,... | collective-permute-start | bytes 61448 | tf_op jit(solution)/shard_map/ppermute | solution.py:689
  19.5 0.1 collective-permute-start.8
  19.6 0.0 collective-permute-done.7
  19.6 1.5 %collective-permute-done.9 = f32[40,128]{1,0:T(8,128)S(1)} collective-permute-done((f32[40,128]{1,0:T(8,128)S(1)}, f32[40,128]{1,0:T(8,128)S(1)}, u32[]{:S(2)}, u32[]{:S(2)}) %collective-permute-start.9) | collective-permute-done | bytes 20512 | tf_op jit(solution)/shard_map/ppermute | solution.py:689
  21.1 2.2 %collective-permute-done.8 = f32[40,128]{1,0:T(8,128)S(1)} collective-permute-done((f32[40,128]{1,0:T(8,128)S(1)}, f32[40,128]{1,0:T(8,128)S(1)}, u32[]{:S(2)}, u32[]{:S(2)}) %collective-permute-start.8) | collective-permute-done | bytes 20512 | tf_op jit(solution)/shard_map/ppermute | solution.py:689
  23.3 0.7 %broadcast_in_dim.6 = f32[8,40,128]{2,1,0:T(8,128)} broadcast(f32[40,128]{1,0:T(8,128)S(1)} %fusion.1), dimensions={1,2} | broadcast | bytes 184320 | tf_op jit(solution)/shard_map/broadcast_in_dim | solution.py:696
  24.0 5.3 %all-to-all-start = ((f32[8,40,128]{2,1,0:T(8,128)}), f32[8,40,128]{2,1,0:T(8,128)S(1)}, u32[]{:S(2)}, u32[]{:S(2)}) async-start(f32[8,40,128]{2,1,0:T(8,128)} %broadcast_in_dim.6), calls=%async_computation | async-start | bytes 327680 | tf_op jit(solution)/shard_map/all_to_all | solution.py:696
  29.3 0.0 copy-start.15
  29.4 0.1 collective-permute-start.14
  29.4 0.5 %collective-permute-start.13 = (f32[5,64,128]{2,1,0:T(8,128)S(1)}, f32[5,64,128]{2,1,0:T(8,128)S(1)}, u32[]{:S(2)}, u32[]{:S(2)}) collective-permute-start(f32[5,64,128]{2,1,0:T(8,128)S(1)} %get-tuple-element.44), channel_id=1, source_target_pairs={{0,1},{1,2},{2,3},{3,0},{4,5},{5,6},{6,7},{7,4},{8,9},{9,10},{10,1... | collective-permute-start | bytes 491528 | tf_op jit(solution)/shard_map/ppermute | solution.py:613
  29.9 7.0 %all-to-all-done.jump_ref = f32[8,40,128]{2,1,0:T(8,128)S(1)} async-done(((f32[8,40,128]{2,1,0:T(8,128)}), f32[8,40,128]{2,1,0:T(8,128)S(1)}, u32[]{:S(2)}, u32[]{:S(2)}) %all-to-all-start) | async-done | bytes 163872 | tf_op jit(solution)/shard_map/all_to_all | solution.py:696
  36.9 0.0 copy-done.13
  36.9 0.0 copy-done.15
  36.9 0.2 shard_map.172.refs_0_
  37.1 0.0 collective-permute-start.12
  37.1 0.6 %collective-permute-start.11 = (f32[48,128]{1,0:T(8,128)S(1)}, f32[48,128]{1,0:T(8,128)S(1)}, u32[]{:S(2)}, u32[]{:S(2)}) collective-permute-start(f32[48,128]{1,0:T(8,128)S(1)} %shard_map.172.refs_0_), channel_id=1, source_target_pairs={{0,2},{1,3},{2,0},{3,1},{4,6},{5,7},{6,4},{7,5},{8,10},{9,11},{10,... | collective-permute-start | bytes 73736 | tf_op jit(solution)/shard_map/ppermute | solution.py:706
  37.7 1.2 %collective-permute-start.10 = (f32[48,128]{1,0:T(8,128)S(1)}, f32[48,128]{1,0:T(8,128)S(1)}, u32[]{:S(2)}, u32[]{:S(2)}) collective-permute-start(f32[48,128]{1,0:T(8,128)S(1)} %shard_map.172.refs_0_), channel_id=1, source_target_pairs={{0,1},{1,0},{2,3},{3,2},{4,5},{5,4},{6,7},{7,6},{8,9},{9,8},{10,11... | collective-permute-start | bytes 73736 | tf_op jit(solution)/shard_map/ppermute | solution.py:706
  38.9 0.0 collective-permute-done.14.above_ref.refs_6_
  38.9 0.0 collective-permute-done.13.below_ref.refs_5_
  39.0 0.0 copy-start.6
  39.0 0.0 copy-start.14
  39.0 0.9 %shard_map.173.refs_11_ = f32[5,4,64,128]{3,2,1,0:T(8,128)} custom-call(f32[5,4,64,128]{3,2,1,0:T(8,128)S(1)} %get-tuple-element.38.fine_ref.refs_4_, f32[5,64,128]{2,1,0:T(8,128)S(1)} %collective-permute-done.13.below_ref.refs_5_, f32[5,64,128]{2,1,0:T(8,128)S(1)} %collective-permute-done.14.above_ref.refs_6_), custom_call_target="tpu_custom_call" | custom-call | tf_op jit(solution)/shard_map/pallas_call | solution.py:147
  39.9 0.5 %collective-permute-done.12.refs_3_ = f32[48,128]{1,0:T(8,128)S(1)} collective-permute-done((f32[48,128]{1,0:T(8,128)S(1)}, f32[48,128]{1,0:T(8,128)S(1)}, u32[]{:S(2)}, u32[]{:S(2)}) %collective-permute-start.12) | collective-permute-done | bytes 24608 | tf_op jit(solution)/shard_map/ppermute | solution.py:706
  40.3 0.6 %collective-permute-done.11.refs_2_ = f32[48,128]{1,0:T(8,128)S(1)} collective-permute-done((f32[48,128]{1,0:T(8,128)S(1)}, f32[48,128]{1,0:T(8,128)S(1)}, u32[]{:S(2)}, u32[]{:S(2)}) %collective-permute-start.11) | collective-permute-done | bytes 24608 | tf_op jit(solution)/shard_map/ppermute | solution.py:706
  41.0 0.0 collective-permute-done.10.refs_1_
  41.0 0.0 copy-done.5
  41.0 0.0 copy-done.6
  41.0 0.0 copy-done.14
  41.0 0.6 %shard_map.174 = (f32[5,4,64,128]{3,2,1,0:T(8,128)}, f32[1,1]{1,0:T(1,128)}, f32[1,1]{1,0:T(1,128)}) custom-call(f32[48,128]{1,0:T(8,128)S(1)} %shard_map.172.refs_0_, f32[48,128]{1,0:T(8,128)S(1)} %collective-permute-done.10.refs_1_, f32[48,128]{1,0:T(8,128)S(1)} %collective-permute-done.11.refs_2_, ...), custom_call_target="tpu_custom_call", output_to_operand_aliasing={{0}: (11, {})} | custom-call | tf_op jit(solution)/shard_map/pallas_call | solution.py:147
  (13 shorter events, 0.1 us)
Async XLA Ops:
  0.6 3.7 %copy-start.12 = (bf16[32,256]{1,0:T(8,128)(2,1)S(1)}, bf16[32,256]{1,0:T(8,128)(2,1)}, u32[]{:S(2)}) copy-start(bf16[32,256]{1,0:T(8,128)(2,1)} %constant.26.clone.table_ref) | copy-start | bytes 49156
  0.6 1.1 %copy-start = (f32[1,5,4,64,128]{4,3,2,1,0:T(8,128)S(1)}, f32[1,5,4,64,128]{4,3,2,1,0:T(8,128)}, u32[]{:S(2)}) copy-start(f32[1,5,4,64,128]{4,3,2,1,0:T(8,128)} %param.15) | copy-start | bytes 1966084
  1.7 2.6 %copy-start.2 = (f32[5,4,64,128]{3,2,1,0:T(8,128)S(1)}, f32[5,4,64,128]{3,2,1,0:T(8,128)}, u32[]{:S(2)}) copy-start(f32[5,4,64,128]{3,2,1,0:T(8,128)} %source_ref.5) | copy-start | bytes 1966084
  1.8 5.6 %collective-permute-start = (f32[5,64,128]{2,1,0:T(8,128)S(1)}, f32[5,64,128]{2,1,0:T(8,128)S(1)}, u32[]{:S(2)}, u32[]{:S(2)}) collective-permute-start(f32[5,64,128]{2,1,0:T(8,128)S(1)} %get-tuple-element.24), channel_id=1, source_target_pairs={{0,1},{1,2},{2,3},{3,0},{4,5},{5,6},{6,7},{7,4},{8,9},{9,10},{10,1... | collective-permute-start | bytes 491528 | tf_op jit(solution)/shard_map/ppermute | solution.py:613
  2.3 6.3 %copy-start.9 = (bf16[512,128]{1,0:T(8,128)(2,1)S(1)}, bf16[512,128]{1,0:T(8,128)(2,1)}, u32[]{:S(2)}) copy-start(bf16[512,128]{1,0:T(8,128)(2,1)} %constant.28.clone.low_ref) | copy-start | bytes 393220
  2.3 6.3 %copy-start.10 = (bf16[512,128]{1,0:T(8,128)(2,1)S(1)}, bf16[512,128]{1,0:T(8,128)(2,1)}, u32[]{:S(2)}) copy-start(bf16[512,128]{1,0:T(8,128)(2,1)} %constant.27.clone.high_ref) | copy-start | bytes 393220
  2.3 7.9 %copy-start.1 = (f32[1,5,4,64,128]{4,3,2,1,0:T(8,128)S(1)}, f32[1,5,4,64,128]{4,3,2,1,0:T(8,128)}, u32[]{:S(2)}) copy-start(f32[1,5,4,64,128]{4,3,2,1,0:T(8,128)} %param.15) | copy-start | bytes 1966084
  2.3 6.6 %collective-permute-start.1 = (f32[5,64,128]{2,1,0:T(8,128)S(1)}, f32[5,64,128]{2,1,0:T(8,128)S(1)}, u32[]{:S(2)}, u32[]{:S(2)}) collective-permute-start(f32[5,64,128]{2,1,0:T(8,128)S(1)} %get-tuple-element.25), channel_id=1, source_target_pairs={{1,0},{2,1},{3,2},{0,3},{5,4},{6,5},{7,6},{4,7},{9,8},{10,9},{11,1... | collective-permute-start | bytes 491528 | tf_op jit(solution)/shard_map/ppermute | solution.py:614
  5.0 6.5 %collective-permute-start.2 = (f32[5,64,128]{2,1,0:T(8,128)S(1)}, f32[5,64,128]{2,1,0:T(8,128)S(1)}, u32[]{:S(2)}, u32[]{:S(2)}) collective-permute-start(f32[5,64,128]{2,1,0:T(8,128)S(1)} %get-tuple-element.28), channel_id=1, source_target_pairs={{0,1},{1,2},{2,3},{3,0},{4,5},{5,6},{6,7},{7,4},{8,9},{9,10},{10,1... | collective-permute-start | bytes 491528 | tf_op jit(solution)/shard_map/ppermute | solution.py:613
  5.7 6.7 %collective-permute-start.3 = (f32[5,64,128]{2,1,0:T(8,128)S(1)}, f32[5,64,128]{2,1,0:T(8,128)S(1)}, u32[]{:S(2)}, u32[]{:S(2)}) collective-permute-start(f32[5,64,128]{2,1,0:T(8,128)S(1)} %get-tuple-element.29), channel_id=1, source_target_pairs={{1,0},{2,1},{3,2},{0,3},{5,4},{6,5},{7,6},{4,7},{9,8},{10,9},{11,1... | collective-permute-start | bytes 491528 | tf_op jit(solution)/shard_map/ppermute | solution.py:614
  6.8 8.3 %collective-permute-start.4 = (f32[5,64,128]{2,1,0:T(8,128)S(1)}, f32[5,64,128]{2,1,0:T(8,128)S(1)}, u32[]{:S(2)}, u32[]{:S(2)}) collective-permute-start(f32[5,64,128]{2,1,0:T(8,128)S(1)} %get-tuple-element.34), channel_id=1, source_target_pairs={{0,1},{1,2},{2,3},{3,0},{4,5},{5,6},{6,7},{7,4},{8,9},{9,10},{10,1... | collective-permute-start | bytes 491528 | tf_op jit(solution)/shard_map/ppermute | solution.py:613
  7.4 8.4 %collective-permute-start.5 = (f32[5,64,128]{2,1,0:T(8,128)S(1)}, f32[5,64,128]{2,1,0:T(8,128)S(1)}, u32[]{:S(2)}, u32[]{:S(2)}) collective-permute-start(f32[5,64,128]{2,1,0:T(8,128)S(1)} %get-tuple-element.35), channel_id=1, source_target_pairs={{1,0},{2,1},{3,2},{0,3},{5,4},{6,5},{7,6},{4,7},{9,8},{10,9},{11,1... | collective-permute-start | bytes 491528 | tf_op jit(solution)/shard_map/ppermute | solution.py:614
  8.9 5.9 %collective-permute-start.6 = (f32[40,128]{1,0:T(8,128)S(1)}, f32[40,128]{1,0:T(8,128)S(1)}, u32[]{:S(2)}, u32[]{:S(2)}) collective-permute-start(f32[40,128]{1,0:T(8,128)S(1)} %shard_map.170), channel_id=1, source_target_pairs={{4,0},{8,4},{12,8},{16,12},{20,16},{24,20},{28,24},{5,1},{9,5},{13... | collective-permute-start | bytes 61448 | tf_op jit(solution)/shard_map/ppermute | solution.py:654
  12.4 3.4 %copy-start.3 = (bf16[768,512]{1,0:T(8,128)(2,1)S(1)}, bf16[768,512]{1,0:T(8,128)(2,1)}, u32[]{:S(2)}) copy-start(bf16[768,512]{1,0:T(8,128)(2,1)} %constant.30.clone.low_ref) | copy-start | bytes 2359300
  12.4 3.4 %copy-start.4 = (bf16[768,512]{1,0:T(8,128)(2,1)S(1)}, bf16[768,512]{1,0:T(8,128)(2,1)}, u32[]{:S(2)}) copy-start(bf16[768,512]{1,0:T(8,128)(2,1)} %constant.29.clone.high_ref) | copy-start | bytes 2359300
  12.4 3.4 %copy-start.7 = (bf16[128,512]{1,0:T(8,128)(2,1)S(1)}, bf16[128,512]{1,0:T(8,128)(2,1)}, u32[]{:S(2)}) copy-start(bf16[128,512]{1,0:T(8,128)(2,1)} %constant.32.clone.shift_low_ref) | copy-start | bytes 393220
  12.4 3.4 %copy-start.8 = (bf16[128,512]{1,0:T(8,128)(2,1)S(1)}, bf16[128,512]{1,0:T(8,128)(2,1)}, u32[]{:S(2)}) copy-start(bf16[128,512]{1,0:T(8,128)(2,1)} %constant.31.clone.shift_high_ref) | copy-start | bytes 393220
  12.4 3.4 %copy-start.11 = (f32[4,2,4,128]{3,2,1,0:T(4,128)S(1)}, f32[4,2,4,128]{3,2,1,0:T(4,128)}, u32[]{:S(2)}) copy-start(f32[4,2,4,128]{3,2,1,0:T(4,128)} %constant.33.clone.phase_ref.refs_10_) | copy-start | bytes 49156
  16.9 2.7 %collective-permute-start.7 = (f32[40,128]{1,0:T(8,128)S(1)}, f32[40,128]{1,0:T(8,128)S(1)}, u32[]{:S(2)}, u32[]{:S(2)}) collective-permute-start(f32[40,128]{1,0:T(8,128)S(1)} %get-tuple-element.45), channel_id=1, source_target_pairs={{0,1},{1,0},{2,3},{3,2},{4,5},{5,4},{6,7},{7,6},{8,9},{9,8},{10,11... | collective-permute-start | bytes 61448 | tf_op jit(solution)/shard_map/ppermute | solution.py:689
  17.9 3.2 %collective-permute-start.9 = (f32[40,128]{1,0:T(8,128)S(1)}, f32[40,128]{1,0:T(8,128)S(1)}, u32[]{:S(2)}, u32[]{:S(2)}) collective-permute-start(f32[40,128]{1,0:T(8,128)S(1)} %get-tuple-element.46), channel_id=1, source_target_pairs={{0,3},{1,2},{2,1},{3,0},{4,7},{5,6},{6,5},{7,4},{8,11},{9,10},{10,... | collective-permute-start | bytes 61448 | tf_op jit(solution)/shard_map/ppermute | solution.py:689
  19.5 3.8 %collective-permute-start.8 = (f32[40,128]{1,0:T(8,128)S(1)}, f32[40,128]{1,0:T(8,128)S(1)}, u32[]{:S(2)}, u32[]{:S(2)}) collective-permute-start(f32[40,128]{1,0:T(8,128)S(1)} %get-tuple-element.47), channel_id=1, source_target_pairs={{0,2},{1,3},{2,0},{3,1},{4,6},{5,7},{6,4},{7,5},{8,10},{9,11},{10,... | collective-permute-start | bytes 61448 | tf_op jit(solution)/shard_map/ppermute | solution.py:689
  24.0 12.9 %all-to-all-start = ((f32[8,40,128]{2,1,0:T(8,128)}), f32[8,40,128]{2,1,0:T(8,128)S(1)}, u32[]{:S(2)}, u32[]{:S(2)}) async-start(f32[8,40,128]{2,1,0:T(8,128)} %broadcast_in_dim.6), calls=%async_computation | async-start | bytes 327680 | tf_op jit(solution)/shard_map/all_to_all | solution.py:696
  29.3 7.6 %copy-start.13 = (f32[4,2,8,128]{3,2,1,0:T(8,128)S(1)}, f32[4,2,8,128]{3,2,1,0:T(8,128)}, u32[]{:S(2)}) copy-start(f32[4,2,8,128]{3,2,1,0:T(8,128)} %constant.34.clone.symbol_ref) | copy-start | bytes 98308
  29.3 7.6 %copy-start.15 = (f32[8,128]{1,0:T(8,128)S(1)}, f32[8,128]{1,0:T(8,128)}, u32[]{:S(2)}) copy-start(f32[8,128]{1,0:T(8,128)} %constant.35.clone.share_ref) | copy-start | bytes 12292
  29.4 9.6 %collective-permute-start.14 = (f32[5,64,128]{2,1,0:T(8,128)S(1)}, f32[5,64,128]{2,1,0:T(8,128)S(1)}, u32[]{:S(2)}, u32[]{:S(2)}) collective-permute-start(f32[5,64,128]{2,1,0:T(8,128)S(1)} %get-tuple-element.43), channel_id=1, source_target_pairs={{1,0},{2,1},{3,2},{0,3},{5,4},{6,5},{7,6},{4,7},{9,8},{10,9},{11,1... | collective-permute-start | bytes 491528 | tf_op jit(solution)/shard_map/ppermute | solution.py:614
  29.4 9.5 %collective-permute-start.13 = (f32[5,64,128]{2,1,0:T(8,128)S(1)}, f32[5,64,128]{2,1,0:T(8,128)S(1)}, u32[]{:S(2)}, u32[]{:S(2)}) collective-permute-start(f32[5,64,128]{2,1,0:T(8,128)S(1)} %get-tuple-element.44), channel_id=1, source_target_pairs={{0,1},{1,2},{2,3},{3,0},{4,5},{5,6},{6,7},{7,4},{8,9},{9,10},{10,1... | collective-permute-start | bytes 491528 | tf_op jit(solution)/shard_map/ppermute | solution.py:613
  37.1 3.3 %collective-permute-start.12 = (f32[48,128]{1,0:T(8,128)S(1)}, f32[48,128]{1,0:T(8,128)S(1)}, u32[]{:S(2)}, u32[]{:S(2)}) collective-permute-start(f32[48,128]{1,0:T(8,128)S(1)} %shard_map.172.refs_0_), channel_id=1, source_target_pairs={{0,3},{1,2},{2,1},{3,0},{4,7},{5,6},{6,5},{7,4},{8,11},{9,10},{10,... | collective-permute-start | bytes 73736 | tf_op jit(solution)/shard_map/ppermute | solution.py:706
  37.1 3.9 %collective-permute-start.11 = (f32[48,128]{1,0:T(8,128)S(1)}, f32[48,128]{1,0:T(8,128)S(1)}, u32[]{:S(2)}, u32[]{:S(2)}) collective-permute-start(f32[48,128]{1,0:T(8,128)S(1)} %shard_map.172.refs_0_), channel_id=1, source_target_pairs={{0,2},{1,3},{2,0},{3,1},{4,6},{5,7},{6,4},{7,5},{8,10},{9,11},{10,... | collective-permute-start | bytes 73736 | tf_op jit(solution)/shard_map/ppermute | solution.py:706
  37.7 3.3 %collective-permute-start.10 = (f32[48,128]{1,0:T(8,128)S(1)}, f32[48,128]{1,0:T(8,128)S(1)}, u32[]{:S(2)}, u32[]{:S(2)}) collective-permute-start(f32[48,128]{1,0:T(8,128)S(1)} %shard_map.172.refs_0_), channel_id=1, source_target_pairs={{0,1},{1,0},{2,3},{3,2},{4,5},{5,4},{6,7},{7,6},{8,9},{9,8},{10,11... | collective-permute-start | bytes 73736 | tf_op jit(solution)/shard_map/ppermute | solution.py:706
  38.9 2.0 %copy-start.5 = (bf16[512,512]{1,0:T(8,128)(2,1)S(1)}, bf16[512,512]{1,0:T(8,128)(2,1)}, u32[]{:S(2)}) copy-start(bf16[512,512]{1,0:T(8,128)(2,1)} %constant.37.clone.refs_8_) | copy-start | bytes 1572868
  39.0 2.0 %copy-start.6 = (bf16[512,512]{1,0:T(8,128)(2,1)S(1)}, bf16[512,512]{1,0:T(8,128)(2,1)}, u32[]{:S(2)}) copy-start(bf16[512,512]{1,0:T(8,128)(2,1)} %constant.36.clone.refs_7_) | copy-start | bytes 1572868
  39.0 2.0 %copy-start.14 = (bf16[48,128]{1,0:T(8,128)(2,1)S(1)}, bf16[48,128]{1,0:T(8,128)(2,1)}, u32[]{:S(2)}) copy-start(bf16[48,128]{1,0:T(8,128)(2,1)} %constant.38.clone.refs_9_) | copy-start | bytes 36868

commit v7 on v5

--- a/solution.py
+++ b/solution.py
@@ -71,7 +71,9 @@
     c, s = np.cos(theta), np.sin(theta)
     real = np.concatenate([c, -s], axis=2).reshape(count, -1).T
     imag = np.concatenate([s, c], axis=2).reshape(count, -1).T
-    tables["yzinverse"] = hi_lo(np.concatenate([real, imag], axis=1))
+    both = np.concatenate([real, imag], axis=1)
+    both[np.arange(both.shape[0]) % (2 * keep_y) == keep_y] = 0.0
+    tables["yzinverse"] = hi_lo(both)
     place = np.arange(width).reshape(-1, 1, 1, 1)
     theta = turn * ((kz.reshape(1, width, slab, 1) * place) % width) / width
     theta = np.broadcast_to(theta, (width, width, slab, 2 * keep_y)).reshape(width, width, half)
@@ -450,7 +452,7 @@
         out_ref[step_between(place, group, width)] = turned
 
 
-def coarse_kernel(jump_ref, symbol_ref, share_ref, out_ref, kept_ref):
+def coarse_kernel(jump_ref, symbol_ref, share_ref, out_ref, kept_ref, *, plane):
     slices, lines, lanes = jump_ref.shape
     keep = share_ref.shape[0]
     fields = lines // keep
@@ -476,12 +478,16 @@
             swapped = pltpu.roll(jump, lanes // 2, 1) + current[f][1]
             current[f] = (value * real + swapped * imag, swapped * real - value * imag)
             kept_ref[moment_id + 1, f * keep : (f + 1) * keep, :] = current[f][0]
-    out_ref[:lines, :] = kept_ref[moment]
     sums = jnp.sum(jnp.concatenate(sizes), axis=1, keepdims=True)
-    spare = out_ref.shape[0] - lines - slices
-    if spare > 0:
-        out_ref[lines + slices :, :] = jnp.zeros((spare, lanes), jnp.float32)
-    out_ref[lines : lines + slices, :] = jnp.broadcast_to(sums, (slices, lanes))
+    lane = lax.broadcasted_iota(jnp.int32, (lines, lanes), 1)
+    message = kept_ref[moment]
+    for chunk in range(-(-slices // lines)):
+        column = sums[chunk * lines : (chunk + 1) * lines]
+        spare = lines - column.shape[0]
+        if spare > 0:
+            column = jnp.concatenate([column, jnp.zeros((spare, 1), jnp.float32)])
+        message = jnp.where(lane == chunk * plane + plane // 2, column, message)
+    out_ref[...] = message
 
 
 def uncorrected_kernel(fine_ref, below_ref, above_ref, ends_ref, held_ref, sems):
@@ -504,7 +510,7 @@
             copy.wait()
 
 
-def inverse_kernel(*refs, width, scales):
+def inverse_kernel(*refs, width, slices, plane, scales):
     block_refs = refs[:width]
     (
         fine_ref,
@@ -520,7 +526,8 @@
         total_ref,
         order_ref,
         held_ref,
-        norm_refs,
+        own_norm_ref,
+        whole_norm_ref,
         sems,
         norm_sems,
     ) = refs[width:]
@@ -530,17 +537,23 @@
     lines, lanes = order_ref.shape[1:]
     keep = lines // fields
 
-    sums = block_refs[0][lines:, :]
+    total = block_refs[0][...]
     for step in range(1, width):
-        sums = sums + block_refs[step][lines:, :]
-    line = lax.broadcasted_iota(jnp.int32, sums.shape, 0)
-    own = jnp.sum(jnp.where(line == moment, sums, 0.0), axis=0, keepdims=True)
-    whole = jnp.sum(sums, axis=0, keepdims=True)
-    norm_refs[0, 0] = jnp.sqrt(own * scales[0] + epsilon)[0, 0]
-    norm_refs[1, 0] = jnp.sqrt(whole * scales[1] + epsilon)[0, 0]
+        total = total + block_refs[step][...]
+    line = lax.broadcasted_iota(jnp.int32, (lines, 1), 0)
+    lane = lax.broadcasted_iota(jnp.int32, (lines, lanes), 1)
+    own, whole = jnp.zeros((1, 1), jnp.float32), jnp.zeros((1, 1), jnp.float32)
+    for chunk in range(-(-slices // lines)):
+        spot = lane == chunk * plane + plane // 2
+        column = jnp.sum(jnp.where(spot, total, 0.0), axis=1, keepdims=True)
+        here = jnp.where(line + chunk * lines == moment, column, 0.0)
+        own = own + jnp.sum(here, axis=0, keepdims=True)
+        whole = whole + jnp.sum(column, axis=0, keepdims=True)
+    own_norm_ref[...] = jnp.sqrt(own * scales[0] + epsilon)
+    whole_norm_ref[...] = jnp.sqrt(whole * scales[1] + epsilon)
     norms = [
-        pltpu.make_async_copy(norm_refs.at[side], out_ref, norm_sems.at[side])
-        for side, out_ref in enumerate((slice_ref, total_ref))
+        pltpu.make_async_copy(own_norm_ref, slice_ref, norm_sems.at[0]),
+        pltpu.make_async_copy(whole_norm_ref, total_ref, norm_sems.at[1]),
     ]
     for copy in norms:
         copy.start()
@@ -549,7 +562,7 @@
     def _():
         for step in range(width):
             group = source_of(place, step, width)
-            block = block_refs[step][:lines, :]
+            block = block_refs[step][...]
             order_ref[group] = (
                 block * phase_ref[place, 0, group, :][None, :]
                 - pltpu.roll(block, lanes // 2, 1) * phase_ref[place, 1, group, :][None, :]
@@ -665,8 +678,8 @@
     jumps = lax.all_to_all(jnp.broadcast_to(jump, (slices, lines, lanes)), "tm", 0, 0, tiled=True)
 
     message = local_call(
-        coarse_kernel,
-        jax.ShapeDtypeStruct((lines + -(-slices // 8) * 8, lanes), real),
+        functools.partial(coarse_kernel, plane=2 * keep_y),
+        jax.ShapeDtypeStruct((lines, lanes), real),
         [jumps, tables["symbol"], tables["share"]],
         [pltpu.VMEM((slices, lines, lanes), real)],
     )
@@ -687,12 +700,12 @@
     cells = fields * depth * rows * cols
     ends, slice_norm, total_norm = local_call(
         functools.partial(
-            inverse_kernel, width=width, scales=(1.0 / cells, 1.0 / (cells * slices))
+            inverse_kernel, width=width, slices=slices, plane=2 * keep_y, scales=(1.0 / cells, 1.0 / (cells * slices))
         ),
         (
             jax.ShapeDtypeStruct((fields, slab, rows, cols), real),
-            jax.ShapeDtypeStruct((1,), real),
-            jax.ShapeDtypeStruct((1,), real),
+            jax.ShapeDtypeStruct((1, 1), real),
+            jax.ShapeDtypeStruct((1, 1), real),
         ),
         [
             *blocks,
@@ -707,7 +720,8 @@
         [
             pltpu.VMEM((width, lines, lanes), real),
             whole_slab,
-            pltpu.SMEM((2, 1), real),
+            pltpu.VMEM((1, 1), real),
+            pltpu.VMEM((1, 1), real),
             pltpu.SemaphoreType.DMA((fields,)),
             pltpu.SemaphoreType.DMA((2,)),
         ],
@@ -715,7 +729,7 @@
         out_specs=(off_chip, off_chip, off_chip),
         aliases={width + 7: 0},
     )
-    return ends[None], slice_norm, total_norm
+    return ends[None], slice_norm[0], total_norm[0]
 
 
 def solution(mesh):

time: 42 us -> 42 us (level)
  no operation moved by 1% of the time
where the time goes in v7:
time: 42 us; the launch traced here: 41.7 us
  starting transfers between devices  17.5 us (42%)
  waiting for transfers between devices  15.3 us (36%)
  Pallas kernels  5.61 us (13%)
  local copies, waits for them, and re-layouts  2.55 us (6%)
  between operations  0.79 us (2%)
    all_to_all x1, waiting for transfers between devices, shards(): lax.all_to_all(jnp.broadcast_to(jump, (slices, lines, lanes)), 'tm', 0, 0...  6.95 us
    ppermute x8, starting transfers between devices, halo(): return (lax.ppermute(up, 'space', ups), lax.ppermute(down, 'space', downs))  6.62 us
    pallas_call x8, Pallas kernels, local_call(): pl.pallas_call(kernel, out_shape=out_shape, in_specs=specs, out_specs=out...  5.61 us
    all_to_all x1, starting transfers between devices, shards(): lax.all_to_all(jnp.broadcast_to(jump, (slices, lines, lanes)), 'tm', 0, 0...  5.44 us
    ppermute x3, waiting for transfers between devices, shards(): lax.ppermute(waves[step], 'space', [(i, target_of(i, step, width)) for i...  3.74 us
    ppermute x1, waiting for transfers between devices, shards(): lax.ppermute(start_waves, 'tm', [(i + 1, i) for i in range(slices - 1)])  2.37 us
    ppermute x3, starting transfers between devices, shards(): lax.ppermute(waves[step], 'space', [(i, target_of(i, step, width)) for i...  2.27 us
    ppermute x3, starting transfers between devices, shards(): lax.ppermute(message, 'space', [(i, target_of(i, step, width)) for i in r...  1.87 us
  transfers between devices with their start and end apart: 16, of which 8 were waited for; matrix products, arithmetic and copies ran while one was open for 0% of the time, Pallas kernels for 9%

profile of v7, /device:TPU:0, one launch (start us, length us, event | category | flops | bytes accessed | tf_op | source)
XLA Modules:
  0.0 41.7 jit_solution(13156296760231835472)
XLA Ops:
  0.6 0.0 copy-start
  0.6 1.1 %copy-done = f32[1,5,4,64,128]{4,3,2,1,0:T(8,128)S(1)} copy-done((f32[1,5,4,64,128]{4,3,2,1,0:T(8,128)S(1)}, f32[1,5,4,64,128]{4,3,2,1,0:T(8,128)}, u32[]{:S(2)}) %copy-start) | copy-done | bytes 655384
  1.7 0.0 copy-start.1
  1.7 0.5 %collective-permute-start = (f32[5,64,128]{2,1,0:T(8,128)S(1)}, f32[5,64,128]{2,1,0:T(8,128)S(1)}, u32[]{:S(2)}, u32[]{:S(2)}) collective-permute-start(f32[5,64,128]{2,1,0:T(8,128)S(1)} %get-tuple-element.24), channel_id=1, source_target_pairs={{0,1},{1,2},{2,3},{3,0},{4,5},{5,6},{6,7},{7,4},{8,9},{9,10},{10,1... | collective-permute-start | bytes 491528 | tf_op jit(solution)/shard_map/ppermute | solution.py:603
  2.3 2.0 %collective-permute-start.1 = (f32[5,64,128]{2,1,0:T(8,128)S(1)}, f32[5,64,128]{2,1,0:T(8,128)S(1)}, u32[]{:S(2)}, u32[]{:S(2)}) collective-permute-start(f32[5,64,128]{2,1,0:T(8,128)S(1)} %get-tuple-element.25), channel_id=1, source_target_pairs={{1,0},{2,1},{3,2},{0,3},{5,4},{6,5},{7,6},{4,7},{9,8},{10,9},{11,1... | collective-permute-start | bytes 491528 | tf_op jit(solution)/shard_map/ppermute | solution.py:603
  4.3 0.0 copy-done.1
  4.3 0.0 copy-start.7
  4.3 0.7 %copy-done.7 = bf16[32,256]{1,0:T(8,128)(2,1)S(1)} copy-done((bf16[32,256]{1,0:T(8,128)(2,1)S(1)}, bf16[32,256]{1,0:T(8,128)(2,1)}, u32[]{:S(2)}) %copy-start.7) | copy-done | bytes 16408
  5.0 0.7 %shard_map.130 = (f32[5,4,64,128]{3,2,1,0:T(8,128)S(1)}, f32[40,512]{1,0:T(8,128)S(1)}, f32[5,64,128]{2,1,0:T(8,128)S(1)}, f32[5,64,128]{2,1,0:T(8,128)S(1)}, f3...) custom-call(f32[5,4,64,128]{3,2,1,0:T(8,128)S(1)} %bitcast.21, f32[5,4,64,128]{3,2,1,0:T(8,128)S(1)} %copy-done.1, ...), custom_call_target="tpu_custom_call" | custom-call | tf_op jit(solution)/shard_map/pallas_call | solution.py:131
  5.7 0.7 %collective-permute-start.2 = (f32[5,64,128]{2,1,0:T(8,128)S(1)}, f32[5,64,128]{2,1,0:T(8,128)S(1)}, u32[]{:S(2)}, u32[]{:S(2)}) collective-permute-start(f32[5,64,128]{2,1,0:T(8,128)S(1)} %get-tuple-element.28), channel_id=1, source_target_pairs={{0,1},{1,2},{2,3},{3,0},{4,5},{5,6},{6,7},{7,4},{8,9},{9,10},{10,1... | collective-permute-start | bytes 491528 | tf_op jit(solution)/shard_map/ppermute | solution.py:603
  6.3 1.1 %collective-permute-start.3 = (f32[5,64,128]{2,1,0:T(8,128)S(1)}, f32[5,64,128]{2,1,0:T(8,128)S(1)}, u32[]{:S(2)}, u32[]{:S(2)}) collective-permute-start(f32[5,64,128]{2,1,0:T(8,128)S(1)} %get-tuple-element.29), channel_id=1, source_target_pairs={{1,0},{2,1},{3,2},{0,3},{5,4},{6,5},{7,6},{4,7},{9,8},{10,9},{11,1... | collective-permute-start | bytes 491528 | tf_op jit(solution)/shard_map/ppermute | solution.py:603
  7.5 0.6 %collective-permute-start.4 = (f32[5,64,128]{2,1,0:T(8,128)S(1)}, f32[5,64,128]{2,1,0:T(8,128)S(1)}, u32[]{:S(2)}, u32[]{:S(2)}) collective-permute-start(f32[5,64,128]{2,1,0:T(8,128)S(1)} %get-tuple-element.34), channel_id=1, source_target_pairs={{0,1},{1,2},{2,3},{3,0},{4,5},{5,6},{6,7},{7,4},{8,9},{9,10},{10,1... | collective-permute-start | bytes 491528 | tf_op jit(solution)/shard_map/ppermute | solution.py:603
  8.1 0.0 collective-permute-done.below_ref
  8.1 1.1 %collective-permute-start.5 = (f32[5,64,128]{2,1,0:T(8,128)S(1)}, f32[5,64,128]{2,1,0:T(8,128)S(1)}, u32[]{:S(2)}, u32[]{:S(2)}) collective-permute-start(f32[5,64,128]{2,1,0:T(8,128)S(1)} %get-tuple-element.35), channel_id=1, source_target_pairs={{1,0},{2,1},{3,2},{0,3},{5,4},{6,5},{7,6},{4,7},{9,8},{10,9},{11,1... | collective-permute-start | bytes 491528 | tf_op jit(solution)/shard_map/ppermute | solution.py:603
  9.2 0.0 collective-permute-done.1.above_ref
  9.2 1.3 %collective-permute-start.6 = (f32[40,512]{1,0:T(8,128)S(1)}, f32[40,512]{1,0:T(8,128)S(1)}, u32[]{:S(2)}, u32[]{:S(2)}) collective-permute-start(f32[40,512]{1,0:T(8,128)S(1)} %get-tuple-element.36), channel_id=1, source_target_pairs={{4,0},{8,4},{12,8},{16,12},{20,16},{24,20},{28,24},{5,1},{9,5},{13... | collective-permute-start | bytes 245768 | tf_op jit(solution)/shard_map/ppermute | solution.py:637
  10.5 0.6 %shard_map.132 = (f32[5,4,64,128]{3,2,1,0:T(8,128)S(1)}, f32[5,4,64,128]{3,2,1,0:T(8,128)S(1)}) custom-call(f32[5,4,64,128]{3,2,1,0:T(8,128)S(1)} %bitcast.22, f32[5,4,64,128]{3,2,1,0:T(8,128)S(1)} %get-tuple-element.23.rate_ref, f32[5,4,64,128]{3,2,1,0:T(8,128)S(1)} %copy-done.1, f32[5,64,128]{2,1,0:T(8,128)S(1)} %collective-permute-done.below_ref, ...), custom_call_target="tpu_custom_call" | custom-call | tf_op jit(solution)/shard_map/pallas_call | solution.py:131
  11.2 0.7 %collective-permute-done.2.below_rate_ref = f32[5,64,128]{2,1,0:T(8,128)S(1)} collective-permute-done((f32[5,64,128]{2,1,0:T(8,128)S(1)}, f32[5,64,128]{2,1,0:T(8,128)S(1)}, u32[]{:S(2)}, u32[]{:S(2)}) %collective-permute-start.2) | collective-permute-done | bytes 163872 | tf_op jit(solution)/shard_map/ppermute | solution.py:603
  11.9 0.5 %collective-permute-done.3.above_rate_ref = f32[5,64,128]{2,1,0:T(8,128)S(1)} collective-permute-done((f32[5,64,128]{2,1,0:T(8,128)S(1)}, f32[5,64,128]{2,1,0:T(8,128)S(1)}, u32[]{:S(2)}, u32[]{:S(2)}) %collective-permute-start.3) | collective-permute-done | bytes 163872 | tf_op jit(solution)/shard_map/ppermute | solution.py:603
  12.4 0.0 copy-start.2
  12.4 0.0 copy-start.3
  12.4 0.0 copy-start.6
  12.4 0.0 copy-start.8
  12.4 1.4 %shard_map.133 = (f32[2,5,64,128]{3,2,1,0:T(8,128)S(1)}, f32[2,5,64,128]{3,2,1,0:T(8,128)S(1)}, f32[2,5,64,128]{3,2,1,0:T(8,128)S(1)}, f32[5,2,64,128]{3,2,1,0:T(8,128)S(1)}) custom-call(f32[5,4,64,128]{3,2,1,0:T(8,128)S(1)} %bitcast.23, f32[5,4,64,128]{3,2,1,0:T(8,128)S(1)} %get-tuple-element.26.second_ref, ...), custom_call_target="tpu_custom_call" | custom-call | tf_op jit(solution)/shard_map/pallas_call | solution.py:131
  13.8 2.4 %collective-permute-done.6.shifted_ref = f32[40,512]{1,0:T(8,128)S(1)} collective-permute-done((f32[40,512]{1,0:T(8,128)S(1)}, f32[40,512]{1,0:T(8,128)S(1)}, u32[]{:S(2)}, u32[]{:S(2)}) %collective-permute-start.6) | collective-permute-done | bytes 81952 | tf_op jit(solution)/shard_map/ppermute | solution.py:637
  16.1 0.0 collective-permute-done.4.below_ref
  16.2 0.0 collective-permute-done.5.above_ref
  16.2 0.0 copy-done.2
  16.2 0.0 copy-done.3
  16.2 0.0 copy-done.6
  16.2 0.0 copy-done.8
  16.2 1.0 %shard_map.134 = (f32[4,40,128]{2,1,0:T(8,128)S(1)}, f32[5,4,64,128]{3,2,1,0:T(8,128)S(1)}, f32[2,5,64,128]{3,2,1,0:T(8,128)S(1)}) custom-call(f32[5,4,64,128]{3,2,1,0:T(8,128)S(1)} %bitcast.24, f32[2,5,64,128]{3,2,1,0:T(8,128)S(1)} %get-tuple-element.30.base_ref, f32[2,5,64,128]{3,2,1,0:T(8,128)S(1)} %get-tuple-element.31.edge_rate_ref, ...), custom_call_target="tpu_custom_call" | custom-call | tf_op jit(solution)/shard_map/pallas_call | solution.py:131
  17.2 0.5 %collective-permute-start.7 = (f32[40,128]{1,0:T(8,128)S(1)}, f32[40,128]{1,0:T(8,128)S(1)}, u32[]{:S(2)}, u32[]{:S(2)}) collective-permute-start(f32[40,128]{1,0:T(8,128)S(1)} %get-tuple-element.45), channel_id=1, source_target_pairs={{0,1},{1,0},{2,3},{3,2},{4,5},{5,4},{6,7},{7,6},{8,9},{9,8},{10,11... | collective-permute-start | bytes 61448 | tf_op jit(solution)/shard_map/ppermute | solution.py:671
  17.8 1.7 %collective-permute-start.9 = (f32[40,128]{1,0:T(8,128)S(1)}, f32[40,128]{1,0:T(8,128)S(1)}, u32[]{:S(2)}, u32[]{:S(2)}) collective-permute-start(f32[40,128]{1,0:T(8,128)S(1)} %get-tuple-element.46), channel_id=1, source_target_pairs={{0,3},{1,2},{2,1},{3,0},{4,7},{5,6},{6,5},{7,4},{8,11},{9,10},{10,... | collective-permute-start | bytes 61448 | tf_op jit(solution)/shard_map/ppermute | solution.py:671
  19.4 0.0 collective-permute-start.8
  19.5 0.0 collective-permute-done.7
  19.5 1.5 %collective-permute-done.9 = f32[40,128]{1,0:T(8,128)S(1)} collective-permute-done((f32[40,128]{1,0:T(8,128)S(1)}, f32[40,128]{1,0:T(8,128)S(1)}, u32[]{:S(2)}, u32[]{:S(2)}) %collective-permute-start.9) | collective-permute-done | bytes 20512 | tf_op jit(solution)/shard_map/ppermute | solution.py:671
  21.0 2.3 %collective-permute-done.8 = f32[40,128]{1,0:T(8,128)S(1)} collective-permute-done((f32[40,128]{1,0:T(8,128)S(1)}, f32[40,128]{1,0:T(8,128)S(1)}, u32[]{:S(2)}, u32[]{:S(2)}) %collective-permute-start.8) | collective-permute-done | bytes 20512 | tf_op jit(solution)/shard_map/ppermute | solution.py:671
  23.2 0.7 %broadcast_in_dim.6 = f32[8,40,128]{2,1,0:T(8,128)} broadcast(f32[40,128]{1,0:T(8,128)S(1)} %fusion.1), dimensions={1,2} | broadcast | bytes 184320 | tf_op jit(solution)/shard_map/broadcast_in_dim | solution.py:678
  23.9 5.4 %all-to-all-start = ((f32[8,40,128]{2,1,0:T(8,128)}), f32[8,40,128]{2,1,0:T(8,128)S(1)}, u32[]{:S(2)}, u32[]{:S(2)}) async-start(f32[8,40,128]{2,1,0:T(8,128)} %broadcast_in_dim.6), calls=%async_computation | async-start | bytes 327680 | tf_op jit(solution)/shard_map/all_to_all | solution.py:678
  29.4 0.0 copy-start.9
  29.4 0.0 copy-start.11
  29.4 0.1 collective-permute-start.14
  29.5 0.5 %collective-permute-start.13 = (f32[5,64,128]{2,1,0:T(8,128)S(1)}, f32[5,64,128]{2,1,0:T(8,128)S(1)}, u32[]{:S(2)}, u32[]{:S(2)}) collective-permute-start(f32[5,64,128]{2,1,0:T(8,128)S(1)} %get-tuple-element.44), channel_id=1, source_target_pairs={{0,1},{1,2},{2,3},{3,0},{4,5},{5,6},{6,7},{7,4},{8,9},{9,10},{10,1... | collective-permute-start | bytes 491528 | tf_op jit(solution)/shard_map/ppermute | solution.py:603
  30.0 7.0 %all-to-all-done.jump_ref = f32[8,40,128]{2,1,0:T(8,128)S(1)} async-done(((f32[8,40,128]{2,1,0:T(8,128)}), f32[8,40,128]{2,1,0:T(8,128)S(1)}, u32[]{:S(2)}, u32[]{:S(2)}) %all-to-all-start) | async-done | bytes 163872 | tf_op jit(solution)/shard_map/all_to_all | solution.py:678
  36.9 0.0 copy-done.9
  36.9 0.0 copy-done.11
  36.9 0.3 shard_map.135.refs_0_
  37.2 0.0 collective-permute-start.12
  37.2 0.6 %collective-permute-start.11 = (f32[40,128]{1,0:T(8,128)S(1)}, f32[40,128]{1,0:T(8,128)S(1)}, u32[]{:S(2)}, u32[]{:S(2)}) collective-permute-start(f32[40,128]{1,0:T(8,128)S(1)} %shard_map.135.refs_0_), channel_id=1, source_target_pairs={{0,2},{1,3},{2,0},{3,1},{4,6},{5,7},{6,4},{7,5},{8,10},{9,11},{10,... | collective-permute-start | bytes 61448 | tf_op jit(solution)/shard_map/ppermute | solution.py:688
  37.8 1.3 %collective-permute-start.10 = (f32[40,128]{1,0:T(8,128)S(1)}, f32[40,128]{1,0:T(8,128)S(1)}, u32[]{:S(2)}, u32[]{:S(2)}) collective-permute-start(f32[40,128]{1,0:T(8,128)S(1)} %shard_map.135.refs_0_), channel_id=1, source_target_pairs={{0,1},{1,0},{2,3},{3,2},{4,5},{5,4},{6,7},{7,6},{8,9},{9,8},{10,11... | collective-permute-start | bytes 61448 | tf_op jit(solution)/shard_map/ppermute | solution.py:688
  39.1 0.0 collective-permute-done.14.above_ref.refs_6_
  39.1 0.0 collective-permute-done.13.below_ref.refs_5_
  39.1 0.0 copy-start.4
  39.1 0.0 copy-start.5
  39.1 0.0 copy-start.10
  39.1 0.9 %shard_map.136.refs_11_ = f32[5,4,64,128]{3,2,1,0:T(8,128)} custom-call(f32[5,4,64,128]{3,2,1,0:T(8,128)S(1)} %get-tuple-element.38.fine_ref.refs_4_, f32[5,64,128]{2,1,0:T(8,128)S(1)} %collective-permute-done.13.below_ref.refs_5_, f32[5,64,128]{2,1,0:T(8,128)S(1)} %collective-permute-done.14.above_ref.refs_6_), custom_call_target="tpu_custom_call" | custom-call | tf_op jit(solution)/shard_map/pallas_call | solution.py:131
  40.0 0.4 collective-permute-done.12.refs_3_
  40.4 0.6 %collective-permute-done.11.refs_2_ = f32[40,128]{1,0:T(8,128)S(1)} collective-permute-done((f32[40,128]{1,0:T(8,128)S(1)}, f32[40,128]{1,0:T(8,128)S(1)}, u32[]{:S(2)}, u32[]{:S(2)}) %collective-permute-start.11) | collective-permute-done | bytes 20512 | tf_op jit(solution)/shard_map/ppermute | solution.py:688
  41.0 0.0 collective-permute-done.10.refs_1_
  41.0 0.0 copy-done.4
  41.0 0.0 copy-done.5
  41.0 0.0 copy-done.10
  41.0 0.7 %shard_map.137 = (f32[5,4,64,128]{3,2,1,0:T(8,128)}, f32[1,1]{1,0:T(1,128)}, f32[1,1]{1,0:T(1,128)}) custom-call(f32[40,128]{1,0:T(8,128)S(1)} %shard_map.135.refs_0_, f32[40,128]{1,0:T(8,128)S(1)} %collective-permute-done.10.refs_1_, f32[40,128]{1,0:T(8,128)S(1)} %collective-permute-done.11.refs_2_, ...), custom_call_target="tpu_custom_call", output_to_operand_aliasing={{0}: (11, {})} | custom-call | tf_op jit(solution)/shard_map/pallas_call | solution.py:131
  (4 shorter events, 0.1 us)
Async XLA Ops:
  0.6 1.1 %copy-start = (f32[1,5,4,64,128]{4,3,2,1,0:T(8,128)S(1)}, f32[1,5,4,64,128]{4,3,2,1,0:T(8,128)}, u32[]{:S(2)}) copy-start(f32[1,5,4,64,128]{4,3,2,1,0:T(8,128)} %param.11) | copy-start | bytes 1966084
  1.7 2.6 %copy-start.1 = (f32[5,4,64,128]{3,2,1,0:T(8,128)S(1)}, f32[5,4,64,128]{3,2,1,0:T(8,128)}, u32[]{:S(2)}) copy-start(f32[5,4,64,128]{3,2,1,0:T(8,128)} %source_ref.5) | copy-start | bytes 1966084
  1.7 6.4 %collective-permute-start = (f32[5,64,128]{2,1,0:T(8,128)S(1)}, f32[5,64,128]{2,1,0:T(8,128)S(1)}, u32[]{:S(2)}, u32[]{:S(2)}) collective-permute-start(f32[5,64,128]{2,1,0:T(8,128)S(1)} %get-tuple-element.24), channel_id=1, source_target_pairs={{0,1},{1,2},{2,3},{3,0},{4,5},{5,6},{6,7},{7,4},{8,9},{9,10},{10,1... | collective-permute-start | bytes 491528 | tf_op jit(solution)/shard_map/ppermute | solution.py:603
  2.3 6.9 %collective-permute-start.1 = (f32[5,64,128]{2,1,0:T(8,128)S(1)}, f32[5,64,128]{2,1,0:T(8,128)S(1)}, u32[]{:S(2)}, u32[]{:S(2)}) collective-permute-start(f32[5,64,128]{2,1,0:T(8,128)S(1)} %get-tuple-element.25), channel_id=1, source_target_pairs={{1,0},{2,1},{3,2},{0,3},{5,4},{6,5},{7,6},{4,7},{9,8},{10,9},{11,1... | collective-permute-start | bytes 491528 | tf_op jit(solution)/shard_map/ppermute | solution.py:603
  4.3 0.7 %copy-start.7 = (bf16[32,256]{1,0:T(8,128)(2,1)S(1)}, bf16[32,256]{1,0:T(8,128)(2,1)}, u32[]{:S(2)}) copy-start(bf16[32,256]{1,0:T(8,128)(2,1)} %constant.18.clone.table_ref) | copy-start | bytes 49156
  5.7 6.2 %collective-permute-start.2 = (f32[5,64,128]{2,1,0:T(8,128)S(1)}, f32[5,64,128]{2,1,0:T(8,128)S(1)}, u32[]{:S(2)}, u32[]{:S(2)}) collective-permute-start(f32[5,64,128]{2,1,0:T(8,128)S(1)} %get-tuple-element.28), channel_id=1, source_target_pairs={{0,1},{1,2},{2,3},{3,0},{4,5},{5,6},{6,7},{7,4},{8,9},{9,10},{10,1... | collective-permute-start | bytes 491528 | tf_op jit(solution)/shard_map/ppermute | solution.py:603
  6.3 6.0 %collective-permute-start.3 = (f32[5,64,128]{2,1,0:T(8,128)S(1)}, f32[5,64,128]{2,1,0:T(8,128)S(1)}, u32[]{:S(2)}, u32[]{:S(2)}) collective-permute-start(f32[5,64,128]{2,1,0:T(8,128)S(1)} %get-tuple-element.29), channel_id=1, source_target_pairs={{1,0},{2,1},{3,2},{0,3},{5,4},{6,5},{7,6},{4,7},{9,8},{10,9},{11,1... | collective-permute-start | bytes 491528 | tf_op jit(solution)/shard_map/ppermute | solution.py:603
  7.5 8.7 %collective-permute-start.4 = (f32[5,64,128]{2,1,0:T(8,128)S(1)}, f32[5,64,128]{2,1,0:T(8,128)S(1)}, u32[]{:S(2)}, u32[]{:S(2)}) collective-permute-start(f32[5,64,128]{2,1,0:T(8,128)S(1)} %get-tuple-element.34), channel_id=1, source_target_pairs={{0,1},{1,2},{2,3},{3,0},{4,5},{5,6},{6,7},{7,4},{8,9},{9,10},{10,1... | collective-permute-start | bytes 491528 | tf_op jit(solution)/shard_map/ppermute | solution.py:603
  8.1 8.1 %collective-permute-start.5 = (f32[5,64,128]{2,1,0:T(8,128)S(1)}, f32[5,64,128]{2,1,0:T(8,128)S(1)}, u32[]{:S(2)}, u32[]{:S(2)}) collective-permute-start(f32[5,64,128]{2,1,0:T(8,128)S(1)} %get-tuple-element.35), channel_id=1, source_target_pairs={{1,0},{2,1},{3,2},{0,3},{5,4},{6,5},{7,6},{4,7},{9,8},{10,9},{11,1... | collective-permute-start | bytes 491528 | tf_op jit(solution)/shard_map/ppermute | solution.py:603
  9.2 6.9 %collective-permute-start.6 = (f32[40,512]{1,0:T(8,128)S(1)}, f32[40,512]{1,0:T(8,128)S(1)}, u32[]{:S(2)}, u32[]{:S(2)}) collective-permute-start(f32[40,512]{1,0:T(8,128)S(1)} %get-tuple-element.36), channel_id=1, source_target_pairs={{4,0},{8,4},{12,8},{16,12},{20,16},{24,20},{28,24},{5,1},{9,5},{13... | collective-permute-start | bytes 245768 | tf_op jit(solution)/shard_map/ppermute | solution.py:637
  12.4 3.8 %copy-start.2 = (bf16[768,512]{1,0:T(8,128)(2,1)S(1)}, bf16[768,512]{1,0:T(8,128)(2,1)}, u32[]{:S(2)}) copy-start(bf16[768,512]{1,0:T(8,128)(2,1)} %constant.20.clone.low_ref) | copy-start | bytes 2359300
  12.4 3.8 %copy-start.3 = (bf16[768,512]{1,0:T(8,128)(2,1)S(1)}, bf16[768,512]{1,0:T(8,128)(2,1)}, u32[]{:S(2)}) copy-start(bf16[768,512]{1,0:T(8,128)(2,1)} %constant.19.clone.high_ref) | copy-start | bytes 2359300
  12.4 3.8 %copy-start.6 = (f32[4,2,4,128]{3,2,1,0:T(4,128)S(1)}, f32[4,2,4,128]{3,2,1,0:T(4,128)}, u32[]{:S(2)}) copy-start(f32[4,2,4,128]{3,2,1,0:T(4,128)} %constant.21.clone.phase_ref.refs_10_) | copy-start | bytes 49156
  12.4 3.8 %copy-start.8 = (bf16[32,256]{1,0:T(8,128)(2,1)S(1)}, bf16[32,256]{1,0:T(8,128)(2,1)}, u32[]{:S(2)}) copy-start(bf16[32,256]{1,0:T(8,128)(2,1)} %constant.18.clone.table_ref) | copy-start | bytes 49156
  17.2 2.3 %collective-permute-start.7 = (f32[40,128]{1,0:T(8,128)S(1)}, f32[40,128]{1,0:T(8,128)S(1)}, u32[]{:S(2)}, u32[]{:S(2)}) collective-permute-start(f32[40,128]{1,0:T(8,128)S(1)} %get-tuple-element.45), channel_id=1, source_target_pairs={{0,1},{1,0},{2,3},{3,2},{4,5},{5,4},{6,7},{7,6},{8,9},{9,8},{10,11... | collective-permute-start | bytes 61448 | tf_op jit(solution)/shard_map/ppermute | solution.py:671
  17.8 3.2 %collective-permute-start.9 = (f32[40,128]{1,0:T(8,128)S(1)}, f32[40,128]{1,0:T(8,128)S(1)}, u32[]{:S(2)}, u32[]{:S(2)}) collective-permute-start(f32[40,128]{1,0:T(8,128)S(1)} %get-tuple-element.46), channel_id=1, source_target_pairs={{0,3},{1,2},{2,1},{3,0},{4,7},{5,6},{6,5},{7,4},{8,11},{9,10},{10,... | collective-permute-start | bytes 61448 | tf_op jit(solution)/shard_map/ppermute | solution.py:671
  19.4 3.8 %collective-permute-start.8 = (f32[40,128]{1,0:T(8,128)S(1)}, f32[40,128]{1,0:T(8,128)S(1)}, u32[]{:S(2)}, u32[]{:S(2)}) collective-permute-start(f32[40,128]{1,0:T(8,128)S(1)} %get-tuple-element.47), channel_id=1, source_target_pairs={{0,2},{1,3},{2,0},{3,1},{4,6},{5,7},{6,4},{7,5},{8,10},{9,11},{10,... | collective-permute-start | bytes 61448 | tf_op jit(solution)/shard_map/ppermute | solution.py:671
  23.9 13.0 %all-to-all-start = ((f32[8,40,128]{2,1,0:T(8,128)}), f32[8,40,128]{2,1,0:T(8,128)S(1)}, u32[]{:S(2)}, u32[]{:S(2)}) async-start(f32[8,40,128]{2,1,0:T(8,128)} %broadcast_in_dim.6), calls=%async_computation | async-start | bytes 327680 | tf_op jit(solution)/shard_map/all_to_all | solution.py:678
  29.4 7.6 %copy-start.9 = (f32[4,2,8,128]{3,2,1,0:T(8,128)S(1)}, f32[4,2,8,128]{3,2,1,0:T(8,128)}, u32[]{:S(2)}) copy-start(f32[4,2,8,128]{3,2,1,0:T(8,128)} %constant.22.clone.symbol_ref) | copy-start | bytes 98308
  29.4 7.6 %copy-start.11 = (f32[8,128]{1,0:T(8,128)S(1)}, f32[8,128]{1,0:T(8,128)}, u32[]{:S(2)}) copy-start(f32[8,128]{1,0:T(8,128)} %constant.23.clone.share_ref) | copy-start | bytes 12292
  29.4 9.7 %collective-permute-start.14 = (f32[5,64,128]{2,1,0:T(8,128)S(1)}, f32[5,64,128]{2,1,0:T(8,128)S(1)}, u32[]{:S(2)}, u32[]{:S(2)}) collective-permute-start(f32[5,64,128]{2,1,0:T(8,128)S(1)} %get-tuple-element.43), channel_id=1, source_target_pairs={{1,0},{2,1},{3,2},{0,3},{5,4},{6,5},{7,6},{4,7},{9,8},{10,9},{11,1... | collective-permute-start | bytes 491528 | tf_op jit(solution)/shard_map/ppermute | solution.py:603
  29.5 9.6 %collective-permute-start.13 = (f32[5,64,128]{2,1,0:T(8,128)S(1)}, f32[5,64,128]{2,1,0:T(8,128)S(1)}, u32[]{:S(2)}, u32[]{:S(2)}) collective-permute-start(f32[5,64,128]{2,1,0:T(8,128)S(1)} %get-tuple-element.44), channel_id=1, source_target_pairs={{0,1},{1,2},{2,3},{3,0},{4,5},{5,6},{6,7},{7,4},{8,9},{9,10},{10,1... | collective-permute-start | bytes 491528 | tf_op jit(solution)/shard_map/ppermute | solution.py:603
  37.2 3.2 %collective-permute-start.12 = (f32[40,128]{1,0:T(8,128)S(1)}, f32[40,128]{1,0:T(8,128)S(1)}, u32[]{:S(2)}, u32[]{:S(2)}) collective-permute-start(f32[40,128]{1,0:T(8,128)S(1)} %shard_map.135.refs_0_), channel_id=1, source_target_pairs={{0,3},{1,2},{2,1},{3,0},{4,7},{5,6},{6,5},{7,4},{8,11},{9,10},{10,... | collective-permute-start | bytes 61448 | tf_op jit(solution)/shard_map/ppermute | solution.py:688
  37.2 3.8 %collective-permute-start.11 = (f32[40,128]{1,0:T(8,128)S(1)}, f32[40,128]{1,0:T(8,128)S(1)}, u32[]{:S(2)}, u32[]{:S(2)}) collective-permute-start(f32[40,128]{1,0:T(8,128)S(1)} %shard_map.135.refs_0_), channel_id=1, source_target_pairs={{0,2},{1,3},{2,0},{3,1},{4,6},{5,7},{6,4},{7,5},{8,10},{9,11},{10,... | collective-permute-start | bytes 61448 | tf_op jit(solution)/shard_map/ppermute | solution.py:688
  37.8 3.2 %collective-permute-start.10 = (f32[40,128]{1,0:T(8,128)S(1)}, f32[40,128]{1,0:T(8,128)S(1)}, u32[]{:S(2)}, u32[]{:S(2)}) collective-permute-start(f32[40,128]{1,0:T(8,128)S(1)} %shard_map.135.refs_0_), channel_id=1, source_target_pairs={{0,1},{1,0},{2,3},{3,2},{4,5},{5,4},{6,7},{7,6},{8,9},{9,8},{10,11... | collective-permute-start | bytes 61448 | tf_op jit(solution)/shard_map/ppermute | solution.py:688
  39.1 1.9 %copy-start.4 = (bf16[512,512]{1,0:T(8,128)(2,1)S(1)}, bf16[512,512]{1,0:T(8,128)(2,1)}, u32[]{:S(2)}) copy-start(bf16[512,512]{1,0:T(8,128)(2,1)} %constant.25.clone.refs_8_) | copy-start | bytes 1572868
  39.1 1.9 %copy-start.5 = (bf16[512,512]{1,0:T(8,128)(2,1)S(1)}, bf16[512,512]{1,0:T(8,128)(2,1)}, u32[]{:S(2)}) copy-start(bf16[512,512]{1,0:T(8,128)(2,1)} %constant.24.clone.refs_7_) | copy-start | bytes 1572868
  39.1 1.9 %copy-start.10 = (bf16[48,128]{1,0:T(8,128)(2,1)S(1)}, bf16[48,128]{1,0:T(8,128)(2,1)}, u32[]{:S(2)}) copy-start(bf16[48,128]{1,0:T(8,128)(2,1)} %constant.26.clone.refs_9_) | copy-start | bytes 36868
